TPU v7x, 128 devices: a whole 4x4x4 slice. The times are simulated.
128 devices in a mesh: lat: 16 (over z, y), lon: 8 (over x, core).
Axes of the slice: x: 4, y: 4, z: 4, core: 2. Of those that a mesh axis runs over, the one named last changes fastest.
Arguments:
- grid_feat: bfloat16 [131072, 512], P(('lat', 'lon')), may hold values from -6 to 6
- mesh_feat: bfloat16 [8192, 512], P(('lat', 'lon')), may hold values from -6 to 6
- enc_send: int32 [128, 9, 256], P(('lat', 'lon')), may hold values from 0 to 1023
- enc_recv: int32 [128, 9, 256], P(('lat', 'lon')), may hold values from 0 to 63
- enc_count: int32 [128, 9], P(('lat', 'lon')), may hold values from 0 to 256, as said below
- dec_send: int32 [128, 9, 512], P(('lat', 'lon')), may hold values from 0 to 63
- dec_recv: int32 [128, 9, 512], P(('lat', 'lon')), may hold values from 0 to 1023
- dec_count: int32 [128, 9], P(('lat', 'lon')), may hold values from 0 to 512, as said below
- enc_src: bfloat16 [512, 512], replicated, may hold values from -0.25 to 0.25
- enc_dst: bfloat16 [512, 512], replicated, may hold values from -0.25 to 0.25
- enc_bias: float32 [512], replicated, may hold values from -3 to 3
- enc_out: bfloat16 [512, 512], replicated, may hold values from -0.03125 to 0.03125
- dec_src: bfloat16 [512, 512], replicated, may hold values from -0.25 to 0.25
- dec_dst: bfloat16 [512, 512], replicated, may hold values from -0.25 to 0.25
- dec_bias: float32 [512], replicated, may hold values from -3 to 3
- dec_out: bfloat16 [512, 512], replicated, may hold values from -0.1875 to 0.1875
- grid_cot: bfloat16 [131072, 512], P(('lat', 'lon')), may hold values from -6 to 6
Outputs:
- grid_new: bfloat16 [131072, 512], P(('lat', 'lon'))
- mesh_grad: bfloat16 [8192, 512], P(('lat', 'lon'))
- grid_grad: bfloat16 [131072, 512], P(('lat', 'lon'))
Inputs may be any that keep to these rules, and one draw needn't show every extreme that they name: `enc_send`: row of the grid device's own tile. `enc_recv`: row of the mesh tile of the block's neighbour. `enc_count`: live slots of each block; 0 where the neighbour would lie beyond a pole; block 4 (the device itself) is full, and in every draw some device receives full blocks from all its neighbours. `dec_send`: row of the mesh tile of the block's neighbour. `dec_recv`: row of the grid device's own tile. `dec_count`: live slots of each block; 0 where the neighbour would lie beyond a pole; block 4 (the device itself) is full, and in every draw some device sends full blocks to all its neighbours.
All inputs are finite; a program needn't handle non-finite values.
Results may differ from a plain program's by a relative error of at most 0.0086.
Values may be sent and summed in bfloat16 or wider, within the bound.
No kernel may reach another device: no remote copies, remote signals or barrier semaphores. Data moves between devices by JAX's collectives and lax.ppermute only.
A program may use at most 128 MiB of HBM per device.

v0:
```python
import jax
import jax.numpy as jnp
from jax import lax
from jax.experimental import pallas as pl
from jax.experimental.pallas import tpu as pltpu
from jax.sharding import PartitionSpec as P

F32 = jnp.float32
BF16 = jnp.bfloat16
LANES = 128
CHUNK = 256

VMEM = pl.BlockSpec(memory_space=pltpu.VMEM)
SMEM = pl.BlockSpec(memory_space=pltpu.SMEM)


def mm(lhs, rhs):
    return jnp.dot(lhs, rhs, preferred_element_type=F32)


def mm_nt(lhs, rhs):
    return lax.dot_general(lhs, rhs, (((1,), (1,)), ((), ())), preferred_element_type=F32)


def as_hot(mask):
    return jnp.where(mask, 1.0, 0.0).astype(BF16)


def down_rows(index_row):
    return jnp.transpose(jnp.broadcast_to(index_row, (LANES, index_row.shape[1])))


def gather_hot(index_row, rows):
    spread = down_rows(index_row)
    lane = lax.broadcasted_iota(jnp.int32, spread.shape, 1)
    return jnp.concatenate(
        [as_hot(spread == lane + start) for start in range(0, rows, LANES)], axis=1
    )


def scatter_hot(index_row, rows, live):
    slots = index_row.shape[1]
    slot = lax.broadcasted_iota(jnp.int32, (1, slots), 1)
    index_row = jnp.where(slot < live, index_row, -1)
    return as_hot(lax.broadcasted_iota(jnp.int32, (rows, slots), 0) == index_row)


def gate(pre):
    return 0.5 * jnp.tanh(0.5 * pre) + 0.5


def chunks_of(live):
    return lax.div(live + (CHUNK - 1), CHUNK)


def chunk_at(c):
    return pl.multiple_of(c * CHUNK, CHUNK)


def block_of(step, flip):
    lon_place = lax.div(step, 3)
    slot = lax.rem(step, 3)
    first = 1 - 2 * flip
    lat_offset = jnp.where(slot == 0, 0, jnp.where(slot == 1, first, -first))
    return 3 * (lat_offset + 1) + lon_place


def enc_gather_kernel(counts, send, feat, weight, out, proj):
    proj[...] = mm(feat[...], weight[...]).astype(BF16)

    @pl.loop(0, send.shape[0])
    def _(k):
        @pl.when(counts[0, k] > 0)
        def _():
            out[k] = mm(gather_hot(send[k], proj.shape[0]), proj[...]).astype(BF16)


def gather_slots(counts, recv, table, out):
    @pl.loop(0, recv.shape[0])
    def _(k):
        @pl.loop(0, chunks_of(counts[0, k]))
        def _(c):
            at = chunk_at(c)
            hot = gather_hot(recv[k, :, pl.ds(at, CHUNK)], table.shape[0])
            out[k, pl.ds(at, CHUNK), :] = mm(hot, table[...]).astype(BF16)


def side_gather_kernel(counts, recv, feat, weight, bias, out, table):
    table[...] = (mm(feat[...], weight[...]) + bias[...]).astype(BF16)
    gather_slots(counts, recv, table, out)


def back_gather_kernel(counts, recv, cot, weight, out, table):
    table[...] = mm_nt(cot[...], weight[...]).astype(BF16)
    gather_slots(counts, recv, table, out)


def near_blocks(flip, body):
    @pl.loop(0, 3)
    def _(slot):
        for place in range(3):
            body(block_of(3 * place + slot, flip[0]), slot, place)


def enc_forward_kernel(
    counts, flip, recv, left, own, right, weight, bias, sent,
    out_left, out_own, out_right, slope, side,
):
    rows = own.shape[1]
    for place, near in enumerate((left, own, right)):
        feats = near[...].reshape(3 * rows, near.shape[2])
        exact = mm(feats, weight[...]) + bias[...]
        high = exact.astype(BF16)
        low = (exact - high.astype(F32)).astype(BF16)
        side[place, :, :rows, :] = high.reshape(3, rows, -1)
        side[place, :, rows:, :] = low.reshape(3, rows, -1)
    outs = (out_left, out_own, out_right)

    def one(k, slot, place):
        live = counts[0, k]
        outs[place][slot] = jnp.zeros(own.shape[1:], BF16)

        @pl.when(live > 0)
        def _():
            index_row = recv[k]
            spread = down_rows(index_row)
            lane = lax.broadcasted_iota(jnp.int32, spread.shape, 1)
            hot = as_hot(spread == jnp.where(lane < rows, lane, lane - rows))
            pre = sent[k].astype(F32) + mm(hot, side[place, slot])
            squashed = gate(pre)
            message = pre * squashed
            slope[k] = (squashed + message * (1.0 - squashed)).astype(BF16)
            total = mm(scatter_hot(index_row, rows, live), message.astype(BF16))
            outs[place][slot] = total.astype(BF16)

    near_blocks(flip, one)


def dec_kernel(
    counts, flip, send, left, own, right, side, back,
    out_left, out_own, out_right, messages, grads, total,
):
    rows = own.shape[1]
    nears = (left, own, right)
    outs = (out_left, out_own, out_right)

    def one(k, slot, place):
        live = counts[0, k]
        total[...] = jnp.zeros(total.shape, F32)

        @pl.loop(0, chunks_of(live))
        def _(c):
            at = chunk_at(c)
            index_row = send[k, :, pl.ds(at, CHUNK)]
            spread = down_rows(index_row)
            lane = lax.broadcasted_iota(jnp.int32, spread.shape, 1)
            hot = as_hot(spread == lane)[:, :rows]
            pre = side[k, pl.ds(at, CHUNK), :].astype(F32) + mm(hot, nears[place][slot])
            squashed = gate(pre)
            message = pre * squashed
            messages[k, pl.ds(at, CHUNK), :] = message.astype(BF16)
            slope = squashed + message * (1.0 - squashed)
            grad = (back[k, pl.ds(at, CHUNK), :].astype(F32) * slope).astype(BF16)
            grads[k, pl.ds(at, CHUNK), :] = grad
            total[...] += mm(scatter_hot(index_row, rows, live - at), grad)

        outs[place][slot] = total[...].astype(BF16)

    near_blocks(flip, one)


def enc_backward_kernel(
    counts, flip, recv, left, own, right, slope, out_left, out_own, out_right, grads
):
    rows = own.shape[1]
    nears = (left, own, right)
    outs = (out_left, out_own, out_right)

    def one(k, slot, place):
        live = counts[0, k]
        outs[place][slot] = jnp.zeros(own.shape[1:], BF16)

        @pl.when(live > 0)
        def _():
            index_row = recv[k]
            spread = down_rows(index_row)
            lane = lax.broadcasted_iota(jnp.int32, spread.shape, 1)
            hot = as_hot(spread == lane)[:, :rows]
            received = mm(hot, nears[place][slot])
            grad = (received * slope[k].astype(F32)).astype(BF16)
            grads[k] = grad
            outs[place][slot] = mm(scatter_hot(index_row, rows, live), grad).astype(BF16)

    near_blocks(flip, one)


def scatter_slots(counts, recv, values, total):
    total[...] = jnp.zeros(total.shape, F32)

    @pl.loop(0, recv.shape[0])
    def _(k):
        live = counts[0, k]

        @pl.loop(0, chunks_of(live))
        def _(c):
            at = chunk_at(c)
            hot = scatter_hot(recv[k, :, pl.ds(at, CHUNK)], total.shape[0], live - at)
            total[...] += mm(hot, values[k, pl.ds(at, CHUNK), :])


def dec_sum_kernel(counts, recv, messages, feat, weight, out, total):
    scatter_slots(counts, recv, messages, total)
    out[...] = (feat[...].astype(F32) + mm(total[...].astype(BF16), weight[...])).astype(BF16)


def dec_local_kernel(counts, recv, grads, out, total):
    scatter_slots(counts, recv, grads, total)
    out[...] = total[...].astype(BF16)


def enc_scatter_kernel(counts, send, grads, cot, local, dec_weight, enc_weight, out, total):
    scatter_slots(counts, send, grads, total)
    back = mm_nt(local[...], dec_weight[...])
    back += mm_nt(total[...].astype(BF16), enc_weight[...])
    out[...] = (cot[...].astype(F32) + back).astype(BF16)


def along(axis, pairs):
    return lambda value: lax.ppermute(value, axis, pairs)


def lat_pairs(size, start):
    edges = [(i, (i + 1) % size) for i in range(start, size, 2)]
    return edges + [(j, i) for i, j in edges]


def on_device(
    grid_feat, mesh_feat, enc_send, enc_recv, enc_count, dec_send, dec_recv, dec_count,
    enc_src, enc_dst, enc_bias, enc_out, dec_src, dec_dst, dec_bias, dec_out, grid_cot,
):
    grid_rows, width = grid_feat.shape
    mesh_rows = mesh_feat.shape[0]
    cap_e = enc_send.shape[2]
    cap_d = dec_send.shape[2]
    lat_size = lax.axis_size("lat")
    lon_size = lax.axis_size("lon")
    flip = lax.rem(lax.axis_index("lat"), 2).astype(jnp.int32).reshape(1)
    first = along("lat", lat_pairs(lat_size, 0))
    second = along("lat", lat_pairs(lat_size, 1))
    east = along("lon", [(i, (i + 1) % lon_size) for i in range(lon_size)])
    west = along("lon", [((i + 1) % lon_size, i) for i in range(lon_size)])

    def spread(tile, name):
        with jax.named_scope(name + "_lat"):
            pieces = [tile, first(tile), second(tile)]
        with jax.named_scope(name + "_lon"):
            three = jnp.stack(pieces)
            return east(three), three, west(three)

    def fold(left, own, right, name):
        with jax.named_scope(name + "_lon"):
            from_east = west(left).astype(F32)
            from_west = east(right).astype(F32)
        three = own.astype(F32) + from_east + from_west
        sent = three[1:].astype(BF16)
        with jax.named_scope(name + "_lat"):
            return three[0] + first(sent[0]).astype(F32) + second(sent[1]).astype(F32)

    def kernel(body, outs, scratch, name, *args, smem=1, mib=12, work=0):
        with jax.named_scope(name):
            return pl.pallas_call(
                body,
                out_shape=outs,
                in_specs=[SMEM] * smem + [VMEM] * (len(args) - smem),
                out_specs=[VMEM] * len(outs),
                scratch_shapes=scratch,
                compiler_params=pltpu.CompilerParams(vmem_limit_bytes=mib * 1024 * 1024),
                cost_estimate=pl.CostEstimate(flops=work, bytes_accessed=0, transcendentals=0),
                name=name,
            )(*args)

    def array(*shape):
        return jax.ShapeDtypeStruct(shape, BF16)

    three = [array(3, mesh_rows, width)] * 3
    enc_slots = [array(9, cap_e, width)]
    dec_slots = [array(9, cap_d, width)]
    grid_tile = [array(grid_rows, width)]
    rounded_grid = [pltpu.VMEM((grid_rows, width), BF16)]
    exact_grid = [pltpu.VMEM((grid_rows, width), F32)]
    enc_work = 2 * grid_rows * width * 9 * cap_e
    dec_work = 2 * grid_rows * width * 9 * cap_d

    enc_send, enc_recv, dec_send, dec_recv = (
        jnp.swapaxes(a, 0, 1) for a in (enc_send, enc_recv, dec_send, dec_recv)
    )

    near_feat = spread(mesh_feat, "e1")
    (sent,) = kernel(
        enc_gather_kernel, enc_slots, rounded_grid, "enc_gather",
        enc_count, enc_send, grid_feat, enc_src, work=enc_work,
    )
    (back_at,) = kernel(
        back_gather_kernel, dec_slots, rounded_grid, "back_gather",
        dec_count, dec_recv, grid_cot, dec_out, work=dec_work,
    )
    (side_at,) = kernel(
        side_gather_kernel, dec_slots, rounded_grid, "side_gather",
        dec_count, dec_recv, grid_feat, dec_dst, dec_bias.reshape(1, width), work=dec_work,
    )

    *enc_partial, slope = kernel(
        enc_forward_kernel, three + enc_slots,
        [pltpu.VMEM((3, 3, 2 * mesh_rows, width), BF16)], "enc_forward",
        enc_count, flip, enc_recv, *near_feat, enc_dst, enc_bias.reshape(1, width), sent,
        smem=2, work=enc_work // 4,
    )
    enc_sum = fold(*enc_partial, "f1").astype(BF16)
    mesh_new = (mesh_feat.astype(F32) + mm(enc_sum, enc_out)).astype(BF16)
    dec_proj = mm(mesh_new, dec_src).astype(BF16)

    *dec_partial, messages, dec_grads = kernel(
        dec_kernel, three + dec_slots * 2, [pltpu.VMEM((mesh_rows, width), F32)], "dec_edges",
        dec_count, flip, dec_send, *spread(dec_proj, "e2"), side_at, back_at,
        smem=2, work=dec_work // 4,
    )
    mesh_total = fold(*dec_partial, "f2").astype(BF16)
    mesh_back = mm_nt(mesh_total, dec_src)
    enc_back = mm_nt(mesh_back.astype(BF16), enc_out).astype(BF16)

    (grid_new,) = kernel(
        dec_sum_kernel, grid_tile, exact_grid, "dec_sum",
        dec_count, dec_recv, messages, grid_feat, dec_out, work=dec_work,
    )
    (local,) = kernel(
        dec_local_kernel, grid_tile, exact_grid, "dec_local",
        dec_count, dec_recv, dec_grads, work=dec_work,
    )

    *grad_partial, grads = kernel(
        enc_backward_kernel, three + enc_slots, [], "enc_backward",
        enc_count, flip, enc_recv, *spread(enc_back, "e3"), slope,
        smem=2, work=enc_work // 4,
    )
    enc_local = fold(*grad_partial, "f3").astype(BF16)
    mesh_grad = (mesh_back + mm_nt(enc_local, enc_dst)).astype(BF16)

    (grid_grad,) = kernel(
        enc_scatter_kernel, grid_tile, exact_grid, "enc_scatter",
        enc_count, enc_send, grads, grid_cot, local, dec_dst, enc_src, work=enc_work,
    )
    return grid_new, mesh_grad, grid_grad


def solution(mesh):
    rows = P(("lat", "lon"), None)
    edges = P(("lat", "lon"), None, None)
    return jax.shard_map(
        on_device,
        mesh=mesh,
        in_specs=(rows, rows, edges, edges, rows, edges, edges, rows)
        + (P(),) * 8
        + (rows,),
        out_specs=(rows, rows, rows),
        check_vma=False,
    )
```

profile of v0, /device:TPU:1, one launch (start us, length us, event | category | flops | bytes accessed | tf_op | source)
XLA Modules:
  0.0 140.9 jit_solution(1259367230317295566)
XLA Ops:
  0.6 0.0 copy-start
  0.7 7.1 %collective-permute-start.1 = (bf16[64,512]{1,0:T(8,128)(2,1)}, bf16[64,512]{1,0:T(8,128)(2,1)S(1)}, u32[]{:S(2)}, u32[]{:S(2)}) collective-permute-start(bf16[64,512]{1,0:T(8,128)(2,1)} %param.18), channel_id=1, source_target_pairs={{8,16},{24,32},{40,48},{56,64},{72,80},{88,96},{104,112},{120,0},{... | collective-permute-start | bytes 196616 | tf_op jit(solution)/shard_map/e1_lat/ppermute | solution.py:229
  7.8 1.9 %collective-permute-done.1 = bf16[64,512]{1,0:T(8,128)(2,1)S(1)} collective-permute-done((bf16[64,512]{1,0:T(8,128)(2,1)}, bf16[64,512]{1,0:T(8,128)(2,1)S(1)}, u32[]{:S(2)}, u32[]{:S(2)}) %collective-permute-start.1) | collective-permute-done | bytes 65568 | tf_op jit(solution)/shard_map/e1_lat/ppermute | solution.py:229
  9.7 1.5 %collective-permute-done = bf16[64,512]{1,0:T(8,128)(2,1)S(1)} collective-permute-done((bf16[64,512]{1,0:T(8,128)(2,1)}, bf16[64,512]{1,0:T(8,128)(2,1)S(1)}, u32[]{:S(2)}, u32[]{:S(2)}) %collective-permute-start) | collective-permute-done | bytes 65568 | tf_op jit(solution)/shard_map/e1_lat/ppermute | solution.py:229
  11.1 0.9 pad_maximum_fusion.own
  12.0 2.1 %collective-permute-start.3 = (bf16[3,64,512]{2,1,0:T(8,128)(2,1)S(1)}, bf16[3,64,512]{2,1,0:T(8,128)(2,1)S(1)}, u32[]{:S(2)}, u32[]{:S(2)}) collective-permute-start(bf16[3,64,512]{2,1,0:T(8,128)(2,1)S(1)} %pad_maximum_fusion.own), channel_id=1, source_target_pairs={{1,0},{2,1},{3,2},{4,3},{5,4},{6,5},{7,6},{0,7},{9,8},{10,9},{11,1... | collective-permute-start | bytes 589832 | tf_op jit(solution)/shard_map/e1_lon/ppermute | solution.py:229
  14.1 1.1 collective-permute-start.2
  15.2 0.7 copy-done.5
  15.9 1.2 copy-done.8
  17.1 1.0 copy-done.14
  18.1 0.7 copy-done.18
  18.8 4.4 %enc_gather.1.sent = bf16[9,256,512]{2,1,0:T(8,128)(2,1)S(1)} custom-call(s32[1,9]{1,0:T(1,128)S(1)} %copy-done.5, s32[9,1,256]{2,1,0:T(1,128)S(1)} %bitcast.69, bf16[1024,512]{1,0:T(8,128)(2,1)S(1)} %copy-done.8, bf16[512,512]{1,0:T(8,128)(2,1)S(1)} %copy-done.14), custom_call_target="tpu_custom_call" | custom-call | flops 2415919104 | tf_op jit(solution)/shard_map/enc_gather/enc_gather/pallas_call | solution.py:271
  23.3 0.0 copy-start.7
  23.3 0.0 copy-start.17
  23.3 0.0 collective-permute-done.3.right
  23.4 4.3 %enc_forward.1 = (bf16[3,64,512]{2,1,0:T(8,128)(2,1)S(1)}, bf16[3,64,512]{2,1,0:T(8,128)(2,1)S(1)}, bf16[3,64,512]{2,1,0:T(8,128)(2,1)S(1)}, bf16[9,256,512]{2,1,0:T(8,128)(2,1)S(1)}) custom-call(s32[1,9]{1,0:T(1,128)S(1)} %copy-done.5, s32[1]{0:T(128)} %bitcast.1.flip, s32[9,1,256]{2,1,0:T(1,128)S(1)} %bitcast.61, ...), custom_call_target="tpu_custom_call" | custom-call | flops 603979776 | tf_op jit(solution)/shard_map/enc_forward/enc_forward/pallas_call | solution.py:271
  27.7 0.0 collective-permute-start.4
  27.7 1.7 %collective-permute-start.5 = (bf16[3,64,512]{2,1,0:T(8,128)(2,1)S(1)}, bf16[3,64,512]{2,1,0:T(8,128)(2,1)S(1)}, u32[]{:S(2)}, u32[]{:S(2)}) collective-permute-start(bf16[3,64,512]{2,1,0:T(8,128)(2,1)S(1)} %get-tuple-element.18), channel_id=1, source_target_pairs={{0,1},{1,2},{2,3},{3,4},{4,5},{5,6},{6,7},{7,0},{8,9},{9,10},{10,1... | collective-permute-start | bytes 589832 | tf_op jit(solution)/shard_map/f1_lon/ppermute | solution.py:229
  29.5 3.3 %collective-permute-done.4 = bf16[3,64,512]{2,1,0:T(8,128)(2,1)S(1)} collective-permute-done((bf16[3,64,512]{2,1,0:T(8,128)(2,1)S(1)}, bf16[3,64,512]{2,1,0:T(8,128)(2,1)S(1)}, u32[]{:S(2)}, u32[]{:S(2)}) %collective-permute-start.4) | collective-permute-done | bytes 196640 | tf_op jit(solution)/shard_map/f1_lon/ppermute | solution.py:229
  32.8 0.0 collective-permute-done.5
  32.8 0.8 fusion.20
  33.7 2.9 %collective-permute-start.6 = (bf16[64,512]{1,0:T(8,128)(2,1)S(1)}, bf16[64,512]{1,0:T(8,128)(2,1)}, u32[]{:S(2)}, u32[]{:S(2)}) collective-permute-start(bf16[64,512]{1,0:T(8,128)(2,1)S(1)} %get-tuple-element.39), channel_id=1, source_target_pairs={{0,8},{16,24},{32,40},{48,56},{64,72},{80,88},{96,104},{112,120},{... | collective-permute-start | bytes 196616 | tf_op jit(solution)/shard_map/f1_lat/ppermute | solution.py:229
  36.6 0.9 collective-permute-start.7
  37.5 0.9 collective-permute-done.6
  38.3 4.8 %collective-permute-done.7 = bf16[64,512]{1,0:T(8,128)(2,1)} collective-permute-done((bf16[64,512]{1,0:T(8,128)(2,1)S(1)}, bf16[64,512]{1,0:T(8,128)(2,1)}, u32[]{:S(2)}, u32[]{:S(2)}) %collective-permute-start.7) | collective-permute-done | bytes 65568 | tf_op jit(solution)/shard_map/f1_lat/ppermute | solution.py:229
  43.1 2.2 %convolution_convert_fusion.1 = bf16[64,512]{1,0:T(8,128)(2,1)} fusion(bf16[512,512]{1,0:T(8,128)(2,1)S(1)} %copy-done, bf16[512,512]{1,0:T(8,128)(2,1)} %param.28, bf16[64,512]{1,0:T(8,128)(2,1)S(1)} %copy-done.22, f32[3,64,512]{2,1,0:T(8,128)} %get-tuple-element.34, bf16[64,512]{1,0:T(8,128)(2,1)} %collective-permute-done.7, ...), kind=kOutput, calls=%fused_computation.5 | convolution fusion | flops 67403776 | bytes 1441792 | tf_op jit(solution)/shard_map/dot_general | solution.py:18
  45.3 0.9 collective-permute-start.9
  46.2 0.0 collective-permute-start.8
  46.2 0.0 copy-start.10
  46.2 1.2 copy-done.10
  47.4 1.0 copy-done.12
  48.5 7.5 %back_gather.1.back = bf16[9,512,512]{2,1,0:T(8,128)(2,1)S(1)} custom-call(s32[1,9]{1,0:T(1,128)S(1)} %copy-done.7, s32[9,1,512]{2,1,0:T(1,128)S(1)} %bitcast.65, bf16[1024,512]{1,0:T(8,128)(2,1)S(1)} %copy-done.10, bf16[512,512]{1,0:T(8,128)(2,1)S(1)} %copy-done.12), custom_call_target="tpu_custom_call" | custom-call | flops 4831838208 | tf_op jit(solution)/shard_map/back_gather/back_gather/pallas_call | solution.py:271
  56.0 0.0 collective-permute-done.9
  56.0 0.0 collective-permute-done.8
  56.1 5.6 %collective-permute-start.11 = (bf16[3,64,512]{2,1,0:T(8,128)(2,1)S(1)}, bf16[3,64,512]{2,1,0:T(8,128)(2,1)S(1)}, u32[]{:S(2)}, u32[]{:S(2)}) collective-permute-start(bf16[3,64,512]{2,1,0:T(8,128)(2,1)S(1)} %pad_maximum_fusion.1.own), channel_id=1, source_target_pairs={{1,0},{2,1},{3,2},{4,3},{5,4},{6,5},{7,6},{0,7},{9,8},{10,9},{11,1... | collective-permute-start | bytes 589832 | tf_op jit(solution)/shard_map/e2_lon/ppermute | solution.py:229
  61.6 0.0 collective-permute-start.10
  61.7 0.0 copy-start.3
  61.7 7.5 %side_gather.1.side = bf16[9,512,512]{2,1,0:T(8,128)(2,1)S(1)} custom-call(s32[1,9]{1,0:T(1,128)S(1)} %copy-done.7, s32[9,1,512]{2,1,0:T(1,128)S(1)} %bitcast.66, bf16[1024,512]{1,0:T(8,128)(2,1)S(1)} %copy-done.9, bf16[512,512]{1,0:T(8,128)(2,1)S(1)} %copy-done.16, f32[1,512]{1,0:T(1,128)S(1)} %bitcast.71), custom_call_target="tpu_custom_call" | custom-call | flops 4831838208 | tf_op jit(solution)/shard_map/side_gather/side_gather/pallas_call | solution.py:271
  69.3 0.0 copy-start.21
  69.3 0.0 copy-start.13
  69.3 7.6 %dec_edges.1 = (bf16[3,64,512]{2,1,0:T(8,128)(2,1)S(1)}, bf16[3,64,512]{2,1,0:T(8,128)(2,1)S(1)}, bf16[3,64,512]{2,1,0:T(8,128)(2,1)S(1)}, bf16[9,512,512]{2,1,0:T(8,128)(2,1)S(1)}, bf16[9,512,512]{2,1,0:T(8,128)(2,1)S(1)}) custom-call(s32[1,9]{1,0:T(1,128)S(1)} %copy-done.7, s32[1]{0:T(128)} %bitcast.1.flip, s32[9,1,512]{2,1,0:T(1,128)S(1)} %bitcast.63, ...), custom_call_target="tpu_custom_call" | custom-call | flops 1207959552 | tf_op jit(solution)/shard_map/dec_edges/dec_edges/pallas_call | solution.py:271
  76.9 0.5 collective-permute-start.12
  77.4 1.3 collective-permute-start.13
  78.7 3.3 %collective-permute-done.12 = bf16[3,64,512]{2,1,0:T(8,128)(2,1)S(1)} collective-permute-done((bf16[3,64,512]{2,1,0:T(8,128)(2,1)S(1)}, bf16[3,64,512]{2,1,0:T(8,128)(2,1)S(1)}, u32[]{:S(2)}, u32[]{:S(2)}) %collective-permute-start.12) | collective-permute-done | bytes 196640 | tf_op jit(solution)/shard_map/f2_lon/ppermute | solution.py:229
  82.0 0.1 fusion.19
  82.1 7.2 %collective-permute-start.14 = (bf16[64,512]{1,0:T(8,128)(2,1)S(1)}, bf16[64,512]{1,0:T(8,128)(2,1)S(1)}, u32[]{:S(2)}, u32[]{:S(2)}) collective-permute-start(bf16[64,512]{1,0:T(8,128)(2,1)S(1)} %get-tuple-element.37), channel_id=1, source_target_pairs={{0,8},{16,24},{32,40},{48,56},{64,72},{80,88},{96,104},{112,120},{... | collective-permute-start | bytes 196616 | tf_op jit(solution)/shard_map/f2_lat/ppermute | solution.py:229
  89.3 4.1 %collective-permute-start.15 = (bf16[64,512]{1,0:T(8,128)(2,1)S(1)}, bf16[64,512]{1,0:T(8,128)(2,1)S(1)}, u32[]{:S(2)}, u32[]{:S(2)}) collective-permute-start(bf16[64,512]{1,0:T(8,128)(2,1)S(1)} %get-tuple-element.38), channel_id=1, source_target_pairs={{8,16},{24,32},{40,48},{56,64},{72,80},{88,96},{104,112},{120,0},{... | collective-permute-start | bytes 196616 | tf_op jit(solution)/shard_map/f2_lat/ppermute | solution.py:229
  93.4 2.3 %collective-permute-done.15 = bf16[64,512]{1,0:T(8,128)(2,1)S(1)} collective-permute-done((bf16[64,512]{1,0:T(8,128)(2,1)S(1)}, bf16[64,512]{1,0:T(8,128)(2,1)S(1)}, u32[]{:S(2)}, u32[]{:S(2)}) %collective-permute-start.15) | collective-permute-done | bytes 65568 | tf_op jit(solution)/shard_map/f2_lat/ppermute | solution.py:229
  95.8 0.3 fusion.14
  96.0 0.3 convolution_convert_fusion
  96.3 4.2 %collective-permute-start.17 = (bf16[64,512]{1,0:T(8,128)(2,1)S(1)}, bf16[64,512]{1,0:T(8,128)(2,1)S(1)}, u32[]{:S(2)}, u32[]{:S(2)}) collective-permute-start(bf16[64,512]{1,0:T(8,128)(2,1)S(1)} %convolution_convert_fusion), channel_id=1, source_target_pairs={{8,16},{24,32},{40,48},{56,64},{72,80},{88,96},{104,112},{120,0},{... | collective-permute-start | bytes 196616 | tf_op jit(solution)/shard_map/e3_lat/ppermute | solution.py:229
  100.5 2.3 %collective-permute-done.17 = bf16[64,512]{1,0:T(8,128)(2,1)S(1)} collective-permute-done((bf16[64,512]{1,0:T(8,128)(2,1)S(1)}, bf16[64,512]{1,0:T(8,128)(2,1)S(1)}, u32[]{:S(2)}, u32[]{:S(2)}) %collective-permute-start.17) | collective-permute-done | bytes 65568 | tf_op jit(solution)/shard_map/e3_lat/ppermute | solution.py:229
  102.8 0.8 collective-permute-done.16
  103.6 5.7 %collective-permute-start.19 = (bf16[3,64,512]{2,1,0:T(8,128)(2,1)S(1)}, bf16[3,64,512]{2,1,0:T(8,128)(2,1)S(1)}, u32[]{:S(2)}, u32[]{:S(2)}) collective-permute-start(bf16[3,64,512]{2,1,0:T(8,128)(2,1)S(1)} %pad_maximum_fusion.2.own), channel_id=1, source_target_pairs={{1,0},{2,1},{3,2},{4,3},{5,4},{6,5},{7,6},{0,7},{9,8},{10,9},{11,1... | collective-permute-start | bytes 589832 | tf_op jit(solution)/shard_map/e3_lon/ppermute | solution.py:229
  109.3 7.7 %dec_sum.1 = bf16[1024,512]{1,0:T(8,128)(2,1)} custom-call(s32[1,9]{1,0:T(1,128)S(1)} %copy-done.7, s32[9,1,512]{2,1,0:T(1,128)S(1)} %bitcast.67, bf16[9,512,512]{2,1,0:T(8,128)(2,1)S(1)} %get-tuple-element.19.messages, bf16[1024,512]{1,0:T(8,128)(2,1)S(1)} %copy-done.9, bf16[512,512]{1,0:T(8,128)(2,1)S(1)} %copy-done.13), custom_call_target="tpu_custom_call" | custom-call | flops 4831838208 | tf_op jit(solution)/shard_map/dec_sum/dec_sum/pallas_call | solution.py:271
  117.1 3.1 %enc_backward.1 = (bf16[3,64,512]{2,1,0:T(8,128)(2,1)S(1)}, bf16[3,64,512]{2,1,0:T(8,128)(2,1)S(1)}, bf16[3,64,512]{2,1,0:T(8,128)(2,1)S(1)}, bf16[9,256,512]{2,1,0:T(8,128)(2,1)S(1)}) custom-call(s32[1,9]{1,0:T(1,128)S(1)} %copy-done.6, s32[1]{0:T(128)} %bitcast.1.flip, s32[9,1,256]{2,1,0:T(1,128)S(1)} %bitcast.62, ...), custom_call_target="tpu_custom_call" | custom-call | flops 603979776 | tf_op jit(solution)/shard_map/enc_backward/enc_backward/pallas_call | solution.py:271
  120.2 0.5 collective-permute-start.20
  120.7 1.2 collective-permute-start.21
  121.9 6.1 %dec_local.1.local = bf16[1024,512]{1,0:T(8,128)(2,1)S(1)} custom-call(s32[1,9]{1,0:T(1,128)S(1)} %copy-done.7, s32[9,1,512]{2,1,0:T(1,128)S(1)} %bitcast.68, bf16[9,512,512]{2,1,0:T(8,128)(2,1)S(1)} %get-tuple-element.28.grads), custom_call_target="tpu_custom_call" | custom-call | flops 4831838208 | tf_op jit(solution)/shard_map/dec_local/dec_local/pallas_call | solution.py:271
  128.1 0.1 fusion.18
  128.2 5.3 %collective-permute-start.22 = (bf16[64,512]{1,0:T(8,128)(2,1)S(1)}, bf16[64,512]{1,0:T(8,128)(2,1)S(1)}, u32[]{:S(2)}, u32[]{:S(2)}) collective-permute-start(bf16[64,512]{1,0:T(8,128)(2,1)S(1)} %get-tuple-element.35), channel_id=1, source_target_pairs={{0,8},{16,24},{32,40},{48,56},{64,72},{80,88},{96,104},{112,120},{... | collective-permute-start | bytes 196616 | tf_op jit(solution)/shard_map/f3_lat/ppermute | solution.py:229
  133.5 5.7 %enc_scatter.1 = bf16[1024,512]{1,0:T(8,128)(2,1)} custom-call(s32[1,9]{1,0:T(1,128)S(1)} %copy-done.6, s32[9,1,256]{2,1,0:T(1,128)S(1)} %bitcast.70, bf16[9,256,512]{2,1,0:T(8,128)(2,1)S(1)} %get-tuple-element.27.grads, bf16[1024,512]{1,0:T(8,128)(2,1)S(1)} %copy-done.11, bf16[1024,512]{1,0:T(8,128)(2,1)S(1)} %dec_local.1.local, ...), custom_call_target="tpu_custom_call" | custom-call | flops 2415919104 | tf_op jit(solution)/shard_map/enc_scatter/enc_scatter/pallas_call | solution.py:271
  139.2 0.7 collective-permute-done.23
  139.9 0.9 fusion.1
  (54 shorter events, 0.2 us)
Async XLA Ops:
  0.6 42.5 %copy-start = (bf16[512,512]{1,0:T(8,128)(2,1)S(1)}, bf16[512,512]{1,0:T(8,128)(2,1)}, u32[]{:S(2)}) copy-start(bf16[512,512]{1,0:T(8,128)(2,1)} %param.29) | copy-start | bytes 1572868
  0.6 22.7 %copy-start.1 = (bf16[512,512]{1,0:T(8,128)(2,1)S(1)}, bf16[512,512]{1,0:T(8,128)(2,1)}, u32[]{:S(2)}) copy-start(bf16[512,512]{1,0:T(8,128)(2,1)} %weight.6) | copy-start | bytes 1572868
  0.7 22.7 %copy-start.4 = (f32[512]{0:T(512)S(1)}, f32[512]{0:T(512)}, u32[]{:S(2)}) copy-start(f32[512]{0:T(512)} %param.27) | copy-start | bytes 6148
  0.7 22.7 %copy-start.2 = (s32[1,9,256]{2,0,1:T(1,128)S(1)}, s32[1,9,256]{2,0,1:T(1,128)}, u32[]{:S(2)}) copy-start(s32[1,9,256]{2,0,1:T(1,128)} %param.20) | copy-start | bytes 27652
  0.7 9.0 %collective-permute-start.1 = (bf16[64,512]{1,0:T(8,128)(2,1)}, bf16[64,512]{1,0:T(8,128)(2,1)S(1)}, u32[]{:S(2)}, u32[]{:S(2)}) collective-permute-start(bf16[64,512]{1,0:T(8,128)(2,1)} %param.18), channel_id=1, source_target_pairs={{8,16},{24,32},{40,48},{56,64},{72,80},{88,96},{104,112},{120,0},{... | collective-permute-start | bytes 196616 | tf_op jit(solution)/shard_map/e1_lat/ppermute | solution.py:229
  7.8 3.3 %collective-permute-start = (bf16[64,512]{1,0:T(8,128)(2,1)}, bf16[64,512]{1,0:T(8,128)(2,1)S(1)}, u32[]{:S(2)}, u32[]{:S(2)}) collective-permute-start(bf16[64,512]{1,0:T(8,128)(2,1)} %param.18), channel_id=1, source_target_pairs={{0,8},{16,24},{32,40},{48,56},{64,72},{80,88},{96,104},{112,120},{... | collective-permute-start | bytes 196616 | tf_op jit(solution)/shard_map/e1_lat/ppermute | solution.py:229
  12.0 11.3 %collective-permute-start.3 = (bf16[3,64,512]{2,1,0:T(8,128)(2,1)S(1)}, bf16[3,64,512]{2,1,0:T(8,128)(2,1)S(1)}, u32[]{:S(2)}, u32[]{:S(2)}) collective-permute-start(bf16[3,64,512]{2,1,0:T(8,128)(2,1)S(1)} %pad_maximum_fusion.own), channel_id=1, source_target_pairs={{1,0},{2,1},{3,2},{4,3},{5,4},{6,5},{7,6},{0,7},{9,8},{10,9},{11,1... | collective-permute-start | bytes 589832 | tf_op jit(solution)/shard_map/e1_lon/ppermute | solution.py:229
  14.1 9.2 %collective-permute-start.2 = (bf16[3,64,512]{2,1,0:T(8,128)(2,1)S(1)}, bf16[3,64,512]{2,1,0:T(8,128)(2,1)S(1)}, u32[]{:S(2)}, u32[]{:S(2)}) collective-permute-start(bf16[3,64,512]{2,1,0:T(8,128)(2,1)S(1)} %pad_maximum_fusion.own), channel_id=1, source_target_pairs={{0,1},{1,2},{2,3},{3,4},{4,5},{5,6},{6,7},{7,0},{8,9},{9,10},{10,1... | collective-permute-start | bytes 589832 | tf_op jit(solution)/shard_map/e1_lon/ppermute | solution.py:229
  15.2 0.7 copy-start.5
  15.9 1.2 copy-start.8
  17.1 1.0 copy-start.14
  18.1 0.7 copy-start.18
  18.8 24.3 %copy-start.22 = (bf16[64,512]{1,0:T(8,128)(2,1)S(1)}, bf16[64,512]{1,0:T(8,128)(2,1)}, u32[]{:S(2)}) copy-start(bf16[64,512]{1,0:T(8,128)(2,1)} %param.18) | copy-start | bytes 196612
  23.3 22.9 %copy-start.7 = (s32[1,9]{1,0:T(1,128)S(1)}, s32[1,9]{1,0:T(1,128)}, u32[]{:S(2)}) copy-start(s32[1,9]{1,0:T(1,128)} %counts.16) | copy-start | bytes 112
  23.3 22.9 %copy-start.17 = (s32[1,9,512]{2,0,1:T(1,128)S(1)}, s32[1,9,512]{2,0,1:T(1,128)}, u32[]{:S(2)}) copy-start(s32[1,9,512]{2,0,1:T(1,128)} %param.23) | copy-start | bytes 55300
  27.7 5.1 %collective-permute-start.4 = (bf16[3,64,512]{2,1,0:T(8,128)(2,1)S(1)}, bf16[3,64,512]{2,1,0:T(8,128)(2,1)S(1)}, u32[]{:S(2)}, u32[]{:S(2)}) collective-permute-start(bf16[3,64,512]{2,1,0:T(8,128)(2,1)S(1)} %get-tuple-element.17), channel_id=1, source_target_pairs={{1,0},{2,1},{3,2},{4,3},{5,4},{6,5},{7,6},{0,7},{9,8},{10,9},{11,1... | collective-permute-start | bytes 589832 | tf_op jit(solution)/shard_map/f1_lon/ppermute | solution.py:229
  27.7 5.1 %collective-permute-start.5 = (bf16[3,64,512]{2,1,0:T(8,128)(2,1)S(1)}, bf16[3,64,512]{2,1,0:T(8,128)(2,1)S(1)}, u32[]{:S(2)}, u32[]{:S(2)}) collective-permute-start(bf16[3,64,512]{2,1,0:T(8,128)(2,1)S(1)} %get-tuple-element.18), channel_id=1, source_target_pairs={{0,1},{1,2},{2,3},{3,4},{4,5},{5,6},{6,7},{7,0},{8,9},{9,10},{10,1... | collective-permute-start | bytes 589832 | tf_op jit(solution)/shard_map/f1_lon/ppermute | solution.py:229
  33.7 4.7 %collective-permute-start.6 = (bf16[64,512]{1,0:T(8,128)(2,1)S(1)}, bf16[64,512]{1,0:T(8,128)(2,1)}, u32[]{:S(2)}, u32[]{:S(2)}) collective-permute-start(bf16[64,512]{1,0:T(8,128)(2,1)S(1)} %get-tuple-element.39), channel_id=1, source_target_pairs={{0,8},{16,24},{32,40},{48,56},{64,72},{80,88},{96,104},{112,120},{... | collective-permute-start | bytes 196616 | tf_op jit(solution)/shard_map/f1_lat/ppermute | solution.py:229
  36.6 6.5 %collective-permute-start.7 = (bf16[64,512]{1,0:T(8,128)(2,1)S(1)}, bf16[64,512]{1,0:T(8,128)(2,1)}, u32[]{:S(2)}, u32[]{:S(2)}) collective-permute-start(bf16[64,512]{1,0:T(8,128)(2,1)S(1)} %get-tuple-element.40), channel_id=1, source_target_pairs={{8,16},{24,32},{40,48},{56,64},{72,80},{88,96},{104,112},{120,0},{... | collective-permute-start | bytes 196616 | tf_op jit(solution)/shard_map/f1_lat/ppermute | solution.py:229
  45.3 10.7 %collective-permute-start.9 = (bf16[64,512]{1,0:T(8,128)(2,1)}, bf16[64,512]{1,0:T(8,128)(2,1)S(1)}, u32[]{:S(2)}, u32[]{:S(2)}) collective-permute-start(bf16[64,512]{1,0:T(8,128)(2,1)} %convolution_convert_fusion.1), channel_id=1, source_target_pairs={{8,16},{24,32},{40,48},{56,64},{72,80},{88,96},{104,112},{120,0},{... | collective-permute-start | bytes 196616 | tf_op jit(solution)/shard_map/e2_lat/ppermute | solution.py:229
  46.2 9.9 %collective-permute-start.8 = (bf16[64,512]{1,0:T(8,128)(2,1)}, bf16[64,512]{1,0:T(8,128)(2,1)S(1)}, u32[]{:S(2)}, u32[]{:S(2)}) collective-permute-start(bf16[64,512]{1,0:T(8,128)(2,1)} %convolution_convert_fusion.1), channel_id=1, source_target_pairs={{0,8},{16,24},{32,40},{48,56},{64,72},{80,88},{96,104},{112,120},{... | collective-permute-start | bytes 196616 | tf_op jit(solution)/shard_map/e2_lat/ppermute | solution.py:229
  46.2 1.2 copy-start.10
  47.4 1.0 copy-start.12
  48.5 7.6 %copy-start.23 = (bf16[64,512]{1,0:T(8,128)(2,1)S(1)}, bf16[64,512]{1,0:T(8,128)(2,1)}, u32[]{:S(2)}) copy-start(bf16[64,512]{1,0:T(8,128)(2,1)} %convolution_convert_fusion.1) | copy-start | bytes 196612
  48.5 13.2 %copy-start.9 = (bf16[1024,512]{1,0:T(8,128)(2,1)S(1)}, bf16[1024,512]{1,0:T(8,128)(2,1)}, u32[]{:S(2)}) copy-start(bf16[1024,512]{1,0:T(8,128)(2,1)} %feat.5) | copy-start | bytes 3145732
  48.5 13.2 %copy-start.16 = (bf16[512,512]{1,0:T(8,128)(2,1)S(1)}, bf16[512,512]{1,0:T(8,128)(2,1)}, u32[]{:S(2)}) copy-start(bf16[512,512]{1,0:T(8,128)(2,1)} %dec_weight.1) | copy-start | bytes 1572868
  48.5 13.2 %copy-start.20 = (f32[512]{0:T(512)S(1)}, f32[512]{0:T(512)}, u32[]{:S(2)}) copy-start(f32[512]{0:T(512)} %param.31) | copy-start | bytes 6148
  56.1 13.1 %collective-permute-start.11 = (bf16[3,64,512]{2,1,0:T(8,128)(2,1)S(1)}, bf16[3,64,512]{2,1,0:T(8,128)(2,1)S(1)}, u32[]{:S(2)}, u32[]{:S(2)}) collective-permute-start(bf16[3,64,512]{2,1,0:T(8,128)(2,1)S(1)} %pad_maximum_fusion.1.own), channel_id=1, source_target_pairs={{1,0},{2,1},{3,2},{4,3},{5,4},{6,5},{7,6},{0,7},{9,8},{10,9},{11,1... | collective-permute-start | bytes 589832 | tf_op jit(solution)/shard_map/e2_lon/ppermute | solution.py:229
  61.6 7.6 %collective-permute-start.10 = (bf16[3,64,512]{2,1,0:T(8,128)(2,1)S(1)}, bf16[3,64,512]{2,1,0:T(8,128)(2,1)S(1)}, u32[]{:S(2)}, u32[]{:S(2)}) collective-permute-start(bf16[3,64,512]{2,1,0:T(8,128)(2,1)S(1)} %pad_maximum_fusion.1.own), channel_id=1, source_target_pairs={{0,1},{1,2},{2,3},{3,4},{4,5},{5,6},{6,7},{7,0},{8,9},{9,10},{10,1... | collective-permute-start | bytes 589832 | tf_op jit(solution)/shard_map/e2_lon/ppermute | solution.py:229
  61.7 7.6 %copy-start.3 = (s32[1,9,512]{2,0,1:T(1,128)S(1)}, s32[1,9,512]{2,0,1:T(1,128)}, u32[]{:S(2)}) copy-start(s32[1,9,512]{2,0,1:T(1,128)} %param.22) | copy-start | bytes 55300
  69.3 26.8 %copy-start.21 = (bf16[512,512]{1,0:T(8,128)(2,1)S(1)}, bf16[512,512]{1,0:T(8,128)(2,1)}, u32[]{:S(2)}) copy-start(bf16[512,512]{1,0:T(8,128)(2,1)} %param.28) | copy-start | bytes 1572868
  69.3 40.1 %copy-start.13 = (bf16[512,512]{1,0:T(8,128)(2,1)S(1)}, bf16[512,512]{1,0:T(8,128)(2,1)}, u32[]{:S(2)}) copy-start(bf16[512,512]{1,0:T(8,128)(2,1)} %weight.9) | copy-start | bytes 1572868
  76.9 5.1 %collective-permute-start.12 = (bf16[3,64,512]{2,1,0:T(8,128)(2,1)S(1)}, bf16[3,64,512]{2,1,0:T(8,128)(2,1)S(1)}, u32[]{:S(2)}, u32[]{:S(2)}) collective-permute-start(bf16[3,64,512]{2,1,0:T(8,128)(2,1)S(1)} %get-tuple-element.21), channel_id=1, source_target_pairs={{1,0},{2,1},{3,2},{4,3},{5,4},{6,5},{7,6},{0,7},{9,8},{10,9},{11,1... | collective-permute-start | bytes 589832 | tf_op jit(solution)/shard_map/f2_lon/ppermute | solution.py:229
  77.4 4.6 %collective-permute-start.13 = (bf16[3,64,512]{2,1,0:T(8,128)(2,1)S(1)}, bf16[3,64,512]{2,1,0:T(8,128)(2,1)S(1)}, u32[]{:S(2)}, u32[]{:S(2)}) collective-permute-start(bf16[3,64,512]{2,1,0:T(8,128)(2,1)S(1)} %get-tuple-element.22), channel_id=1, source_target_pairs={{0,1},{1,2},{2,3},{3,4},{4,5},{5,6},{6,7},{7,0},{8,9},{9,10},{10,1... | collective-permute-start | bytes 589832 | tf_op jit(solution)/shard_map/f2_lon/ppermute | solution.py:229
  82.1 11.3 %collective-permute-start.14 = (bf16[64,512]{1,0:T(8,128)(2,1)S(1)}, bf16[64,512]{1,0:T(8,128)(2,1)S(1)}, u32[]{:S(2)}, u32[]{:S(2)}) collective-permute-start(bf16[64,512]{1,0:T(8,128)(2,1)S(1)} %get-tuple-element.37), channel_id=1, source_target_pairs={{0,8},{16,24},{32,40},{48,56},{64,72},{80,88},{96,104},{112,120},{... | collective-permute-start | bytes 196616 | tf_op jit(solution)/shard_map/f2_lat/ppermute | solution.py:229
  89.3 6.4 %collective-permute-start.15 = (bf16[64,512]{1,0:T(8,128)(2,1)S(1)}, bf16[64,512]{1,0:T(8,128)(2,1)S(1)}, u32[]{:S(2)}, u32[]{:S(2)}) collective-permute-start(bf16[64,512]{1,0:T(8,128)(2,1)S(1)} %get-tuple-element.38), channel_id=1, source_target_pairs={{8,16},{24,32},{40,48},{56,64},{72,80},{88,96},{104,112},{120,0},{... | collective-permute-start | bytes 196616 | tf_op jit(solution)/shard_map/f2_lat/ppermute | solution.py:229
  96.3 6.5 %collective-permute-start.17 = (bf16[64,512]{1,0:T(8,128)(2,1)S(1)}, bf16[64,512]{1,0:T(8,128)(2,1)S(1)}, u32[]{:S(2)}, u32[]{:S(2)}) collective-permute-start(bf16[64,512]{1,0:T(8,128)(2,1)S(1)} %convolution_convert_fusion), channel_id=1, source_target_pairs={{8,16},{24,32},{40,48},{56,64},{72,80},{88,96},{104,112},{120,0},{... | collective-permute-start | bytes 196616 | tf_op jit(solution)/shard_map/e3_lat/ppermute | solution.py:229
  100.5 3.1 %collective-permute-start.16 = (bf16[64,512]{1,0:T(8,128)(2,1)S(1)}, bf16[64,512]{1,0:T(8,128)(2,1)S(1)}, u32[]{:S(2)}, u32[]{:S(2)}) collective-permute-start(bf16[64,512]{1,0:T(8,128)(2,1)S(1)} %convolution_convert_fusion), channel_id=1, source_target_pairs={{0,8},{16,24},{32,40},{48,56},{64,72},{80,88},{96,104},{112,120},{... | collective-permute-start | bytes 196616 | tf_op jit(solution)/shard_map/e3_lat/ppermute | solution.py:229
  103.6 13.4 %collective-permute-start.19 = (bf16[3,64,512]{2,1,0:T(8,128)(2,1)S(1)}, bf16[3,64,512]{2,1,0:T(8,128)(2,1)S(1)}, u32[]{:S(2)}, u32[]{:S(2)}) collective-permute-start(bf16[3,64,512]{2,1,0:T(8,128)(2,1)S(1)} %pad_maximum_fusion.2.own), channel_id=1, source_target_pairs={{1,0},{2,1},{3,2},{4,3},{5,4},{6,5},{7,6},{0,7},{9,8},{10,9},{11,1... | collective-permute-start | bytes 589832 | tf_op jit(solution)/shard_map/e3_lon/ppermute | solution.py:229
  109.3 7.7 %collective-permute-start.18 = (bf16[3,64,512]{2,1,0:T(8,128)(2,1)S(1)}, bf16[3,64,512]{2,1,0:T(8,128)(2,1)S(1)}, u32[]{:S(2)}, u32[]{:S(2)}) collective-permute-start(bf16[3,64,512]{2,1,0:T(8,128)(2,1)S(1)} %pad_maximum_fusion.2.own), channel_id=1, source_target_pairs={{0,1},{1,2},{2,3},{3,4},{4,5},{5,6},{6,7},{7,0},{8,9},{9,10},{10,1... | collective-permute-start | bytes 589832 | tf_op jit(solution)/shard_map/e3_lon/ppermute | solution.py:229
  109.3 7.7 %copy-start.6 = (s32[1,9]{1,0:T(1,128)S(1)}, s32[1,9]{1,0:T(1,128)}, u32[]{:S(2)}) copy-start(s32[1,9]{1,0:T(1,128)} %counts.17) | copy-start | bytes 112
  120.2 7.9 %collective-permute-start.20 = (bf16[3,64,512]{2,1,0:T(8,128)(2,1)S(1)}, bf16[3,64,512]{2,1,0:T(8,128)(2,1)S(1)}, u32[]{:S(2)}, u32[]{:S(2)}) collective-permute-start(bf16[3,64,512]{2,1,0:T(8,128)(2,1)S(1)} %get-tuple-element.25), channel_id=1, source_target_pairs={{1,0},{2,1},{3,2},{4,3},{5,4},{6,5},{7,6},{0,7},{9,8},{10,9},{11,1... | collective-permute-start | bytes 589832 | tf_op jit(solution)/shard_map/f3_lon/ppermute | solution.py:229
  120.7 7.4 %collective-permute-start.21 = (bf16[3,64,512]{2,1,0:T(8,128)(2,1)S(1)}, bf16[3,64,512]{2,1,0:T(8,128)(2,1)S(1)}, u32[]{:S(2)}, u32[]{:S(2)}) collective-permute-start(bf16[3,64,512]{2,1,0:T(8,128)(2,1)S(1)} %get-tuple-element.26), channel_id=1, source_target_pairs={{0,1},{1,2},{2,3},{3,4},{4,5},{5,6},{6,7},{7,0},{8,9},{9,10},{10,1... | collective-permute-start | bytes 589832 | tf_op jit(solution)/shard_map/f3_lon/ppermute | solution.py:229
  121.9 11.6 %copy-start.11 = (bf16[1024,512]{1,0:T(8,128)(2,1)S(1)}, bf16[1024,512]{1,0:T(8,128)(2,1)}, u32[]{:S(2)}) copy-start(bf16[1024,512]{1,0:T(8,128)(2,1)} %cot.3) | copy-start | bytes 3145732
  121.9 11.6 %copy-start.15 = (bf16[512,512]{1,0:T(8,128)(2,1)S(1)}, bf16[512,512]{1,0:T(8,128)(2,1)}, u32[]{:S(2)}) copy-start(bf16[512,512]{1,0:T(8,128)(2,1)} %enc_weight.1) | copy-start | bytes 1572868
  121.9 11.6 %copy-start.19 = (s32[1,9,256]{2,0,1:T(1,128)S(1)}, s32[1,9,256]{2,0,1:T(1,128)}, u32[]{:S(2)}) copy-start(s32[1,9,256]{2,0,1:T(1,128)} %param.19) | copy-start | bytes 27652
  128.2 11.0 %collective-permute-start.22 = (bf16[64,512]{1,0:T(8,128)(2,1)S(1)}, bf16[64,512]{1,0:T(8,128)(2,1)S(1)}, u32[]{:S(2)}, u32[]{:S(2)}) collective-permute-start(bf16[64,512]{1,0:T(8,128)(2,1)S(1)} %get-tuple-element.35), channel_id=1, source_target_pairs={{0,8},{16,24},{32,40},{48,56},{64,72},{80,88},{96,104},{112,120},{... | collective-permute-start | bytes 196616 | tf_op jit(solution)/shard_map/f3_lat/ppermute | solution.py:229
  133.5 6.4 %collective-permute-start.23 = (bf16[64,512]{1,0:T(8,128)(2,1)S(1)}, bf16[64,512]{1,0:T(8,128)(2,1)S(1)}, u32[]{:S(2)}, u32[]{:S(2)}) collective-permute-start(bf16[64,512]{1,0:T(8,128)(2,1)S(1)} %get-tuple-element.36), channel_id=1, source_target_pairs={{8,16},{24,32},{40,48},{56,64},{72,80},{88,96},{104,112},{120,0},{... | collective-permute-start | bytes 196616 | tf_op jit(solution)/shard_map/f3_lat/ppermute | solution.py:229
where the time goes:
time: 142 us; the launch traced here: 141 us
  Pallas kernels  54.1 us (38%)
  starting transfers between devices  52.3 us (37%)
  waiting for transfers between devices  21.9 us (15%)
  local copies, waits for them, and re-layouts  6 us (4%)
  matrix products  3.66 us (3%)
  other arithmetic  1.91 us (1%)
    pallas_call x9, Pallas kernels, kernel(): pl.pallas_call(body, out_shape=outs, in_specs=[SMEM] * smem + [VMEM] * (l...  54.1 us
    ppermute x24, starting transfers between devices, along(): return lambda value: lax.ppermute(value, axis, pairs)  52.3 us
    ppermute x24, waiting for transfers between devices, along(): return lambda value: lax.ppermute(value, axis, pairs)  21.9 us
    unnamed x48, local copies, waits for them, and re-layouts  5.97 us
  transfers between devices with their start and end apart: 24, of which 10 were waited for; matrix products, arithmetic and copies ran while one was open for 0% of the time, Pallas kernels for 28%

commit v1 on v0

v1 whole, which is shorter than its diff:
```python
import jax
import jax.numpy as jnp
from jax import lax
from jax.experimental import pallas as pl
from jax.experimental.pallas import tpu as pltpu
from jax.sharding import PartitionSpec as P

F32 = jnp.float32
BF16 = jnp.bfloat16
LANES = 128
CHUNK = 128
GROUP = 4

VMEM = pl.BlockSpec(memory_space=pltpu.VMEM)
SMEM = pl.BlockSpec(memory_space=pltpu.SMEM)


def mm(lhs, rhs):
    return jnp.dot(lhs, rhs, preferred_element_type=F32)


def mm_nt(lhs, rhs):
    return lax.dot_general(lhs, rhs, (((1,), (1,)), ((), ())), preferred_element_type=F32)


def as_hot(mask):
    return jnp.where(mask, 1.0, 0.0).astype(BF16)


def down_rows(index_row):
    return jnp.transpose(jnp.broadcast_to(index_row, (LANES, index_row.shape[1])))


def gather_hot(index_row, rows):
    spread = down_rows(index_row)
    lane = lax.broadcasted_iota(jnp.int32, spread.shape, 1)
    return jnp.concatenate(
        [as_hot(spread == lane + start) for start in range(0, rows, LANES)], axis=1
    )


def scatter_hot(index_row, rows, live):
    slots = index_row.shape[1]
    slot = lax.broadcasted_iota(jnp.int32, (1, slots), 1)
    index_row = jnp.where(slot < live, index_row, -1)
    return as_hot(lax.broadcasted_iota(jnp.int32, (rows, slots), 0) == index_row)


def gate(pre):
    return 0.5 * jnp.tanh(0.5 * pre) + 0.5


def list_chunks(counts, capacity, block, start, live):
    found = jnp.int32(0)
    for k in range(counts.shape[1]):
        count = counts[0, k]
        for at in range(0, capacity, CHUNK):
            block[found] = k
            start[found] = at
            live[found] = count - at
            found += (count > at).astype(jnp.int32)
    for j in range(GROUP - 1):
        block[found + j] = counts.shape[1] // 2
        start[found + j] = 0
        live[found + j] = 0
    return lax.div(found + (GROUP - 1), GROUP)


def each_group(groups, chunk_list, body):
    block, start, live = chunk_list

    @pl.loop(0, groups)
    def _(g):
        at = [GROUP * g + j for j in range(GROUP)]
        body([(block[n], pl.multiple_of(start[n], CHUNK), live[n]) for n in at])


def rows_of(index_ref, chunk):
    k, at, _ = chunk
    return index_ref[k, :, pl.ds(at, CHUNK)]


def place_of(k, flip):
    lat_offset = lax.div(k, 3) - 1
    first = 1 - 2 * flip
    slot = jnp.where(lat_offset == 0, 0, jnp.where(lat_offset == first, 1, 2))
    return 3 * lax.rem(k, 3) + slot


def gather_slots(counts, index_ref, table, out, chunk_list):
    groups = list_chunks(counts, index_ref.shape[2], *chunk_list)

    def body(chunks):
        hots = [gather_hot(rows_of(index_ref, c), table.shape[0]) for c in chunks]
        rows = mm(jnp.concatenate(hots, axis=0), table[...]).astype(BF16)
        for j, (k, at, _) in enumerate(chunks):
            out[k, pl.ds(at, CHUNK), :] = rows[j * CHUNK : (j + 1) * CHUNK]

    each_group(groups, chunk_list, body)


def enc_gather_kernel(counts, send, feat, weight, out, table, *chunk_list):
    table[...] = mm(feat[...], weight[...]).astype(BF16)
    gather_slots(counts, send, table, out, chunk_list)


def side_gather_kernel(counts, recv, feat, weight, bias, out, table, *chunk_list):
    table[...] = (mm(feat[...], weight[...]) + bias[...]).astype(BF16)
    gather_slots(counts, recv, table, out, chunk_list)


def back_gather_kernel(counts, recv, cot, weight, out, table, *chunk_list):
    table[...] = mm_nt(cot[...], weight[...]).astype(BF16)
    gather_slots(counts, recv, table, out, chunk_list)


def near_hot(index_row, rows):
    spread = down_rows(index_row)
    lane = lax.broadcasted_iota(jnp.int32, spread.shape, 1)
    return as_hot(spread == jnp.where(lane < rows, lane, lane - rows))


def edge_groups(counts, index_ref, flip, side, total, outs, chunk_list, edges):
    rows = total.shape[1]
    groups = list_chunks(counts, index_ref.shape[2], *chunk_list)
    total[...] = jnp.zeros(total.shape, F32)

    def body(chunks):
        for chunk in chunks:
            k, _, live = chunk
            place = place_of(k, flip[0])
            index_row = rows_of(index_ref, chunk)
            received = mm(near_hot(index_row, rows)[:, : side.shape[1]], side[place])
            value = edges(chunk, received)
            total[place] += mm(scatter_hot(index_row, rows, live), value)

    each_group(groups, chunk_list, body)
    for place, out in enumerate(outs):
        out[...] = total[3 * place : 3 * place + 3].astype(BF16)


def enc_forward_kernel(
    counts, flip, recv, left, own, right, weight, bias, sent,
    out_left, out_own, out_right, slope, side, total, *chunk_list,
):
    rows = own.shape[1]
    for place, near in enumerate((left, own, right)):
        feats = near[...].reshape(3 * rows, near.shape[2])
        exact = mm(feats, weight[...]) + bias[...]
        high = exact.astype(BF16)
        low = (exact - high.astype(F32)).astype(BF16)
        side[3 * place : 3 * place + 3, :rows, :] = high.reshape(3, rows, -1)
        side[3 * place : 3 * place + 3, rows:, :] = low.reshape(3, rows, -1)

    def edges(chunk, received):
        k, at, _ = chunk
        pre = sent[k, pl.ds(at, CHUNK), :].astype(F32) + received
        squashed = gate(pre)
        message = pre * squashed
        slope[k, pl.ds(at, CHUNK), :] = (squashed + message * (1.0 - squashed)).astype(BF16)
        return message.astype(BF16)

    outs = (out_left, out_own, out_right)
    edge_groups(counts, recv, flip, side, total, outs, chunk_list, edges)


def dec_kernel(
    counts, flip, send, left, own, right, side, back,
    out_left, out_own, out_right, messages, grads, near, total, *chunk_list,
):
    for place, tiles in enumerate((left, own, right)):
        near[3 * place : 3 * place + 3] = tiles[...]

    def edges(chunk, received):
        k, at, _ = chunk
        here = (k, pl.ds(at, CHUNK), slice(None))
        pre = side[here].astype(F32) + received
        squashed = gate(pre)
        message = pre * squashed
        messages[here] = message.astype(BF16)
        slope = squashed + message * (1.0 - squashed)
        grad = (back[here].astype(F32) * slope).astype(BF16)
        grads[here] = grad
        return grad

    outs = (out_left, out_own, out_right)
    edge_groups(counts, send, flip, near, total, outs, chunk_list, edges)


def enc_backward_kernel(
    counts, flip, recv, left, own, right, slope,
    out_left, out_own, out_right, grads, near, total, *chunk_list,
):
    for place, tiles in enumerate((left, own, right)):
        near[3 * place : 3 * place + 3] = tiles[...]

    def edges(chunk, received):
        k, at, _ = chunk
        here = (k, pl.ds(at, CHUNK), slice(None))
        grad = (received * slope[here].astype(F32)).astype(BF16)
        grads[here] = grad
        return grad

    outs = (out_left, out_own, out_right)
    edge_groups(counts, recv, flip, near, total, outs, chunk_list, edges)


def scatter_slots(counts, index_ref, values, total, chunk_list):
    groups = list_chunks(counts, index_ref.shape[2], *chunk_list)
    total[...] = jnp.zeros(total.shape, F32)

    def body(chunks):
        hots = [scatter_hot(rows_of(index_ref, c), total.shape[0], c[2]) for c in chunks]
        rows = [values[k, pl.ds(at, CHUNK), :] for k, at, _ in chunks]
        total[...] += mm(jnp.concatenate(hots, axis=1), jnp.concatenate(rows, axis=0))

    each_group(groups, chunk_list, body)


def dec_sum_kernel(counts, recv, messages, feat, weight, out, total, *chunk_list):
    scatter_slots(counts, recv, messages, total, chunk_list)
    out[...] = (feat[...].astype(F32) + mm(total[...].astype(BF16), weight[...])).astype(BF16)


def dec_local_kernel(counts, recv, grads, out, total, *chunk_list):
    scatter_slots(counts, recv, grads, total, chunk_list)
    out[...] = total[...].astype(BF16)


def enc_scatter_kernel(
    counts, send, grads, cot, local, dec_weight, enc_weight, out, total, *chunk_list
):
    scatter_slots(counts, send, grads, total, chunk_list)
    back = mm_nt(local[...], dec_weight[...])
    back += mm_nt(total[...].astype(BF16), enc_weight[...])
    out[...] = (cot[...].astype(F32) + back).astype(BF16)


def fold_kernel(own, east, west, kept, to_first, to_second):
    total = own[...].astype(F32) + east[...].astype(F32) + west[...].astype(F32)
    kept[...] = total[0]
    to_first[...] = total[1].astype(BF16)
    to_second[...] = total[2].astype(BF16)


def mesh_new_kernel(kept, first, second, feat, out_weight, weight, proj):
    summed = kept[...] + first[...].astype(F32) + second[...].astype(F32)
    update = mm(summed.astype(BF16), out_weight[...])
    proj[...] = mm((feat[...].astype(F32) + update).astype(BF16), weight[...]).astype(BF16)


def mesh_back_kernel(kept, first, second, weight, out_weight, back, enc_back):
    summed = kept[...] + first[...].astype(F32) + second[...].astype(F32)
    exact = mm_nt(summed.astype(BF16), weight[...])
    back[...] = exact
    enc_back[...] = mm_nt(exact.astype(BF16), out_weight[...]).astype(BF16)


def mesh_grad_kernel(kept, first, second, back, weight, out):
    summed = kept[...] + first[...].astype(F32) + second[...].astype(F32)
    out[...] = (back[...] + mm_nt(summed.astype(BF16), weight[...])).astype(BF16)


def along(axis, pairs):
    return lambda value: lax.ppermute(value, axis, pairs)


def lat_pairs(size, start):
    edges = [(i, (i + 1) % size) for i in range(start, size, 2)]
    return edges + [(j, i) for i, j in edges]


def on_device(
    grid_feat, mesh_feat, enc_send, enc_recv, enc_count, dec_send, dec_recv, dec_count,
    enc_src, enc_dst, enc_bias, enc_out, dec_src, dec_dst, dec_bias, dec_out, grid_cot,
):
    grid_rows, width = grid_feat.shape
    mesh_rows = mesh_feat.shape[0]
    cap_e = enc_send.shape[2]
    cap_d = dec_send.shape[2]
    lat_size = lax.axis_size("lat")
    lon_size = lax.axis_size("lon")
    flip = lax.rem(lax.axis_index("lat"), 2).astype(jnp.int32).reshape(1)
    first = along("lat", lat_pairs(lat_size, 0))
    second = along("lat", lat_pairs(lat_size, 1))
    east = along("lon", [(i, (i + 1) % lon_size) for i in range(lon_size)])
    west = along("lon", [((i + 1) % lon_size, i) for i in range(lon_size)])

    def spread(local_tile, name):
        with jax.named_scope(name + "_lat"):
            pieces = [local_tile, first(local_tile), second(local_tile)]
        with jax.named_scope(name + "_lon"):
            three = jnp.stack(pieces)
            return east(three), three, west(three)

    def fold(left, own, right, name):
        with jax.named_scope(name + "_lon"):
            arrived = west(left), east(right)
        kept, to_first, to_second = kernel(
            fold_kernel, [exact_tile, tile, tile], [], name + "_fold", own, *arrived, smem=0
        )
        with jax.named_scope(name + "_lat"):
            return kept, first(to_first), second(to_second)

    def kernel(body, outs, scratch, name, *args, smem=1, mib=12, work=0):
        with jax.named_scope(name):
            return pl.pallas_call(
                body,
                out_shape=outs,
                in_specs=[SMEM] * smem + [VMEM] * (len(args) - smem),
                out_specs=[VMEM] * len(outs),
                scratch_shapes=scratch,
                compiler_params=pltpu.CompilerParams(vmem_limit_bytes=mib * 1024 * 1024),
                cost_estimate=pl.CostEstimate(flops=work, bytes_accessed=0, transcendentals=0),
                name=name,
            )(*args)

    def array(*shape):
        return jax.ShapeDtypeStruct(shape, BF16)

    tile = array(mesh_rows, width)
    exact_tile = jax.ShapeDtypeStruct((mesh_rows, width), F32)
    three = [array(3, mesh_rows, width)] * 3
    enc_slots = [array(9, cap_e, width)]
    dec_slots = [array(9, cap_d, width)]
    grid_tile = [array(grid_rows, width)]
    chunk_list = [pltpu.SMEM((9 * cap_d // CHUNK + GROUP,), jnp.int32)] * 3
    rounded_grid = [pltpu.VMEM((grid_rows, width), BF16)] + chunk_list
    exact_grid = [pltpu.VMEM((grid_rows, width), F32)] + chunk_list
    near = pltpu.VMEM((9, mesh_rows, width), BF16)
    near_split = pltpu.VMEM((9, 2 * mesh_rows, width), BF16)
    near_total = pltpu.VMEM((9, mesh_rows, width), F32)
    enc_work = 2 * grid_rows * width * 9 * cap_e
    dec_work = 2 * grid_rows * width * 9 * cap_d

    enc_send, enc_recv, dec_send, dec_recv = (
        jnp.swapaxes(a, 0, 1) for a in (enc_send, enc_recv, dec_send, dec_recv)
    )

    near_feat = spread(mesh_feat, "e1")
    (sent,) = kernel(
        enc_gather_kernel, enc_slots, rounded_grid, "enc_gather",
        enc_count, enc_send, grid_feat, enc_src, work=enc_work,
    )
    (back_at,) = kernel(
        back_gather_kernel, dec_slots, rounded_grid, "back_gather",
        dec_count, dec_recv, grid_cot, dec_out, work=dec_work,
    )
    (side_at,) = kernel(
        side_gather_kernel, dec_slots, rounded_grid, "side_gather",
        dec_count, dec_recv, grid_feat, dec_dst, dec_bias.reshape(1, width), work=dec_work,
    )

    *enc_partial, slope = kernel(
        enc_forward_kernel, three + enc_slots,
        [near_split, near_total] + chunk_list, "enc_forward",
        enc_count, flip, enc_recv, *near_feat, enc_dst, enc_bias.reshape(1, width), sent,
        smem=2, work=enc_work // 4,
    )
    (dec_proj,) = kernel(
        mesh_new_kernel, [tile], [], "mesh_new",
        *fold(*enc_partial, "f1"), mesh_feat, enc_out, dec_src, smem=0,
    )

    *dec_partial, messages, dec_grads = kernel(
        dec_kernel, three + dec_slots * 2, [near, near_total] + chunk_list, "dec_edges",
        dec_count, flip, dec_send, *spread(dec_proj, "e2"), side_at, back_at,
        smem=2, work=dec_work // 4,
    )
    mesh_back, enc_back = kernel(
        mesh_back_kernel, [exact_tile, tile], [], "mesh_back",
        *fold(*dec_partial, "f2"), dec_src, enc_out, smem=0,
    )

    (grid_new,) = kernel(
        dec_sum_kernel, grid_tile, exact_grid, "dec_sum",
        dec_count, dec_recv, messages, grid_feat, dec_out, work=dec_work,
    )
    (local,) = kernel(
        dec_local_kernel, grid_tile, exact_grid, "dec_local",
        dec_count, dec_recv, dec_grads, work=dec_work,
    )

    *grad_partial, grads = kernel(
        enc_backward_kernel, three + enc_slots, [near, near_total] + chunk_list,
        "enc_backward",
        enc_count, flip, enc_recv, *spread(enc_back, "e3"), slope,
        smem=2, work=enc_work // 4,
    )
    (mesh_grad,) = kernel(
        mesh_grad_kernel, [tile], [], "mesh_grad",
        *fold(*grad_partial, "f3"), mesh_back, enc_dst, smem=0,
    )

    (grid_grad,) = kernel(
        enc_scatter_kernel, grid_tile, exact_grid, "enc_scatter",
        enc_count, enc_send, grads, grid_cot, local, dec_dst, enc_src, work=enc_work,
    )
    return grid_new, mesh_grad, grid_grad


def solution(mesh):
    rows = P(("lat", "lon"), None)
    edges = P(("lat", "lon"), None, None)
    return jax.shard_map(
        on_device,
        mesh=mesh,
        in_specs=(rows, rows, edges, edges, rows, edges, edges, rows)
        + (P(),) * 8
        + (rows,),
        out_specs=(rows, rows, rows),
        check_vma=False,
    )
```

time: 142 us -> 125 us (0.88)
  Pallas kernels: 54.1 us -> 46.1 us
  starting transfers between devices: 52.3 us -> 48 us
  matrix products: 3.66 us -> 0 us
  local copies, waits for them, and re-layouts: 6 us -> 3.7 us
    pallas_call x9 -> x15, Pallas kernels: 54.1 us -> 46.1 us  [kernel(): pl.pallas_call(body, out_shape=outs, in_specs=[SMEM] * smem + [VMEM] * (l...]
    ppermute x24, starting transfers between devices: 52.3 us -> 48 us  [along(): return lambda value: lax.ppermute(value, axis, pairs)]
    dot_general x4 -> x0, matrix products: 3.66 us -> none  [the longest x1 2.19 us: mm(): return jnp.dot(lhs, rhs, preferred_element_type=F32)]
    unnamed x48 -> x42, local copies, waits for them, and re-layouts: 5.97 us -> 3.7 us
  transfers between devices with their start and end apart: 24 -> 24, of which waited for: 10 -> 8; matrix products, arithmetic and copies ran while one was open for 0% -> 0% of each run, Pallas kernels for 28% -> 24%
where the time goes in v1:
time: 125 us; the launch traced here: 123 us
  starting transfers between devices  48 us (38%)
  Pallas kernels  46.1 us (37%)
  waiting for transfers between devices  23.1 us (18%)
  local copies, waits for them, and re-layouts  3.7 us (3%)
    ppermute x24, starting transfers between devices, along(): return lambda value: lax.ppermute(value, axis, pairs)  48 us
    pallas_call x15, Pallas kernels, kernel(): pl.pallas_call(body, out_shape=outs, in_specs=[SMEM] * smem + [VMEM] * (l...  46.1 us
    ppermute x24, waiting for transfers between devices, along(): return lambda value: lax.ppermute(value, axis, pairs)  23.1 us
    unnamed x42, local copies, waits for them, and re-layouts  3.7 us
  transfers between devices with their start and end apart: 24, of which 8 were waited for; matrix products, arithmetic and copies ran while one was open for 0% of the time, Pallas kernels for 24%

profile of v1, /device:TPU:1, one launch (start us, length us, event | category | flops | bytes accessed | tf_op | source)
XLA Modules:
  0.0 122.9 jit_solution(13309604007813977096)
XLA Ops:
  0.7 2.2 %collective-permute-start = (bf16[64,512]{1,0:T(8,128)(2,1)}, bf16[64,512]{1,0:T(8,128)(2,1)S(1)}, u32[]{:S(2)}, u32[]{:S(2)}) collective-permute-start(bf16[64,512]{1,0:T(8,128)(2,1)} %feat.5), channel_id=1, source_target_pairs={{0,8},{16,24},{32,40},{48,56},{64,72},{80,88},{96,104},{112,120},{... | collective-permute-start | bytes 196616 | tf_op jit(solution)/shard_map/e1_lat/ppermute | solution.py:265
  2.9 5.4 %collective-permute-start.1 = (bf16[64,512]{1,0:T(8,128)(2,1)}, bf16[64,512]{1,0:T(8,128)(2,1)S(1)}, u32[]{:S(2)}, u32[]{:S(2)}) collective-permute-start(bf16[64,512]{1,0:T(8,128)(2,1)} %feat.5), channel_id=1, source_target_pairs={{8,16},{24,32},{40,48},{56,64},{72,80},{88,96},{104,112},{120,0},{... | collective-permute-start | bytes 196616 | tf_op jit(solution)/shard_map/e1_lat/ppermute | solution.py:265
  8.2 0.0 collective-permute-done
  8.2 1.9 %collective-permute-done.1 = bf16[64,512]{1,0:T(8,128)(2,1)S(1)} collective-permute-done((bf16[64,512]{1,0:T(8,128)(2,1)}, bf16[64,512]{1,0:T(8,128)(2,1)S(1)}, u32[]{:S(2)}, u32[]{:S(2)}) %collective-permute-start.1) | collective-permute-done | bytes 65568 | tf_op jit(solution)/shard_map/e1_lat/ppermute | solution.py:265
  10.1 0.9 pad_maximum_fusion.own
  11.0 1.8 %collective-permute-start.3 = (bf16[3,64,512]{2,1,0:T(8,128)(2,1)S(1)}, bf16[3,64,512]{2,1,0:T(8,128)(2,1)S(1)}, u32[]{:S(2)}, u32[]{:S(2)}) collective-permute-start(bf16[3,64,512]{2,1,0:T(8,128)(2,1)S(1)} %pad_maximum_fusion.own), channel_id=1, source_target_pairs={{1,0},{2,1},{3,2},{4,3},{5,4},{6,5},{7,6},{0,7},{9,8},{10,9},{11,1... | collective-permute-start | bytes 589832 | tf_op jit(solution)/shard_map/e1_lon/ppermute | solution.py:265
  12.8 1.1 collective-permute-start.2
  14.0 0.7 copy-done.7
  14.6 1.2 copy-done.10
  15.8 1.0 copy-done.14
  16.9 0.7 copy-done.18
  17.6 3.5 %enc_gather.1.sent = bf16[9,256,512]{2,1,0:T(8,128)(2,1)S(1)} custom-call(s32[1,9]{1,0:T(1,128)S(1)} %copy-done.7, s32[9,1,256]{2,1,0:T(1,128)S(1)} %bitcast.27, bf16[1024,512]{1,0:T(8,128)(2,1)S(1)} %copy-done.10, bf16[512,512]{1,0:T(8,128)(2,1)S(1)} %copy-done.14), custom_call_target="tpu_custom_call" | custom-call | flops 2415919104 | tf_op jit(solution)/shard_map/enc_gather/enc_gather/pallas_call | solution.py:307
  21.1 0.0 copy-start.9
  21.1 0.0 copy-start.12
  21.1 0.0 copy-start.13
  21.1 0.0 copy-start.17
  21.2 0.0 collective-permute-done.3.right
  21.2 0.0 collective-permute-done.2.left
  21.2 4.7 %enc_forward.1 = (bf16[3,64,512]{2,1,0:T(8,128)(2,1)S(1)}, bf16[3,64,512]{2,1,0:T(8,128)(2,1)S(1)}, bf16[3,64,512]{2,1,0:T(8,128)(2,1)S(1)}, bf16[9,256,512]{2,1,0:T(8,128)(2,1)S(1)}) custom-call(s32[1,9]{1,0:T(1,128)S(1)} %copy-done.7, s32[1]{0:T(128)} %bitcast.1.flip, s32[9,1,256]{2,1,0:T(1,128)S(1)} %bitcast.19, ...), custom_call_target="tpu_custom_call" | custom-call | flops 603979776 | tf_op jit(solution)/shard_map/enc_forward/enc_forward/pallas_call | solution.py:307
  25.9 0.0 collective-permute-start.4
  25.9 1.7 %collective-permute-start.5 = (bf16[3,64,512]{2,1,0:T(8,128)(2,1)S(1)}, bf16[3,64,512]{2,1,0:T(8,128)(2,1)S(1)}, u32[]{:S(2)}, u32[]{:S(2)}) collective-permute-start(bf16[3,64,512]{2,1,0:T(8,128)(2,1)S(1)} %get-tuple-element.29), channel_id=1, source_target_pairs={{0,1},{1,2},{2,3},{3,4},{4,5},{5,6},{6,7},{7,0},{8,9},{9,10},{10,1... | collective-permute-start | bytes 589832 | tf_op jit(solution)/shard_map/f1_lon/ppermute | solution.py:265
  27.6 3.3 %collective-permute-done.4.east = bf16[3,64,512]{2,1,0:T(8,128)(2,1)S(1)} collective-permute-done((bf16[3,64,512]{2,1,0:T(8,128)(2,1)S(1)}, bf16[3,64,512]{2,1,0:T(8,128)(2,1)S(1)}, u32[]{:S(2)}, u32[]{:S(2)}) %collective-permute-start.4) | collective-permute-done | bytes 196640 | tf_op jit(solution)/shard_map/f1_lon/ppermute | solution.py:265
  31.0 0.1 f1_fold.1
  31.1 0.1 collective-permute-start.6
  31.2 5.1 %collective-permute-start.7 = (bf16[64,512]{1,0:T(8,128)(2,1)S(1)}, bf16[64,512]{1,0:T(8,128)(2,1)S(1)}, u32[]{:S(2)}, u32[]{:S(2)}) collective-permute-start(bf16[64,512]{1,0:T(8,128)(2,1)S(1)} %get-tuple-element.32), channel_id=1, source_target_pairs={{8,16},{24,32},{40,48},{56,64},{72,80},{88,96},{104,112},{120,0},{... | collective-permute-start | bytes 196616 | tf_op jit(solution)/shard_map/f1_lat/ppermute | solution.py:265
  36.3 1.7 %collective-permute-done.7.second = bf16[64,512]{1,0:T(8,128)(2,1)S(1)} collective-permute-done((bf16[64,512]{1,0:T(8,128)(2,1)S(1)}, bf16[64,512]{1,0:T(8,128)(2,1)S(1)}, u32[]{:S(2)}, u32[]{:S(2)}) %collective-permute-start.7) | collective-permute-done | bytes 65568 | tf_op jit(solution)/shard_map/f1_lat/ppermute | solution.py:265
  37.9 0.4 mesh_new.1
  38.3 4.9 %collective-permute-start.9 = (bf16[64,512]{1,0:T(8,128)(2,1)S(1)}, bf16[64,512]{1,0:T(8,128)(2,1)S(1)}, u32[]{:S(2)}, u32[]{:S(2)}) collective-permute-start(bf16[64,512]{1,0:T(8,128)(2,1)S(1)} %mesh_new.1), channel_id=1, source_target_pairs={{8,16},{24,32},{40,48},{56,64},{72,80},{88,96},{104,112},{120,0},{... | collective-permute-start | bytes 196616 | tf_op jit(solution)/shard_map/e2_lat/ppermute | solution.py:265
  43.2 0.0 copy-start.11
  43.2 0.0 copy-start.16
  43.2 0.0 copy-start.20
  43.3 5.1 %back_gather.1.back = bf16[9,512,512]{2,1,0:T(8,128)(2,1)S(1)} custom-call(s32[1,9]{1,0:T(1,128)S(1)} %copy-done.9, s32[9,1,512]{2,1,0:T(1,128)S(1)} %bitcast.23, bf16[1024,512]{1,0:T(8,128)(2,1)S(1)} %copy-done.12, bf16[512,512]{1,0:T(8,128)(2,1)S(1)} %copy-done.13), custom_call_target="tpu_custom_call" | custom-call | flops 4831838208 | tf_op jit(solution)/shard_map/back_gather/back_gather/pallas_call | solution.py:307
  48.4 0.0 collective-permute-done.8
  48.4 6.1 %collective-permute-start.11 = (bf16[3,64,512]{2,1,0:T(8,128)(2,1)S(1)}, bf16[3,64,512]{2,1,0:T(8,128)(2,1)S(1)}, u32[]{:S(2)}, u32[]{:S(2)}) collective-permute-start(bf16[3,64,512]{2,1,0:T(8,128)(2,1)S(1)} %pad_maximum_fusion.1.own), channel_id=1, source_target_pairs={{1,0},{2,1},{3,2},{4,3},{5,4},{6,5},{7,6},{0,7},{9,8},{10,9},{11,1... | collective-permute-start | bytes 589832 | tf_op jit(solution)/shard_map/e2_lon/ppermute | solution.py:265
  54.5 0.0 collective-permute-start.10
  54.6 0.0 copy-start.5
  54.6 5.0 %side_gather.1.side = bf16[9,512,512]{2,1,0:T(8,128)(2,1)S(1)} custom-call(s32[1,9]{1,0:T(1,128)S(1)} %copy-done.9, s32[9,1,512]{2,1,0:T(1,128)S(1)} %bitcast.24, bf16[1024,512]{1,0:T(8,128)(2,1)S(1)} %copy-done.11, bf16[512,512]{1,0:T(8,128)(2,1)S(1)} %copy-done.16, f32[1,512]{1,0:T(1,128)S(1)} %bitcast.29), custom_call_target="tpu_custom_call" | custom-call | flops 4831838208 | tf_op jit(solution)/shard_map/side_gather/side_gather/pallas_call | solution.py:307
  59.6 0.0 collective-permute-done.11.right
  59.6 7.0 %dec_edges.1 = (bf16[3,64,512]{2,1,0:T(8,128)(2,1)S(1)}, bf16[3,64,512]{2,1,0:T(8,128)(2,1)S(1)}, bf16[3,64,512]{2,1,0:T(8,128)(2,1)S(1)}, bf16[9,512,512]{2,1,0:T(8,128)(2,1)S(1)}, bf16[9,512,512]{2,1,0:T(8,128)(2,1)S(1)}) custom-call(s32[1,9]{1,0:T(1,128)S(1)} %copy-done.9, s32[1]{0:T(128)} %bitcast.1.flip, s32[9,1,512]{2,1,0:T(1,128)S(1)} %bitcast.21, ...), custom_call_target="tpu_custom_call" | custom-call | flops 1207959552 | tf_op jit(solution)/shard_map/dec_edges/dec_edges/pallas_call | solution.py:307
  66.7 2.5 %collective-permute-start.12 = (bf16[3,64,512]{2,1,0:T(8,128)(2,1)S(1)}, bf16[3,64,512]{2,1,0:T(8,128)(2,1)S(1)}, u32[]{:S(2)}, u32[]{:S(2)}) collective-permute-start(bf16[3,64,512]{2,1,0:T(8,128)(2,1)S(1)} %get-tuple-element.35), channel_id=1, source_target_pairs={{1,0},{2,1},{3,2},{4,3},{5,4},{6,5},{7,6},{0,7},{9,8},{10,9},{11,1... | collective-permute-start | bytes 589832 | tf_op jit(solution)/shard_map/f2_lon/ppermute | solution.py:265
  69.2 2.6 %collective-permute-done.12.east = bf16[3,64,512]{2,1,0:T(8,128)(2,1)S(1)} collective-permute-done((bf16[3,64,512]{2,1,0:T(8,128)(2,1)S(1)}, bf16[3,64,512]{2,1,0:T(8,128)(2,1)S(1)}, u32[]{:S(2)}, u32[]{:S(2)}) %collective-permute-start.12) | collective-permute-done | bytes 196640 | tf_op jit(solution)/shard_map/f2_lon/ppermute | solution.py:265
  71.8 0.8 collective-permute-done.13.west
  72.6 0.1 f2_fold.1
  72.7 3.8 %collective-permute-start.14 = (bf16[64,512]{1,0:T(8,128)(2,1)S(1)}, bf16[64,512]{1,0:T(8,128)(2,1)S(1)}, u32[]{:S(2)}, u32[]{:S(2)}) collective-permute-start(bf16[64,512]{1,0:T(8,128)(2,1)S(1)} %get-tuple-element.38), channel_id=1, source_target_pairs={{0,8},{16,24},{32,40},{48,56},{64,72},{80,88},{96,104},{112,120},{... | collective-permute-start | bytes 196616 | tf_op jit(solution)/shard_map/f2_lat/ppermute | solution.py:265
  76.5 0.0 collective-permute-start.15
  76.5 1.7 %collective-permute-done.14.first = bf16[64,512]{1,0:T(8,128)(2,1)S(1)} collective-permute-done((bf16[64,512]{1,0:T(8,128)(2,1)S(1)}, bf16[64,512]{1,0:T(8,128)(2,1)S(1)}, u32[]{:S(2)}, u32[]{:S(2)}) %collective-permute-start.14) | collective-permute-done | bytes 65568 | tf_op jit(solution)/shard_map/f2_lat/ppermute | solution.py:265
  78.2 4.8 %collective-permute-done.15.second = bf16[64,512]{1,0:T(8,128)(2,1)S(1)} collective-permute-done((bf16[64,512]{1,0:T(8,128)(2,1)S(1)}, bf16[64,512]{1,0:T(8,128)(2,1)S(1)}, u32[]{:S(2)}, u32[]{:S(2)}) %collective-permute-start.15) | collective-permute-done | bytes 65568 | tf_op jit(solution)/shard_map/f2_lat/ppermute | solution.py:265
  83.0 0.5 mesh_back.1
  83.4 0.1 collective-permute-start.17
  83.5 0.1 collective-permute-start.16
  83.6 6.3 %collective-permute-done.17 = bf16[64,512]{1,0:T(8,128)(2,1)S(1)} collective-permute-done((bf16[64,512]{1,0:T(8,128)(2,1)S(1)}, bf16[64,512]{1,0:T(8,128)(2,1)S(1)}, u32[]{:S(2)}, u32[]{:S(2)}) %collective-permute-start.17) | collective-permute-done | bytes 65568 | tf_op jit(solution)/shard_map/e3_lat/ppermute | solution.py:265
  90.0 8.0 %collective-permute-start.19 = (bf16[3,64,512]{2,1,0:T(8,128)(2,1)S(1)}, bf16[3,64,512]{2,1,0:T(8,128)(2,1)S(1)}, u32[]{:S(2)}, u32[]{:S(2)}) collective-permute-start(bf16[3,64,512]{2,1,0:T(8,128)(2,1)S(1)} %pad_maximum_fusion.2.own), channel_id=1, source_target_pairs={{1,0},{2,1},{3,2},{4,3},{5,4},{6,5},{7,6},{0,7},{9,8},{10,9},{11,1... | collective-permute-start | bytes 589832 | tf_op jit(solution)/shard_map/e3_lon/ppermute | solution.py:265
  98.0 0.0 collective-permute-start.18
  98.0 5.9 %dec_sum.1 = bf16[1024,512]{1,0:T(8,128)(2,1)} custom-call(s32[1,9]{1,0:T(1,128)S(1)} %copy-done.9, s32[9,1,512]{2,1,0:T(1,128)S(1)} %bitcast.25, bf16[9,512,512]{2,1,0:T(8,128)(2,1)S(1)} %get-tuple-element.33.messages, bf16[1024,512]{1,0:T(8,128)(2,1)S(1)} %copy-done.11, bf16[512,512]{1,0:T(8,128)(2,1)S(1)} %copy-done.13), custom_call_target="tpu_custom_call" | custom-call | flops 4831838208 | tf_op jit(solution)/shard_map/dec_sum/dec_sum/pallas_call | solution.py:307
  103.9 3.5 %enc_backward.1 = (bf16[3,64,512]{2,1,0:T(8,128)(2,1)S(1)}, bf16[3,64,512]{2,1,0:T(8,128)(2,1)S(1)}, bf16[3,64,512]{2,1,0:T(8,128)(2,1)S(1)}, bf16[9,256,512]{2,1,0:T(8,128)(2,1)S(1)}) custom-call(s32[1,9]{1,0:T(1,128)S(1)} %copy-done.8, s32[1]{0:T(128)} %bitcast.1.flip, s32[9,1,256]{2,1,0:T(1,128)S(1)} %bitcast.20, ...), custom_call_target="tpu_custom_call" | custom-call | flops 603979776 | tf_op jit(solution)/shard_map/enc_backward/enc_backward/pallas_call | solution.py:307
  107.3 1.2 %collective-permute-start.20 = (bf16[3,64,512]{2,1,0:T(8,128)(2,1)S(1)}, bf16[3,64,512]{2,1,0:T(8,128)(2,1)S(1)}, u32[]{:S(2)}, u32[]{:S(2)}) collective-permute-start(bf16[3,64,512]{2,1,0:T(8,128)(2,1)S(1)} %get-tuple-element.43), channel_id=1, source_target_pairs={{1,0},{2,1},{3,2},{4,3},{5,4},{6,5},{7,6},{0,7},{9,8},{10,9},{11,1... | collective-permute-start | bytes 589832 | tf_op jit(solution)/shard_map/f3_lon/ppermute | solution.py:265
  108.6 0.5 collective-permute-start.21
  109.1 4.3 %dec_local.1.local = bf16[1024,512]{1,0:T(8,128)(2,1)S(1)} custom-call(s32[1,9]{1,0:T(1,128)S(1)} %copy-done.9, s32[9,1,512]{2,1,0:T(1,128)S(1)} %bitcast.26, bf16[9,512,512]{2,1,0:T(8,128)(2,1)S(1)} %get-tuple-element.50.grads), custom_call_target="tpu_custom_call" | custom-call | flops 4831838208 | tf_op jit(solution)/shard_map/dec_local/dec_local/pallas_call | solution.py:307
  113.4 0.0 collective-permute-done.21.west
  113.4 0.1 f3_fold.1
  113.5 0.1 collective-permute-start.22
  113.6 3.2 %collective-permute-start.23 = (bf16[64,512]{1,0:T(8,128)(2,1)S(1)}, bf16[64,512]{1,0:T(8,128)(2,1)S(1)}, u32[]{:S(2)}, u32[]{:S(2)}) collective-permute-start(bf16[64,512]{1,0:T(8,128)(2,1)S(1)} %get-tuple-element.47), channel_id=1, source_target_pairs={{8,16},{24,32},{40,48},{56,64},{72,80},{88,96},{104,112},{120,0},{... | collective-permute-start | bytes 196616 | tf_op jit(solution)/shard_map/f3_lat/ppermute | solution.py:265
  116.9 5.1 %enc_scatter.1 = bf16[1024,512]{1,0:T(8,128)(2,1)} custom-call(s32[1,9]{1,0:T(1,128)S(1)} %copy-done.8, s32[9,1,256]{2,1,0:T(1,128)S(1)} %bitcast.28, bf16[9,256,512]{2,1,0:T(8,128)(2,1)S(1)} %get-tuple-element.49.grads, bf16[1024,512]{1,0:T(8,128)(2,1)S(1)} %copy-done.12, bf16[1024,512]{1,0:T(8,128)(2,1)S(1)} %dec_local.1.local, ...), custom_call_target="tpu_custom_call" | custom-call | flops 2415919104 | tf_op jit(solution)/shard_map/enc_scatter/enc_scatter/pallas_call | solution.py:307
  121.9 0.9 mesh_grad.1
  (44 shorter events, 0.1 us)
Async XLA Ops:
  0.6 20.6 %copy-start.2 = (bf16[512,512]{1,0:T(8,128)(2,1)S(1)}, bf16[512,512]{1,0:T(8,128)(2,1)}, u32[]{:S(2)}) copy-start(bf16[512,512]{1,0:T(8,128)(2,1)} %weight.15) | copy-start | bytes 1572868
  0.6 20.6 %copy-start.6 = (f32[512]{0:T(512)S(1)}, f32[512]{0:T(512)}, u32[]{:S(2)}) copy-start(f32[512]{0:T(512)} %param.27) | copy-start | bytes 6148
  0.7 20.6 %copy-start.4 = (s32[1,9,256]{2,0,1:T(1,128)S(1)}, s32[1,9,256]{2,0,1:T(1,128)}, u32[]{:S(2)}) copy-start(s32[1,9,256]{2,0,1:T(1,128)} %param.20) | copy-start | bytes 27652
  0.7 7.6 %collective-permute-start = (bf16[64,512]{1,0:T(8,128)(2,1)}, bf16[64,512]{1,0:T(8,128)(2,1)S(1)}, u32[]{:S(2)}, u32[]{:S(2)}) collective-permute-start(bf16[64,512]{1,0:T(8,128)(2,1)} %feat.5), channel_id=1, source_target_pairs={{0,8},{16,24},{32,40},{48,56},{64,72},{80,88},{96,104},{112,120},{... | collective-permute-start | bytes 196616 | tf_op jit(solution)/shard_map/e1_lat/ppermute | solution.py:265
  2.9 7.3 %collective-permute-start.1 = (bf16[64,512]{1,0:T(8,128)(2,1)}, bf16[64,512]{1,0:T(8,128)(2,1)S(1)}, u32[]{:S(2)}, u32[]{:S(2)}) collective-permute-start(bf16[64,512]{1,0:T(8,128)(2,1)} %feat.5), channel_id=1, source_target_pairs={{8,16},{24,32},{40,48},{56,64},{72,80},{88,96},{104,112},{120,0},{... | collective-permute-start | bytes 196616 | tf_op jit(solution)/shard_map/e1_lat/ppermute | solution.py:265
  11.0 10.2 %collective-permute-start.3 = (bf16[3,64,512]{2,1,0:T(8,128)(2,1)S(1)}, bf16[3,64,512]{2,1,0:T(8,128)(2,1)S(1)}, u32[]{:S(2)}, u32[]{:S(2)}) collective-permute-start(bf16[3,64,512]{2,1,0:T(8,128)(2,1)S(1)} %pad_maximum_fusion.own), channel_id=1, source_target_pairs={{1,0},{2,1},{3,2},{4,3},{5,4},{6,5},{7,6},{0,7},{9,8},{10,9},{11,1... | collective-permute-start | bytes 589832 | tf_op jit(solution)/shard_map/e1_lon/ppermute | solution.py:265
  12.8 8.3 %collective-permute-start.2 = (bf16[3,64,512]{2,1,0:T(8,128)(2,1)S(1)}, bf16[3,64,512]{2,1,0:T(8,128)(2,1)S(1)}, u32[]{:S(2)}, u32[]{:S(2)}) collective-permute-start(bf16[3,64,512]{2,1,0:T(8,128)(2,1)S(1)} %pad_maximum_fusion.own), channel_id=1, source_target_pairs={{0,1},{1,2},{2,3},{3,4},{4,5},{5,6},{6,7},{7,0},{8,9},{9,10},{10,1... | collective-permute-start | bytes 589832 | tf_op jit(solution)/shard_map/e1_lon/ppermute | solution.py:265
  13.9 0.7 copy-start.7
  14.6 1.2 copy-start.10
  15.8 1.0 copy-start.14
  16.9 0.7 copy-start.18
  17.6 20.4 %copy-start = (bf16[512,512]{1,0:T(8,128)(2,1)S(1)}, bf16[512,512]{1,0:T(8,128)(2,1)}, u32[]{:S(2)}) copy-start(bf16[512,512]{1,0:T(8,128)(2,1)} %out_weight.3) | copy-start | bytes 1572868
  17.6 20.4 %copy-start.1 = (bf16[512,512]{1,0:T(8,128)(2,1)S(1)}, bf16[512,512]{1,0:T(8,128)(2,1)}, u32[]{:S(2)}) copy-start(bf16[512,512]{1,0:T(8,128)(2,1)} %weight.14) | copy-start | bytes 1572868
  17.6 20.4 %copy-start.3 = (bf16[64,512]{1,0:T(8,128)(2,1)S(1)}, bf16[64,512]{1,0:T(8,128)(2,1)}, u32[]{:S(2)}) copy-start(bf16[64,512]{1,0:T(8,128)(2,1)} %feat.5) | copy-start | bytes 196612
  21.1 22.1 %copy-start.9 = (s32[1,9]{1,0:T(1,128)S(1)}, s32[1,9]{1,0:T(1,128)}, u32[]{:S(2)}) copy-start(s32[1,9]{1,0:T(1,128)} %counts.16) | copy-start | bytes 112
  21.1 22.1 %copy-start.12 = (bf16[1024,512]{1,0:T(8,128)(2,1)S(1)}, bf16[1024,512]{1,0:T(8,128)(2,1)}, u32[]{:S(2)}) copy-start(bf16[1024,512]{1,0:T(8,128)(2,1)} %cot.3) | copy-start | bytes 3145732
  21.1 22.1 %copy-start.13 = (bf16[512,512]{1,0:T(8,128)(2,1)S(1)}, bf16[512,512]{1,0:T(8,128)(2,1)}, u32[]{:S(2)}) copy-start(bf16[512,512]{1,0:T(8,128)(2,1)} %weight.13) | copy-start | bytes 1572868
  21.1 22.1 %copy-start.17 = (s32[1,9,512]{2,0,1:T(1,128)S(1)}, s32[1,9,512]{2,0,1:T(1,128)}, u32[]{:S(2)}) copy-start(s32[1,9,512]{2,0,1:T(1,128)} %param.23) | copy-start | bytes 55300
  25.9 5.1 %collective-permute-start.4 = (bf16[3,64,512]{2,1,0:T(8,128)(2,1)S(1)}, bf16[3,64,512]{2,1,0:T(8,128)(2,1)S(1)}, u32[]{:S(2)}, u32[]{:S(2)}) collective-permute-start(bf16[3,64,512]{2,1,0:T(8,128)(2,1)S(1)} %get-tuple-element.28), channel_id=1, source_target_pairs={{1,0},{2,1},{3,2},{4,3},{5,4},{6,5},{7,6},{0,7},{9,8},{10,9},{11,1... | collective-permute-start | bytes 589832 | tf_op jit(solution)/shard_map/f1_lon/ppermute | solution.py:265
  25.9 5.1 %collective-permute-start.5 = (bf16[3,64,512]{2,1,0:T(8,128)(2,1)S(1)}, bf16[3,64,512]{2,1,0:T(8,128)(2,1)S(1)}, u32[]{:S(2)}, u32[]{:S(2)}) collective-permute-start(bf16[3,64,512]{2,1,0:T(8,128)(2,1)S(1)} %get-tuple-element.29), channel_id=1, source_target_pairs={{0,1},{1,2},{2,3},{3,4},{4,5},{5,6},{6,7},{7,0},{8,9},{9,10},{10,1... | collective-permute-start | bytes 589832 | tf_op jit(solution)/shard_map/f1_lon/ppermute | solution.py:265
  31.1 5.2 %collective-permute-start.6 = (bf16[64,512]{1,0:T(8,128)(2,1)S(1)}, bf16[64,512]{1,0:T(8,128)(2,1)S(1)}, u32[]{:S(2)}, u32[]{:S(2)}) collective-permute-start(bf16[64,512]{1,0:T(8,128)(2,1)S(1)} %get-tuple-element.31), channel_id=1, source_target_pairs={{0,8},{16,24},{32,40},{48,56},{64,72},{80,88},{96,104},{112,120},{... | collective-permute-start | bytes 196616 | tf_op jit(solution)/shard_map/f1_lat/ppermute | solution.py:265
  31.2 6.8 %collective-permute-start.7 = (bf16[64,512]{1,0:T(8,128)(2,1)S(1)}, bf16[64,512]{1,0:T(8,128)(2,1)S(1)}, u32[]{:S(2)}, u32[]{:S(2)}) collective-permute-start(bf16[64,512]{1,0:T(8,128)(2,1)S(1)} %get-tuple-element.32), channel_id=1, source_target_pairs={{8,16},{24,32},{40,48},{56,64},{72,80},{88,96},{104,112},{120,0},{... | collective-permute-start | bytes 196616 | tf_op jit(solution)/shard_map/f1_lat/ppermute | solution.py:265
  38.3 10.0 %collective-permute-start.9 = (bf16[64,512]{1,0:T(8,128)(2,1)S(1)}, bf16[64,512]{1,0:T(8,128)(2,1)S(1)}, u32[]{:S(2)}, u32[]{:S(2)}) collective-permute-start(bf16[64,512]{1,0:T(8,128)(2,1)S(1)} %mesh_new.1), channel_id=1, source_target_pairs={{8,16},{24,32},{40,48},{56,64},{72,80},{88,96},{104,112},{120,0},{... | collective-permute-start | bytes 196616 | tf_op jit(solution)/shard_map/e2_lat/ppermute | solution.py:265
  43.2 5.2 %collective-permute-start.8 = (bf16[64,512]{1,0:T(8,128)(2,1)S(1)}, bf16[64,512]{1,0:T(8,128)(2,1)S(1)}, u32[]{:S(2)}, u32[]{:S(2)}) collective-permute-start(bf16[64,512]{1,0:T(8,128)(2,1)S(1)} %mesh_new.1), channel_id=1, source_target_pairs={{0,8},{16,24},{32,40},{48,56},{64,72},{80,88},{96,104},{112,120},{... | collective-permute-start | bytes 196616 | tf_op jit(solution)/shard_map/e2_lat/ppermute | solution.py:265
  43.2 11.3 %copy-start.11 = (bf16[1024,512]{1,0:T(8,128)(2,1)S(1)}, bf16[1024,512]{1,0:T(8,128)(2,1)}, u32[]{:S(2)}) copy-start(bf16[1024,512]{1,0:T(8,128)(2,1)} %feat.7) | copy-start | bytes 3145732
  43.2 11.3 %copy-start.16 = (bf16[512,512]{1,0:T(8,128)(2,1)S(1)}, bf16[512,512]{1,0:T(8,128)(2,1)}, u32[]{:S(2)}) copy-start(bf16[512,512]{1,0:T(8,128)(2,1)} %dec_weight.1) | copy-start | bytes 1572868
  43.2 11.3 %copy-start.20 = (f32[512]{0:T(512)S(1)}, f32[512]{0:T(512)}, u32[]{:S(2)}) copy-start(f32[512]{0:T(512)} %param.31) | copy-start | bytes 6148
  48.4 11.2 %collective-permute-start.11 = (bf16[3,64,512]{2,1,0:T(8,128)(2,1)S(1)}, bf16[3,64,512]{2,1,0:T(8,128)(2,1)S(1)}, u32[]{:S(2)}, u32[]{:S(2)}) collective-permute-start(bf16[3,64,512]{2,1,0:T(8,128)(2,1)S(1)} %pad_maximum_fusion.1.own), channel_id=1, source_target_pairs={{1,0},{2,1},{3,2},{4,3},{5,4},{6,5},{7,6},{0,7},{9,8},{10,9},{11,1... | collective-permute-start | bytes 589832 | tf_op jit(solution)/shard_map/e2_lon/ppermute | solution.py:265
  54.5 5.1 %collective-permute-start.10 = (bf16[3,64,512]{2,1,0:T(8,128)(2,1)S(1)}, bf16[3,64,512]{2,1,0:T(8,128)(2,1)S(1)}, u32[]{:S(2)}, u32[]{:S(2)}) collective-permute-start(bf16[3,64,512]{2,1,0:T(8,128)(2,1)S(1)} %pad_maximum_fusion.1.own), channel_id=1, source_target_pairs={{0,1},{1,2},{2,3},{3,4},{4,5},{5,6},{6,7},{7,0},{8,9},{9,10},{10,1... | collective-permute-start | bytes 589832 | tf_op jit(solution)/shard_map/e2_lon/ppermute | solution.py:265
  54.6 5.1 %copy-start.5 = (s32[1,9,512]{2,0,1:T(1,128)S(1)}, s32[1,9,512]{2,0,1:T(1,128)}, u32[]{:S(2)}) copy-start(s32[1,9,512]{2,0,1:T(1,128)} %param.22) | copy-start | bytes 55300
  66.7 5.1 %collective-permute-start.12 = (bf16[3,64,512]{2,1,0:T(8,128)(2,1)S(1)}, bf16[3,64,512]{2,1,0:T(8,128)(2,1)S(1)}, u32[]{:S(2)}, u32[]{:S(2)}) collective-permute-start(bf16[3,64,512]{2,1,0:T(8,128)(2,1)S(1)} %get-tuple-element.35), channel_id=1, source_target_pairs={{1,0},{2,1},{3,2},{4,3},{5,4},{6,5},{7,6},{0,7},{9,8},{10,9},{11,1... | collective-permute-start | bytes 589832 | tf_op jit(solution)/shard_map/f2_lon/ppermute | solution.py:265
  69.2 3.4 %collective-permute-start.13 = (bf16[3,64,512]{2,1,0:T(8,128)(2,1)S(1)}, bf16[3,64,512]{2,1,0:T(8,128)(2,1)S(1)}, u32[]{:S(2)}, u32[]{:S(2)}) collective-permute-start(bf16[3,64,512]{2,1,0:T(8,128)(2,1)S(1)} %get-tuple-element.36), channel_id=1, source_target_pairs={{0,1},{1,2},{2,3},{3,4},{4,5},{5,6},{6,7},{7,0},{8,9},{9,10},{10,1... | collective-permute-start | bytes 589832 | tf_op jit(solution)/shard_map/f2_lon/ppermute | solution.py:265
  72.7 5.5 %collective-permute-start.14 = (bf16[64,512]{1,0:T(8,128)(2,1)S(1)}, bf16[64,512]{1,0:T(8,128)(2,1)S(1)}, u32[]{:S(2)}, u32[]{:S(2)}) collective-permute-start(bf16[64,512]{1,0:T(8,128)(2,1)S(1)} %get-tuple-element.38), channel_id=1, source_target_pairs={{0,8},{16,24},{32,40},{48,56},{64,72},{80,88},{96,104},{112,120},{... | collective-permute-start | bytes 196616 | tf_op jit(solution)/shard_map/f2_lat/ppermute | solution.py:265
  76.5 6.4 %collective-permute-start.15 = (bf16[64,512]{1,0:T(8,128)(2,1)S(1)}, bf16[64,512]{1,0:T(8,128)(2,1)S(1)}, u32[]{:S(2)}, u32[]{:S(2)}) collective-permute-start(bf16[64,512]{1,0:T(8,128)(2,1)S(1)} %get-tuple-element.39), channel_id=1, source_target_pairs={{8,16},{24,32},{40,48},{56,64},{72,80},{88,96},{104,112},{120,0},{... | collective-permute-start | bytes 196616 | tf_op jit(solution)/shard_map/f2_lat/ppermute | solution.py:265
  83.4 6.5 %collective-permute-start.17 = (bf16[64,512]{1,0:T(8,128)(2,1)S(1)}, bf16[64,512]{1,0:T(8,128)(2,1)S(1)}, u32[]{:S(2)}, u32[]{:S(2)}) collective-permute-start(bf16[64,512]{1,0:T(8,128)(2,1)S(1)} %get-tuple-element.40), channel_id=1, source_target_pairs={{8,16},{24,32},{40,48},{56,64},{72,80},{88,96},{104,112},{120,0},{... | collective-permute-start | bytes 196616 | tf_op jit(solution)/shard_map/e3_lat/ppermute | solution.py:265
  83.5 6.4 %collective-permute-start.16 = (bf16[64,512]{1,0:T(8,128)(2,1)S(1)}, bf16[64,512]{1,0:T(8,128)(2,1)S(1)}, u32[]{:S(2)}, u32[]{:S(2)}) collective-permute-start(bf16[64,512]{1,0:T(8,128)(2,1)S(1)} %get-tuple-element.40), channel_id=1, source_target_pairs={{0,8},{16,24},{32,40},{48,56},{64,72},{80,88},{96,104},{112,120},{... | collective-permute-start | bytes 196616 | tf_op jit(solution)/shard_map/e3_lat/ppermute | solution.py:265
  90.0 13.9 %collective-permute-start.19 = (bf16[3,64,512]{2,1,0:T(8,128)(2,1)S(1)}, bf16[3,64,512]{2,1,0:T(8,128)(2,1)S(1)}, u32[]{:S(2)}, u32[]{:S(2)}) collective-permute-start(bf16[3,64,512]{2,1,0:T(8,128)(2,1)S(1)} %pad_maximum_fusion.2.own), channel_id=1, source_target_pairs={{1,0},{2,1},{3,2},{4,3},{5,4},{6,5},{7,6},{0,7},{9,8},{10,9},{11,1... | collective-permute-start | bytes 589832 | tf_op jit(solution)/shard_map/e3_lon/ppermute | solution.py:265
  98.0 5.9 %collective-permute-start.18 = (bf16[3,64,512]{2,1,0:T(8,128)(2,1)S(1)}, bf16[3,64,512]{2,1,0:T(8,128)(2,1)S(1)}, u32[]{:S(2)}, u32[]{:S(2)}) collective-permute-start(bf16[3,64,512]{2,1,0:T(8,128)(2,1)S(1)} %pad_maximum_fusion.2.own), channel_id=1, source_target_pairs={{0,1},{1,2},{2,3},{3,4},{4,5},{5,6},{6,7},{7,0},{8,9},{9,10},{10,1... | collective-permute-start | bytes 589832 | tf_op jit(solution)/shard_map/e3_lon/ppermute | solution.py:265
  98.0 5.9 %copy-start.8 = (s32[1,9]{1,0:T(1,128)S(1)}, s32[1,9]{1,0:T(1,128)}, u32[]{:S(2)}) copy-start(s32[1,9]{1,0:T(1,128)} %counts.17) | copy-start | bytes 112
  107.3 6.1 %collective-permute-start.20 = (bf16[3,64,512]{2,1,0:T(8,128)(2,1)S(1)}, bf16[3,64,512]{2,1,0:T(8,128)(2,1)S(1)}, u32[]{:S(2)}, u32[]{:S(2)}) collective-permute-start(bf16[3,64,512]{2,1,0:T(8,128)(2,1)S(1)} %get-tuple-element.43), channel_id=1, source_target_pairs={{1,0},{2,1},{3,2},{4,3},{5,4},{6,5},{7,6},{0,7},{9,8},{10,9},{11,1... | collective-permute-start | bytes 589832 | tf_op jit(solution)/shard_map/f3_lon/ppermute | solution.py:265
  108.6 4.9 %collective-permute-start.21 = (bf16[3,64,512]{2,1,0:T(8,128)(2,1)S(1)}, bf16[3,64,512]{2,1,0:T(8,128)(2,1)S(1)}, u32[]{:S(2)}, u32[]{:S(2)}) collective-permute-start(bf16[3,64,512]{2,1,0:T(8,128)(2,1)S(1)} %get-tuple-element.44), channel_id=1, source_target_pairs={{0,1},{1,2},{2,3},{3,4},{4,5},{5,6},{6,7},{7,0},{8,9},{9,10},{10,1... | collective-permute-start | bytes 589832 | tf_op jit(solution)/shard_map/f3_lon/ppermute | solution.py:265
  109.1 7.8 %copy-start.15 = (bf16[512,512]{1,0:T(8,128)(2,1)S(1)}, bf16[512,512]{1,0:T(8,128)(2,1)}, u32[]{:S(2)}) copy-start(bf16[512,512]{1,0:T(8,128)(2,1)} %enc_weight.1) | copy-start | bytes 1572868
  109.1 7.8 %copy-start.19 = (s32[1,9,256]{2,0,1:T(1,128)S(1)}, s32[1,9,256]{2,0,1:T(1,128)}, u32[]{:S(2)}) copy-start(s32[1,9,256]{2,0,1:T(1,128)} %param.19) | copy-start | bytes 27652
  113.5 8.4 %collective-permute-start.22 = (bf16[64,512]{1,0:T(8,128)(2,1)S(1)}, bf16[64,512]{1,0:T(8,128)(2,1)S(1)}, u32[]{:S(2)}, u32[]{:S(2)}) collective-permute-start(bf16[64,512]{1,0:T(8,128)(2,1)S(1)} %get-tuple-element.46), channel_id=1, source_target_pairs={{0,8},{16,24},{32,40},{48,56},{64,72},{80,88},{96,104},{112,120},{... | collective-permute-start | bytes 196616 | tf_op jit(solution)/shard_map/f3_lat/ppermute | solution.py:265
  113.6 8.3 %collective-permute-start.23 = (bf16[64,512]{1,0:T(8,128)(2,1)S(1)}, bf16[64,512]{1,0:T(8,128)(2,1)S(1)}, u32[]{:S(2)}, u32[]{:S(2)}) collective-permute-start(bf16[64,512]{1,0:T(8,128)(2,1)S(1)} %get-tuple-element.47), channel_id=1, source_target_pairs={{8,16},{24,32},{40,48},{56,64},{72,80},{88,96},{104,112},{120,0},{... | collective-permute-start | bytes 196616 | tf_op jit(solution)/shard_map/f3_lat/ppermute | solution.py:265

commit v2 on v1

v2 whole, which is shorter than its diff:
```python
import functools

import jax
import jax.numpy as jnp
from jax import lax
from jax.experimental import pallas as pl
from jax.experimental.pallas import tpu as pltpu
from jax.sharding import PartitionSpec as P


F32 = jnp.float32
BF16 = jnp.bfloat16
LANES = 128
CHUNK = 128
GROUP = 4

VMEM = pl.BlockSpec(memory_space=pltpu.VMEM)
SMEM = pl.BlockSpec(memory_space=pltpu.SMEM)


def mm(lhs, rhs):
    return jnp.dot(lhs, rhs, preferred_element_type=F32)


def mm_nt(lhs, rhs):
    return lax.dot_general(lhs, rhs, (((1,), (1,)), ((), ())), preferred_element_type=F32)


def as_hot(mask):
    return jnp.where(mask, 1.0, 0.0).astype(BF16)


def down_rows(index_row):
    return jnp.transpose(jnp.broadcast_to(index_row, (LANES, index_row.shape[1])))


def gather_hot(index_row, rows):
    spread = down_rows(index_row)
    lane = lax.broadcasted_iota(jnp.int32, spread.shape, 1)
    return jnp.concatenate(
        [as_hot(spread == lane + start) for start in range(0, rows, LANES)], axis=1
    )


def scatter_hot(index_row, rows, live):
    slots = index_row.shape[1]
    slot = lax.broadcasted_iota(jnp.int32, (1, slots), 1)
    index_row = jnp.where(slot < live, index_row, -1)
    return as_hot(lax.broadcasted_iota(jnp.int32, (rows, slots), 0) == index_row)


def gate(pre):
    return 0.5 * jnp.tanh(0.5 * pre) + 0.5


def list_chunks(counts, capacity, block, start, live):
    found = jnp.int32(0)
    for k in range(counts.shape[1]):
        count = counts[0, k]
        for at in range(0, capacity, CHUNK):
            block[found] = k
            start[found] = at
            live[found] = count - at
            found += (count > at).astype(jnp.int32)
    for j in range(GROUP - 1):
        block[found + j] = counts.shape[1] // 2
        start[found + j] = 0
        live[found + j] = 0
    return lax.div(found + (GROUP - 1), GROUP)


def each_group(groups, chunk_list, body):
    block, start, live = chunk_list

    @pl.loop(0, groups)
    def _(g):
        at = [GROUP * g + j for j in range(GROUP)]
        body([(block[n], pl.multiple_of(start[n], CHUNK), live[n]) for n in at])


def rows_of(index_ref, chunk):
    k, at, _ = chunk
    return index_ref[k, :, pl.ds(at, CHUNK)]


def place_of(k, flips):
    def place(offset, flip):
        return jnp.where(offset == 0, 0, jnp.where(offset == 1 - 2 * flip, 1, 2))

    return 3 * place(lax.rem(k, 3) - 1, flips[1]) + place(lax.div(k, 3) - 1, flips[0])


def gather_slots(counts, index_ref, table, out, chunk_list):
    groups = list_chunks(counts, index_ref.shape[2], *chunk_list)

    def body(chunks):
        hots = [gather_hot(rows_of(index_ref, c), table.shape[0]) for c in chunks]
        rows = mm(jnp.concatenate(hots, axis=0), table[...]).astype(BF16)
        for j, (k, at, _) in enumerate(chunks):
            out[k, pl.ds(at, CHUNK), :] = rows[j * CHUNK : (j + 1) * CHUNK]

    each_group(groups, chunk_list, body)


def enc_gather_kernel(counts, send, feat, weight, out, table, *chunk_list):
    table[...] = mm(feat[...], weight[...]).astype(BF16)
    gather_slots(counts, send, table, out, chunk_list)


def side_gather_kernel(cols, counts, recv, feat, weight, bias, out, table, *chunk_list):
    table[...] = (mm(feat[...], weight[:, cols]) + bias[:, cols]).astype(BF16)
    gather_slots(counts, recv, table, out, chunk_list)


def back_gather_kernel(cols, counts, recv, cot, weight, out, table, *chunk_list):
    table[...] = mm_nt(cot[...], weight[cols, :]).astype(BF16)
    gather_slots(counts, recv, table, out, chunk_list)


def near_hot(index_row, rows):
    spread = down_rows(index_row)
    lane = lax.broadcasted_iota(jnp.int32, spread.shape, 1)
    return as_hot(spread == jnp.where(lane < rows, lane, lane - rows))


def edge_groups(counts, index_ref, flips, side, total, outs, chunk_list, edges):
    rows = total.shape[1]
    groups = list_chunks(counts, index_ref.shape[2], *chunk_list)
    total[...] = jnp.zeros(total.shape, F32)

    def body(chunks):
        places = [place_of(k, flips) for k, _, _ in chunks]
        index_rows = [rows_of(index_ref, chunk) for chunk in chunks]

        def gather(j):
            return mm(near_hot(index_rows[j], rows)[:, : side.shape[1]], side[places[j]])

        received = gather(0)
        for j, chunk in enumerate(chunks):
            following = gather(j + 1) if j + 1 < len(chunks) else None
            value = edges(chunk, received)
            total[places[j]] += mm(scatter_hot(index_rows[j], rows, chunk[2]), value)
            received = following

    each_group(groups, chunk_list, body)
    for place, out in enumerate(outs):
        out[...] = total[3 * place : 3 * place + 3].astype(BF16)


def enc_forward_kernel(
    counts, flips, recv, own, first, second, weight, bias, sent,
    out_own, out_first, out_second, slope, side, total, *chunk_list,
):
    rows = own.shape[1]
    for place, near in enumerate((own, first, second)):
        feats = near[...].reshape(3 * rows, near.shape[2])
        exact = mm(feats, weight[...]) + bias[...]
        high = exact.astype(BF16)
        low = (exact - high.astype(F32)).astype(BF16)
        side[3 * place : 3 * place + 3, :rows, :] = high.reshape(3, rows, -1)
        side[3 * place : 3 * place + 3, rows:, :] = low.reshape(3, rows, -1)

    def edges(chunk, received):
        k, at, _ = chunk
        pre = sent[k, pl.ds(at, CHUNK), :].astype(F32) + received
        squashed = gate(pre)
        message = pre * squashed
        slope[k, pl.ds(at, CHUNK), :] = (squashed + message * (1.0 - squashed)).astype(BF16)
        return message.astype(BF16)

    outs = (out_own, out_first, out_second)
    edge_groups(counts, recv, flips, side, total, outs, chunk_list, edges)


def halves(lower, upper, at):
    return jnp.concatenate([lower[at], upper[at]], axis=1).astype(F32)


def dec_kernel(
    counts, flips, send, own, first, second, side_a, side_b, back_a, back_b,
    out_own, out_first, out_second, messages, grads, near, total, *chunk_list,
):
    for place, tiles in enumerate((own, first, second)):
        near[3 * place : 3 * place + 3] = tiles[...]

    def edges(chunk, received):
        k, at, _ = chunk
        here = (k, pl.ds(at, CHUNK), slice(None))
        pre = halves(side_a, side_b, here) + received
        squashed = gate(pre)
        message = pre * squashed
        messages[here] = message.astype(BF16)
        slope = squashed + message * (1.0 - squashed)
        grad = (halves(back_a, back_b, here) * slope).astype(BF16)
        grads[here] = grad
        return grad

    outs = (out_own, out_first, out_second)
    edge_groups(counts, send, flips, near, total, outs, chunk_list, edges)


def enc_backward_kernel(
    counts, flips, recv, own, first, second, slope,
    out_own, out_first, out_second, grads, near, total, *chunk_list,
):
    for place, tiles in enumerate((own, first, second)):
        near[3 * place : 3 * place + 3] = tiles[...]

    def edges(chunk, received):
        k, at, _ = chunk
        here = (k, pl.ds(at, CHUNK), slice(None))
        grad = (received * slope[here].astype(F32)).astype(BF16)
        grads[here] = grad
        return grad

    outs = (out_own, out_first, out_second)
    edge_groups(counts, recv, flips, near, total, outs, chunk_list, edges)


def scatter_slots(counts, index_ref, values, total, chunk_list, cols=slice(None)):
    groups = list_chunks(counts, index_ref.shape[2], *chunk_list)
    total[...] = jnp.zeros(total.shape, F32)

    def body(chunks):
        hots = [scatter_hot(rows_of(index_ref, c), total.shape[0], c[2]) for c in chunks]
        rows = [values[k, pl.ds(at, CHUNK), cols] for k, at, _ in chunks]
        total[...] += mm(jnp.concatenate(hots, axis=1), jnp.concatenate(rows, axis=0))

    each_group(groups, chunk_list, body)


def scatter_kernel(cols, counts, index_ref, values, out, total, *chunk_list):
    scatter_slots(counts, index_ref, values, total, chunk_list, cols)
    out[...] = total[...].astype(BF16)


def grid_new_kernel(
    cols, counts, recv, messages, feat, lower, weight, out, total, *chunk_list
):
    scatter_slots(counts, recv, messages, total, chunk_list, cols)
    half = lower.shape[1]
    update = mm(lower[...], weight[:half, :]) + mm(total[...].astype(BF16), weight[half:, :])
    out[...] = (feat[...].astype(F32) + update).astype(BF16)


def grid_grad_kernel(
    cols, counts, send, grads, cot, dec_lower, dec_upper, lower, dec_weight, enc_weight,
    out, total, *chunk_list,
):
    scatter_slots(counts, send, grads, total, chunk_list, cols)
    half = lower.shape[1]
    back = mm_nt(dec_lower[...], dec_weight[:, :half]) + mm_nt(dec_upper[...], dec_weight[:, half:])
    back += mm_nt(lower[...], enc_weight[:, :half])
    back += mm_nt(total[...].astype(BF16), enc_weight[:, half:])
    out[...] = (cot[...].astype(F32) + back).astype(BF16)


def fold_kernel(own, east, west, kept, to_first, to_second):
    total = own[...].astype(F32) + east[...].astype(F32) + west[...].astype(F32)
    kept[...] = total[0]
    to_first[...] = total[1].astype(BF16)
    to_second[...] = total[2].astype(BF16)


def mesh_new_kernel(kept, first, second, feat, out_weight, weight, proj):
    summed = kept[...] + first[...].astype(F32) + second[...].astype(F32)
    update = mm(summed.astype(BF16), out_weight[...])
    proj[...] = mm((feat[...].astype(F32) + update).astype(BF16), weight[...]).astype(BF16)


def mesh_back_kernel(kept, first, second, weight, out_weight, back, enc_back):
    summed = kept[...] + first[...].astype(F32) + second[...].astype(F32)
    exact = mm_nt(summed.astype(BF16), weight[...])
    back[...] = exact
    enc_back[...] = mm_nt(exact.astype(BF16), out_weight[...]).astype(BF16)


def mesh_grad_kernel(kept, first, second, back, weight, out):
    summed = kept[...] + first[...].astype(F32) + second[...].astype(F32)
    out[...] = (back[...] + mm_nt(summed.astype(BF16), weight[...])).astype(BF16)


def along(axis, pairs):
    return lambda value: lax.ppermute(value, axis, pairs)


def swaps(size, start):
    edges = [(i, (i + 1) % size) for i in range(start, size, 2)]
    return edges + [(j, i) for i, j in edges]


def on_device(
    grid_feat, mesh_feat, enc_send, enc_recv, enc_count, dec_send, dec_recv, dec_count,
    enc_src, enc_dst, enc_bias, enc_out, dec_src, dec_dst, dec_bias, dec_out, grid_cot,
):
    grid_rows, width = grid_feat.shape
    mesh_rows = mesh_feat.shape[0]
    cap_e = enc_send.shape[2]
    cap_d = dec_send.shape[2]
    lat_size = lax.axis_size("lat")
    lon_size = lax.axis_size("lon")
    flips = jnp.stack([lax.rem(lax.axis_index(a), 2) for a in ("lat", "lon")]).astype(jnp.int32)
    lat_first, lat_second = (along("lat", swaps(lat_size, i)) for i in range(2))
    lon_first, lon_second = (along("lon", swaps(lon_size, i)) for i in range(2))

    def spread(local_tile):
        pieces = [local_tile, lat_first(local_tile), lat_second(local_tile)]
        three = jnp.stack(pieces)
        return three, lon_first(three), lon_second(three)

    def fold(own, to_first, to_second):
        arrived = lon_first(to_first), lon_second(to_second)
        kept, to_first, to_second = kernel(
            fold_kernel, [exact_tile, tile, tile], [], own, *arrived, smem=0
        )
        return kept, lat_first(to_first), lat_second(to_second)

    def kernel(body, outs, scratch, *args, smem=1, mib=12, work=0):
        return pl.pallas_call(
            body,
            out_shape=outs,
            in_specs=[SMEM] * smem + [VMEM] * (len(args) - smem),
            out_specs=[VMEM] * len(outs),
            scratch_shapes=scratch,
            compiler_params=pltpu.CompilerParams(vmem_limit_bytes=mib * 1024 * 1024),
            cost_estimate=pl.CostEstimate(flops=work, bytes_accessed=0, transcendentals=0),
        )(*args)

    def array(*shape):
        return jax.ShapeDtypeStruct(shape, BF16)

    tile = array(mesh_rows, width)
    exact_tile = jax.ShapeDtypeStruct((mesh_rows, width), F32)
    three = [array(3, mesh_rows, width)] * 3
    enc_slots = [array(9, cap_e, width)]
    dec_slots = [array(9, cap_d, width)]
    grid_tile = [array(grid_rows, width)]
    chunk_list = [pltpu.SMEM((9 * cap_d // CHUNK + GROUP,), jnp.int32)] * 3
    lower, upper = slice(0, width // 2), slice(width // 2, width)
    half_grid = [array(grid_rows, width // 2)]
    half_slots = [array(9, cap_d, width // 2)]
    rounded_half = [pltpu.VMEM((grid_rows, width // 2), BF16)] + chunk_list
    exact_half = [pltpu.VMEM((grid_rows, width // 2), F32)] + chunk_list
    rounded_grid = [pltpu.VMEM((grid_rows, width), BF16)] + chunk_list
    near = pltpu.VMEM((9, mesh_rows, width), BF16)
    near_split = pltpu.VMEM((9, 2 * mesh_rows, width), BF16)
    near_total = pltpu.VMEM((9, mesh_rows, width), F32)
    enc_work = 2 * grid_rows * width * 9 * cap_e
    dec_work = 2 * grid_rows * width * 9 * cap_d

    enc_send, enc_recv, dec_send, dec_recv = (
        jnp.swapaxes(a, 0, 1) for a in (enc_send, enc_recv, dec_send, dec_recv)
    )

    near_feat = spread(mesh_feat)
    (sent,) = kernel(
        enc_gather_kernel, enc_slots, rounded_grid,
        enc_count, enc_send, grid_feat, enc_src, work=enc_work,
    )
    back_at = [
        kernel(
            functools.partial(back_gather_kernel, cols), half_slots, rounded_half,
            dec_count, dec_recv, grid_cot, dec_out, work=dec_work // 2,
        )[0]
        for cols in (lower, upper)
    ]
    side_at = [
        kernel(
            functools.partial(side_gather_kernel, cols), half_slots, rounded_half,
            dec_count, dec_recv, grid_feat, dec_dst, dec_bias.reshape(1, width),
            work=dec_work // 2,
        )[0]
        for cols in (lower, upper)
    ]

    *enc_partial, slope = kernel(
        enc_forward_kernel, three + enc_slots,
        [near_split, near_total] + chunk_list,
        enc_count, flips, enc_recv, *near_feat, enc_dst, enc_bias.reshape(1, width), sent,
        smem=2, work=enc_work // 4,
    )
    (dec_proj,) = kernel(
        mesh_new_kernel, [tile], [],
        *fold(*enc_partial), mesh_feat, enc_out, dec_src, smem=0,
    )

    *dec_partial, messages, dec_grads = kernel(
        dec_kernel, three + dec_slots * 2, [near, near_total] + chunk_list,
        dec_count, flips, dec_send, *spread(dec_proj), *side_at, *back_at,
        smem=2, work=dec_work // 4,
    )
    mesh_back, enc_back = kernel(
        mesh_back_kernel, [exact_tile, tile], [],
        *fold(*dec_partial), dec_src, enc_out, smem=0,
    )

    (sum_lower,) = kernel(
        functools.partial(scatter_kernel, lower), half_grid, exact_half,
        dec_count, dec_recv, messages, work=dec_work // 2,
    )
    (grid_new,) = kernel(
        functools.partial(grid_new_kernel, upper), grid_tile, exact_half,
        dec_count, dec_recv, messages, grid_feat, sum_lower, dec_out, work=dec_work // 2,
    )
    dec_local = [
        kernel(
            functools.partial(scatter_kernel, cols), half_grid, exact_half,
            dec_count, dec_recv, dec_grads, work=dec_work // 2,
        )[0]
        for cols in (lower, upper)
    ]

    *grad_partial, grads = kernel(
        enc_backward_kernel, three + enc_slots, [near, near_total] + chunk_list,
        enc_count, flips, enc_recv, *spread(enc_back), slope,
        smem=2, work=enc_work // 4,
    )
    (mesh_grad,) = kernel(
        mesh_grad_kernel, [tile], [],
        *fold(*grad_partial), mesh_back, enc_dst, smem=0,
    )

    (total_lower,) = kernel(
        functools.partial(scatter_kernel, lower), half_grid, exact_half,
        enc_count, enc_send, grads, work=enc_work // 2,
    )
    (grid_grad,) = kernel(
        functools.partial(grid_grad_kernel, upper), grid_tile, exact_half,
        enc_count, enc_send, grads, grid_cot, *dec_local, total_lower, dec_dst, enc_src,
        work=enc_work // 2,
    )
    return grid_new, mesh_grad, grid_grad


def solution(mesh):
    rows = P(("lat", "lon"), None)
    edges = P(("lat", "lon"), None, None)
    return jax.shard_map(
        on_device,
        mesh=mesh,
        in_specs=(rows, rows, edges, edges, rows, edges, edges, rows)
        + (P(),) * 8
        + (rows,),
        out_specs=(rows, rows, rows),
        check_vma=False,
    )
```

time: 125 us -> 114 us (0.912)
  waiting for transfers between devices: 23.1 us -> 8.12 us
  Pallas kernels: 46.1 us -> 56.3 us
  starting transfers between devices: 48 us -> 42.9 us
    ppermute x24, waiting for transfers between devices: 23.1 us -> 8.12 us  [along(): return lambda value: lax.ppermute(value, axis, pairs)]
    pallas_call x15 -> x20, Pallas kernels: 46.1 us -> 56.3 us  [kernel(): pl.pallas_call(body, out_shape=outs, in_specs=[SMEM] * smem + [VMEM] * (l...]
    ppermute x24, starting transfers between devices: 48 us -> 42.9 us  [along(): return lambda value: lax.ppermute(value, axis, pairs)]
  transfers between devices with their start and end apart: 24 -> 24, of which waited for: 8 -> 7; matrix products, arithmetic and copies ran while one was open for 0% -> 0% of each run, Pallas kernels for 24% -> 37%
where the time goes in v2:
time: 114 us; the launch traced here: 113 us
  Pallas kernels  56.3 us (49%)
  starting transfers between devices  42.9 us (38%)
  waiting for transfers between devices  8.12 us (7%)
  local copies, waits for them, and re-layouts  3.71 us (3%)
    pallas_call x20, Pallas kernels, kernel(): pl.pallas_call(body, out_shape=outs, in_specs=[SMEM] * smem + [VMEM] * (l...  56.3 us
    ppermute x24, starting transfers between devices, along(): return lambda value: lax.ppermute(value, axis, pairs)  42.9 us
    ppermute x24, waiting for transfers between devices, along(): return lambda value: lax.ppermute(value, axis, pairs)  8.12 us
    unnamed x42, local copies, waits for them, and re-layouts  3.71 us
  transfers between devices with their start and end apart: 24, of which 7 were waited for; matrix products, arithmetic and copies ran while one was open for 0% of the time, Pallas kernels for 37%

profile of v2, /device:TPU:1, one launch (start us, length us, event | category | flops | bytes accessed | tf_op | source)
XLA Modules:
  0.0 113.0 jit_solution(15513699686109489858)
XLA Ops:
  0.6 2.2 %collective-permute-start = (bf16[64,512]{1,0:T(8,128)(2,1)}, bf16[64,512]{1,0:T(8,128)(2,1)S(1)}, u32[]{:S(2)}, u32[]{:S(2)}) collective-permute-start(bf16[64,512]{1,0:T(8,128)(2,1)} %feat.6), channel_id=1, source_target_pairs={{0,8},{16,24},{32,40},{48,56},{64,72},{80,88},{96,104},{112,120},{... | collective-permute-start | bytes 196616 | tf_op jit(solution)/shard_map/ppermute | solution.py:284
  2.8 5.4 %collective-permute-start.1 = (bf16[64,512]{1,0:T(8,128)(2,1)}, bf16[64,512]{1,0:T(8,128)(2,1)S(1)}, u32[]{:S(2)}, u32[]{:S(2)}) collective-permute-start(bf16[64,512]{1,0:T(8,128)(2,1)} %feat.6), channel_id=1, source_target_pairs={{8,16},{24,32},{40,48},{56,64},{72,80},{88,96},{104,112},{120,0},{... | collective-permute-start | bytes 196616 | tf_op jit(solution)/shard_map/ppermute | solution.py:284
  8.2 0.1 pad_add_fusion.flips
  8.3 1.8 %collective-permute-done.1 = bf16[64,512]{1,0:T(8,128)(2,1)S(1)} collective-permute-done((bf16[64,512]{1,0:T(8,128)(2,1)}, bf16[64,512]{1,0:T(8,128)(2,1)S(1)}, u32[]{:S(2)}, u32[]{:S(2)}) %collective-permute-start.1) | collective-permute-done | bytes 65568 | tf_op jit(solution)/shard_map/ppermute | solution.py:284
  10.1 0.9 pad_maximum_fusion.own
  11.0 3.0 %collective-permute-start.3 = (bf16[3,64,512]{2,1,0:T(8,128)(2,1)S(1)}, bf16[3,64,512]{2,1,0:T(8,128)(2,1)S(1)}, u32[]{:S(2)}, u32[]{:S(2)}) collective-permute-start(bf16[3,64,512]{2,1,0:T(8,128)(2,1)S(1)} %pad_maximum_fusion.own), channel_id=1, source_target_pairs={{1,2},{3,4},{5,6},{7,0},{2,1},{4,3},{6,5},{0,7},{9,10},{11,12},{13... | collective-permute-start | bytes 589832 | tf_op jit(solution)/shard_map/ppermute | solution.py:284
  14.0 1.0 copy-done.4
  15.0 0.7 copy-done.10
  15.7 0.7 copy-done.12
  16.4 1.2 %copy-done.16 = bf16[1024,512]{1,0:T(8,128)(2,1)S(1)} copy-done((bf16[1024,512]{1,0:T(8,128)(2,1)S(1)}, bf16[1024,512]{1,0:T(8,128)(2,1)}, u32[]{:S(2)}) %copy-start.16) | copy-done | bytes 1048600
  17.6 3.5 %shard_map.184.sent = bf16[9,256,512]{2,1,0:T(8,128)(2,1)S(1)} custom-call(s32[1,9]{1,0:T(1,128)S(1)} %copy-done.12, s32[9,1,256]{2,1,0:T(1,128)S(1)} %bitcast.23, bf16[1024,512]{1,0:T(8,128)(2,1)S(1)} %copy-done.16, bf16[512,512]{1,0:T(8,128)(2,1)S(1)} %copy-done.4), custom_call_target="tpu_custom_call" | custom-call | flops 2415919104 | tf_op jit(solution)/shard_map/pallas_call | solution.py:319
  21.1 0.0 copy-start.3
  21.2 0.0 copy-start.15
  21.2 0.0 copy-start.18
  21.2 0.0 copy-start.19
  21.2 0.0 collective-permute-done.3.second
  21.2 3.8 %shard_map.185 = (bf16[3,64,512]{2,1,0:T(8,128)(2,1)S(1)}, bf16[3,64,512]{2,1,0:T(8,128)(2,1)S(1)}, bf16[3,64,512]{2,1,0:T(8,128)(2,1)S(1)}, bf16[9,256,512]{2,1,0:T(8,128)(2,1)S(1)}) custom-call(s32[1,9]{1,0:T(1,128)S(1)} %copy-done.12, s32[2]{0:T(128)S(1)} %pad_add_fusion.flips, s32[9,1,256]{2,1,0:T(1,128)S(1)} %bitcast.20, ...), custom_call_target="tpu_custom_call" | custom-call | flops 603979776 | tf_op jit(solution)/shard_map/pallas_call | solution.py:319
  25.0 0.6 collective-permute-start.4
  25.6 1.2 %collective-permute-start.5 = (bf16[3,64,512]{2,1,0:T(8,128)(2,1)S(1)}, bf16[3,64,512]{2,1,0:T(8,128)(2,1)S(1)}, u32[]{:S(2)}, u32[]{:S(2)}) collective-permute-start(bf16[3,64,512]{2,1,0:T(8,128)(2,1)S(1)} %get-tuple-element.29), channel_id=1, source_target_pairs={{1,2},{3,4},{5,6},{7,0},{2,1},{4,3},{6,5},{0,7},{9,10},{11,12},{13... | collective-permute-start | bytes 589832 | tf_op jit(solution)/shard_map/ppermute | solution.py:284
  26.8 4.1 %shard_map.191.back_b = bf16[9,512,256]{2,1,0:T(8,128)(2,1)S(1)} custom-call(s32[1,9]{1,0:T(1,128)S(1)} %copy-done.15, s32[9,1,512]{2,1,0:T(1,128)S(1)} %bitcast.27, bf16[1024,512]{1,0:T(8,128)(2,1)S(1)} %copy-done.3, bf16[512,512]{1,0:T(8,128)(2,1)S(1)} %copy-done.18), custom_call_target="tpu_custom_call" | custom-call | flops 2415919104 | tf_op jit(solution)/shard_map/pallas_call | solution.py:319
  30.9 0.1 collective-permute-done.5.west
  31.0 0.1 shard_map.186
  31.1 0.1 collective-permute-start.6
  31.2 0.0 copy-start
  31.2 0.0 copy-start.1
  31.2 0.0 copy-start.7
  31.2 0.0 copy-start.6
  31.2 0.0 copy-start.17
  31.2 0.0 copy-start.20
  31.2 5.1 %collective-permute-start.7 = (bf16[64,512]{1,0:T(8,128)(2,1)S(1)}, bf16[64,512]{1,0:T(8,128)(2,1)S(1)}, u32[]{:S(2)}, u32[]{:S(2)}) collective-permute-start(bf16[64,512]{1,0:T(8,128)(2,1)S(1)} %get-tuple-element.32), channel_id=1, source_target_pairs={{8,16},{24,32},{40,48},{56,64},{72,80},{88,96},{104,112},{120,0},{... | collective-permute-start | bytes 196616 | tf_op jit(solution)/shard_map/ppermute | solution.py:284
  36.3 4.1 %shard_map.190.back_a = bf16[9,512,256]{2,1,0:T(8,128)(2,1)S(1)} custom-call(s32[1,9]{1,0:T(1,128)S(1)} %copy-done.15, s32[9,1,512]{2,1,0:T(1,128)S(1)} %bitcast.28, bf16[1024,512]{1,0:T(8,128)(2,1)S(1)} %copy-done.3, bf16[512,512]{1,0:T(8,128)(2,1)S(1)} %copy-done.18), custom_call_target="tpu_custom_call" | custom-call | flops 2415919104 | tf_op jit(solution)/shard_map/pallas_call | solution.py:319
  40.5 0.4 shard_map.187
  40.9 2.4 %collective-permute-start.9 = (bf16[64,512]{1,0:T(8,128)(2,1)S(1)}, bf16[64,512]{1,0:T(8,128)(2,1)S(1)}, u32[]{:S(2)}, u32[]{:S(2)}) collective-permute-start(bf16[64,512]{1,0:T(8,128)(2,1)S(1)} %shard_map.187), channel_id=1, source_target_pairs={{8,16},{24,32},{40,48},{56,64},{72,80},{88,96},{104,112},{120,0},{... | collective-permute-start | bytes 196616 | tf_op jit(solution)/shard_map/ppermute | solution.py:284
  43.3 4.0 %shard_map.189.side_b = bf16[9,512,256]{2,1,0:T(8,128)(2,1)S(1)} custom-call(s32[1,9]{1,0:T(1,128)S(1)} %copy-done.15, s32[9,1,512]{2,1,0:T(1,128)S(1)} %bitcast.29, bf16[1024,512]{1,0:T(8,128)(2,1)S(1)} %copy-done.17, bf16[512,512]{1,0:T(8,128)(2,1)S(1)} %copy-done.6, f32[1,512]{1,0:T(1,128)S(1)} %bitcast.35), custom_call_target="tpu_custom_call" | custom-call | flops 2415919104 | tf_op jit(solution)/shard_map/pallas_call | solution.py:319
  47.3 0.1 collective-permute-done.9
  47.4 0.0 copy-start.9
  47.4 2.7 %collective-permute-start.11 = (bf16[3,64,512]{2,1,0:T(8,128)(2,1)S(1)}, bf16[3,64,512]{2,1,0:T(8,128)(2,1)S(1)}, u32[]{:S(2)}, u32[]{:S(2)}) collective-permute-start(bf16[3,64,512]{2,1,0:T(8,128)(2,1)S(1)} %pad_maximum_fusion.1.own), channel_id=1, source_target_pairs={{1,2},{3,4},{5,6},{7,0},{2,1},{4,3},{6,5},{0,7},{9,10},{11,12},{13... | collective-permute-start | bytes 589832 | tf_op jit(solution)/shard_map/ppermute | solution.py:284
  50.1 0.3 collective-permute-start.10
  50.4 4.0 %shard_map.188.side_a = bf16[9,512,256]{2,1,0:T(8,128)(2,1)S(1)} custom-call(s32[1,9]{1,0:T(1,128)S(1)} %copy-done.15, s32[9,1,512]{2,1,0:T(1,128)S(1)} %bitcast.30, bf16[1024,512]{1,0:T(8,128)(2,1)S(1)} %copy-done.17, bf16[512,512]{1,0:T(8,128)(2,1)S(1)} %copy-done.6, f32[1,512]{1,0:T(1,128)S(1)} %bitcast.36), custom_call_target="tpu_custom_call" | custom-call | flops 2415919104 | tf_op jit(solution)/shard_map/pallas_call | solution.py:319
  54.5 6.5 %shard_map.192 = (bf16[3,64,512]{2,1,0:T(8,128)(2,1)S(1)}, bf16[3,64,512]{2,1,0:T(8,128)(2,1)S(1)}, bf16[3,64,512]{2,1,0:T(8,128)(2,1)S(1)}, bf16[9,512,512]{2,1,0:T(8,128)(2,1)S(1)}, bf16[9,512,512]{2,1,0:T(8,128)(2,1)S(1)}) custom-call(s32[1,9]{1,0:T(1,128)S(1)} %copy-done.15, s32[2]{0:T(128)S(1)} %pad_add_fusion.flips, s32[9,1,512]{2,1,0:T(1,128)S(1)} %bitcast.22, ...), custom_call_target="tpu_custom_call" | custom-call | flops 1207959552 | tf_op jit(solution)/shard_map/pallas_call | solution.py:319
  61.1 1.0 collective-permute-start.12
  62.0 1.1 collective-permute-done.12.east
  63.1 4.3 %collective-permute-done.13.west = bf16[3,64,512]{2,1,0:T(8,128)(2,1)S(1)} collective-permute-done((bf16[3,64,512]{2,1,0:T(8,128)(2,1)S(1)}, bf16[3,64,512]{2,1,0:T(8,128)(2,1)S(1)}, u32[]{:S(2)}, u32[]{:S(2)}) %collective-permute-start.13) | collective-permute-done | bytes 196640 | tf_op jit(solution)/shard_map/ppermute | solution.py:284
  67.4 0.1 shard_map.195
  67.5 2.6 %collective-permute-start.14 = (bf16[64,512]{1,0:T(8,128)(2,1)S(1)}, bf16[64,512]{1,0:T(8,128)(2,1)S(1)}, u32[]{:S(2)}, u32[]{:S(2)}) collective-permute-start(bf16[64,512]{1,0:T(8,128)(2,1)S(1)} %get-tuple-element.38), channel_id=1, source_target_pairs={{0,8},{16,24},{32,40},{48,56},{64,72},{80,88},{96,104},{112,120},{... | collective-permute-start | bytes 196616 | tf_op jit(solution)/shard_map/ppermute | solution.py:284
  70.1 2.6 %collective-permute-start.15 = (bf16[64,512]{1,0:T(8,128)(2,1)S(1)}, bf16[64,512]{1,0:T(8,128)(2,1)S(1)}, u32[]{:S(2)}, u32[]{:S(2)}) collective-permute-start(bf16[64,512]{1,0:T(8,128)(2,1)S(1)} %get-tuple-element.39), channel_id=1, source_target_pairs={{8,16},{24,32},{40,48},{56,64},{72,80},{88,96},{104,112},{120,0},{... | collective-permute-start | bytes 196616 | tf_op jit(solution)/shard_map/ppermute | solution.py:284
  72.7 3.6 %shard_map.201.dec_upper = bf16[1024,256]{1,0:T(8,128)(2,1)S(1)} custom-call(s32[1,9]{1,0:T(1,128)S(1)} %copy-done.15, s32[9,1,512]{2,1,0:T(1,128)S(1)} %bitcast.31, bf16[9,512,512]{2,1,0:T(8,128)(2,1)S(1)} %get-tuple-element.50.values), custom_call_target="tpu_custom_call" | custom-call | flops 2415919104 | tf_op jit(solution)/shard_map/pallas_call | solution.py:319
  76.3 0.3 collective-permute-done.15.second
  76.6 0.5 shard_map.196
  77.0 2.6 %collective-permute-start.17 = (bf16[64,512]{1,0:T(8,128)(2,1)S(1)}, bf16[64,512]{1,0:T(8,128)(2,1)S(1)}, u32[]{:S(2)}, u32[]{:S(2)}) collective-permute-start(bf16[64,512]{1,0:T(8,128)(2,1)S(1)} %get-tuple-element.40), channel_id=1, source_target_pairs={{8,16},{24,32},{40,48},{56,64},{72,80},{88,96},{104,112},{120,0},{... | collective-permute-start | bytes 196616 | tf_op jit(solution)/shard_map/ppermute | solution.py:284
  79.7 3.4 %shard_map.200.dec_lower = bf16[1024,256]{1,0:T(8,128)(2,1)S(1)} custom-call(s32[1,9]{1,0:T(1,128)S(1)} %copy-done.15, s32[9,1,512]{2,1,0:T(1,128)S(1)} %bitcast.32, bf16[9,512,512]{2,1,0:T(8,128)(2,1)S(1)} %get-tuple-element.50.values), custom_call_target="tpu_custom_call" | custom-call | flops 2415919104 | tf_op jit(solution)/shard_map/pallas_call | solution.py:319
  83.1 0.4 collective-permute-done.17
  83.6 3.6 %collective-permute-start.19 = (bf16[3,64,512]{2,1,0:T(8,128)(2,1)S(1)}, bf16[3,64,512]{2,1,0:T(8,128)(2,1)S(1)}, u32[]{:S(2)}, u32[]{:S(2)}) collective-permute-start(bf16[3,64,512]{2,1,0:T(8,128)(2,1)S(1)} %pad_maximum_fusion.2.own), channel_id=1, source_target_pairs={{1,2},{3,4},{5,6},{7,0},{2,1},{4,3},{6,5},{0,7},{9,10},{11,12},{13... | collective-permute-start | bytes 589832 | tf_op jit(solution)/shard_map/ppermute | solution.py:284
  87.1 0.4 collective-permute-start.18
  87.5 3.4 %shard_map.193.lower = bf16[1024,256]{1,0:T(8,128)(2,1)S(1)} custom-call(s32[1,9]{1,0:T(1,128)S(1)} %copy-done.15, s32[9,1,512]{2,1,0:T(1,128)S(1)} %bitcast.33, bf16[9,512,512]{2,1,0:T(8,128)(2,1)S(1)} %get-tuple-element.33.values.messages), custom_call_target="tpu_custom_call" | custom-call | flops 2415919104 | tf_op jit(solution)/shard_map/pallas_call | solution.py:319
  91.0 2.6 %shard_map.197 = (bf16[3,64,512]{2,1,0:T(8,128)(2,1)S(1)}, bf16[3,64,512]{2,1,0:T(8,128)(2,1)S(1)}, bf16[3,64,512]{2,1,0:T(8,128)(2,1)S(1)}, bf16[9,256,512]{2,1,0:T(8,128)(2,1)S(1)}) custom-call(s32[1,9]{1,0:T(1,128)S(1)} %copy-done.13, s32[2]{0:T(128)S(1)} %pad_add_fusion.flips, s32[9,1,256]{2,1,0:T(1,128)S(1)} %bitcast.21, ...), custom_call_target="tpu_custom_call" | custom-call | flops 603979776 | tf_op jit(solution)/shard_map/pallas_call | solution.py:319
  93.6 2.9 %collective-permute-start.20 = (bf16[3,64,512]{2,1,0:T(8,128)(2,1)S(1)}, bf16[3,64,512]{2,1,0:T(8,128)(2,1)S(1)}, u32[]{:S(2)}, u32[]{:S(2)}) collective-permute-start(bf16[3,64,512]{2,1,0:T(8,128)(2,1)S(1)} %get-tuple-element.43), channel_id=1, source_target_pairs={{0,1},{2,3},{4,5},{6,7},{1,0},{3,2},{5,4},{7,6},{8,9},{10,11},{12,... | collective-permute-start | bytes 589832 | tf_op jit(solution)/shard_map/ppermute | solution.py:284
  96.5 5.0 %shard_map.194 = bf16[1024,512]{1,0:T(8,128)(2,1)} custom-call(s32[1,9]{1,0:T(1,128)S(1)} %copy-done.15, s32[9,1,512]{2,1,0:T(1,128)S(1)} %bitcast.34, bf16[9,512,512]{2,1,0:T(8,128)(2,1)S(1)} %get-tuple-element.33.values.messages, bf16[1024,512]{1,0:T(8,128)(2,1)S(1)} %copy-done.17, bf16[1024,256]{1,0:T(8,128)(2,1)S(1)} %shard_map.193.lower, ...), custom_call_target="tpu_custom_call" | custom-call | flops 2415919104 | tf_op jit(solution)/shard_map/pallas_call | solution.py:319
  101.5 2.0 %shard_map.202.lower = bf16[1024,256]{1,0:T(8,128)(2,1)S(1)} custom-call(s32[1,9]{1,0:T(1,128)S(1)} %copy-done.13, s32[9,1,256]{2,1,0:T(1,128)S(1)} %bitcast.24, bf16[9,256,512]{2,1,0:T(8,128)(2,1)S(1)} %get-tuple-element.49.values.grads), custom_call_target="tpu_custom_call" | custom-call | flops 1207959552 | tf_op jit(solution)/shard_map/pallas_call | solution.py:319
  103.6 0.1 shard_map.198
  103.6 1.4 %collective-permute-start.22 = (bf16[64,512]{1,0:T(8,128)(2,1)S(1)}, bf16[64,512]{1,0:T(8,128)(2,1)S(1)}, u32[]{:S(2)}, u32[]{:S(2)}) collective-permute-start(bf16[64,512]{1,0:T(8,128)(2,1)S(1)} %get-tuple-element.46), channel_id=1, source_target_pairs={{0,8},{16,24},{32,40},{48,56},{64,72},{80,88},{96,104},{112,120},{... | collective-permute-start | bytes 196616 | tf_op jit(solution)/shard_map/ppermute | solution.py:284
  105.0 2.9 %collective-permute-start.23 = (bf16[64,512]{1,0:T(8,128)(2,1)S(1)}, bf16[64,512]{1,0:T(8,128)(2,1)S(1)}, u32[]{:S(2)}, u32[]{:S(2)}) collective-permute-start(bf16[64,512]{1,0:T(8,128)(2,1)S(1)} %get-tuple-element.47), channel_id=1, source_target_pairs={{8,16},{24,32},{40,48},{56,64},{72,80},{88,96},{104,112},{120,0},{... | collective-permute-start | bytes 196616 | tf_op jit(solution)/shard_map/ppermute | solution.py:284
  107.9 4.2 %shard_map.203 = bf16[1024,512]{1,0:T(8,128)(2,1)} custom-call(s32[1,9]{1,0:T(1,128)S(1)} %copy-done.13, s32[9,1,256]{2,1,0:T(1,128)S(1)} %bitcast.25, bf16[9,256,512]{2,1,0:T(8,128)(2,1)S(1)} %get-tuple-element.49.values.grads, bf16[1024,512]{1,0:T(8,128)(2,1)S(1)} %copy-done.3, bf16[1024,256]{1,0:T(8,128)(2,1)S(1)} %shard_map.200.dec_lower, ...), custom_call_target="tpu_custom_call" | custom-call | flops 1207959552 | tf_op jit(solution)/shard_map/pallas_call | solution.py:319
  112.1 0.9 shard_map.199
  (50 shorter events, 0.2 us)
Async XLA Ops:
  0.6 7.6 %collective-permute-start = (bf16[64,512]{1,0:T(8,128)(2,1)}, bf16[64,512]{1,0:T(8,128)(2,1)S(1)}, u32[]{:S(2)}, u32[]{:S(2)}) collective-permute-start(bf16[64,512]{1,0:T(8,128)(2,1)} %feat.6), channel_id=1, source_target_pairs={{0,8},{16,24},{32,40},{48,56},{64,72},{80,88},{96,104},{112,120},{... | collective-permute-start | bytes 196616 | tf_op jit(solution)/shard_map/ppermute | solution.py:284
  2.8 7.3 %collective-permute-start.1 = (bf16[64,512]{1,0:T(8,128)(2,1)}, bf16[64,512]{1,0:T(8,128)(2,1)S(1)}, u32[]{:S(2)}, u32[]{:S(2)}) collective-permute-start(bf16[64,512]{1,0:T(8,128)(2,1)} %feat.6), channel_id=1, source_target_pairs={{8,16},{24,32},{40,48},{56,64},{72,80},{88,96},{104,112},{120,0},{... | collective-permute-start | bytes 196616 | tf_op jit(solution)/shard_map/ppermute | solution.py:284
  11.0 10.2 %collective-permute-start.3 = (bf16[3,64,512]{2,1,0:T(8,128)(2,1)S(1)}, bf16[3,64,512]{2,1,0:T(8,128)(2,1)S(1)}, u32[]{:S(2)}, u32[]{:S(2)}) collective-permute-start(bf16[3,64,512]{2,1,0:T(8,128)(2,1)S(1)} %pad_maximum_fusion.own), channel_id=1, source_target_pairs={{1,2},{3,4},{5,6},{7,0},{2,1},{4,3},{6,5},{0,7},{9,10},{11,12},{13... | collective-permute-start | bytes 589832 | tf_op jit(solution)/shard_map/ppermute | solution.py:284
  14.0 7.2 %collective-permute-start.2 = (bf16[3,64,512]{2,1,0:T(8,128)(2,1)S(1)}, bf16[3,64,512]{2,1,0:T(8,128)(2,1)S(1)}, u32[]{:S(2)}, u32[]{:S(2)}) collective-permute-start(bf16[3,64,512]{2,1,0:T(8,128)(2,1)S(1)} %pad_maximum_fusion.own), channel_id=1, source_target_pairs={{0,1},{2,3},{4,5},{6,7},{1,0},{3,2},{5,4},{7,6},{8,9},{10,11},{12,... | collective-permute-start | bytes 589832 | tf_op jit(solution)/shard_map/ppermute | solution.py:284
  14.0 1.0 copy-start.4
  15.0 0.7 copy-start.10
  15.7 0.7 copy-start.12
  16.4 1.2 %copy-start.16 = (bf16[1024,512]{1,0:T(8,128)(2,1)S(1)}, bf16[1024,512]{1,0:T(8,128)(2,1)}, u32[]{:S(2)}) copy-start(bf16[1024,512]{1,0:T(8,128)(2,1)} %feat.9) | copy-start | bytes 3145732
  17.6 3.6 %copy-start.2 = (bf16[512,512]{1,0:T(8,128)(2,1)S(1)}, bf16[512,512]{1,0:T(8,128)(2,1)}, u32[]{:S(2)}) copy-start(bf16[512,512]{1,0:T(8,128)(2,1)} %weight.19) | copy-start | bytes 1572868
  17.6 3.6 %copy-start.8 = (s32[1,9,256]{2,0,1:T(1,128)S(1)}, s32[1,9,256]{2,0,1:T(1,128)}, u32[]{:S(2)}) copy-start(s32[1,9,256]{2,0,1:T(1,128)} %param.20) | copy-start | bytes 27652
  17.6 3.6 %copy-start.14 = (f32[512]{0:T(512)S(1)}, f32[512]{0:T(512)}, u32[]{:S(2)}) copy-start(f32[512]{0:T(512)} %param.27) | copy-start | bytes 6148
  21.1 5.6 %copy-start.3 = (bf16[1024,512]{1,0:T(8,128)(2,1)S(1)}, bf16[1024,512]{1,0:T(8,128)(2,1)}, u32[]{:S(2)}) copy-start(bf16[1024,512]{1,0:T(8,128)(2,1)} %cot.5) | copy-start | bytes 3145732
  21.2 5.6 %copy-start.15 = (s32[1,9]{1,0:T(1,128)S(1)}, s32[1,9]{1,0:T(1,128)}, u32[]{:S(2)}) copy-start(s32[1,9]{1,0:T(1,128)} %counts.25) | copy-start | bytes 112
  21.2 5.6 %copy-start.18 = (bf16[512,512]{1,0:T(8,128)(2,1)S(1)}, bf16[512,512]{1,0:T(8,128)(2,1)}, u32[]{:S(2)}) copy-start(bf16[512,512]{1,0:T(8,128)(2,1)} %weight.17) | copy-start | bytes 1572868
  21.2 5.6 %copy-start.19 = (s32[1,9,512]{2,0,1:T(1,128)S(1)}, s32[1,9,512]{2,0,1:T(1,128)}, u32[]{:S(2)}) copy-start(s32[1,9,512]{2,0,1:T(1,128)} %param.23) | copy-start | bytes 55300
  25.0 5.9 %collective-permute-start.4 = (bf16[3,64,512]{2,1,0:T(8,128)(2,1)S(1)}, bf16[3,64,512]{2,1,0:T(8,128)(2,1)S(1)}, u32[]{:S(2)}, u32[]{:S(2)}) collective-permute-start(bf16[3,64,512]{2,1,0:T(8,128)(2,1)S(1)} %get-tuple-element.28), channel_id=1, source_target_pairs={{0,1},{2,3},{4,5},{6,7},{1,0},{3,2},{5,4},{7,6},{8,9},{10,11},{12,... | collective-permute-start | bytes 589832 | tf_op jit(solution)/shard_map/ppermute | solution.py:284
  25.6 5.4 %collective-permute-start.5 = (bf16[3,64,512]{2,1,0:T(8,128)(2,1)S(1)}, bf16[3,64,512]{2,1,0:T(8,128)(2,1)S(1)}, u32[]{:S(2)}, u32[]{:S(2)}) collective-permute-start(bf16[3,64,512]{2,1,0:T(8,128)(2,1)S(1)} %get-tuple-element.29), channel_id=1, source_target_pairs={{1,2},{3,4},{5,6},{7,0},{2,1},{4,3},{6,5},{0,7},{9,10},{11,12},{13... | collective-permute-start | bytes 589832 | tf_op jit(solution)/shard_map/ppermute | solution.py:284
  31.1 9.4 %collective-permute-start.6 = (bf16[64,512]{1,0:T(8,128)(2,1)S(1)}, bf16[64,512]{1,0:T(8,128)(2,1)S(1)}, u32[]{:S(2)}, u32[]{:S(2)}) collective-permute-start(bf16[64,512]{1,0:T(8,128)(2,1)S(1)} %get-tuple-element.31), channel_id=1, source_target_pairs={{0,8},{16,24},{32,40},{48,56},{64,72},{80,88},{96,104},{112,120},{... | collective-permute-start | bytes 196616 | tf_op jit(solution)/shard_map/ppermute | solution.py:284
  31.2 9.3 %copy-start = (bf16[512,512]{1,0:T(8,128)(2,1)S(1)}, bf16[512,512]{1,0:T(8,128)(2,1)}, u32[]{:S(2)}) copy-start(bf16[512,512]{1,0:T(8,128)(2,1)} %out_weight.3) | copy-start | bytes 1572868
  31.2 9.3 %copy-start.1 = (bf16[512,512]{1,0:T(8,128)(2,1)S(1)}, bf16[512,512]{1,0:T(8,128)(2,1)}, u32[]{:S(2)}) copy-start(bf16[512,512]{1,0:T(8,128)(2,1)} %weight.18) | copy-start | bytes 1572868
  31.2 9.3 %copy-start.7 = (bf16[64,512]{1,0:T(8,128)(2,1)S(1)}, bf16[64,512]{1,0:T(8,128)(2,1)}, u32[]{:S(2)}) copy-start(bf16[64,512]{1,0:T(8,128)(2,1)} %feat.6) | copy-start | bytes 196612
  31.2 12.1 %copy-start.6 = (bf16[512,512]{1,0:T(8,128)(2,1)S(1)}, bf16[512,512]{1,0:T(8,128)(2,1)}, u32[]{:S(2)}) copy-start(bf16[512,512]{1,0:T(8,128)(2,1)} %dec_weight.1) | copy-start | bytes 1572868
  31.2 12.1 %copy-start.17 = (bf16[1024,512]{1,0:T(8,128)(2,1)S(1)}, bf16[1024,512]{1,0:T(8,128)(2,1)}, u32[]{:S(2)}) copy-start(bf16[1024,512]{1,0:T(8,128)(2,1)} %feat.9) | copy-start | bytes 3145732
  31.2 12.0 %copy-start.20 = (f32[512]{0:T(512)S(1)}, f32[512]{0:T(512)}, u32[]{:S(2)}) copy-start(f32[512]{0:T(512)} %param.31) | copy-start | bytes 6148
  31.2 9.2 %collective-permute-start.7 = (bf16[64,512]{1,0:T(8,128)(2,1)S(1)}, bf16[64,512]{1,0:T(8,128)(2,1)S(1)}, u32[]{:S(2)}, u32[]{:S(2)}) collective-permute-start(bf16[64,512]{1,0:T(8,128)(2,1)S(1)} %get-tuple-element.32), channel_id=1, source_target_pairs={{8,16},{24,32},{40,48},{56,64},{72,80},{88,96},{104,112},{120,0},{... | collective-permute-start | bytes 196616 | tf_op jit(solution)/shard_map/ppermute | solution.py:284
  40.9 6.5 %collective-permute-start.9 = (bf16[64,512]{1,0:T(8,128)(2,1)S(1)}, bf16[64,512]{1,0:T(8,128)(2,1)S(1)}, u32[]{:S(2)}, u32[]{:S(2)}) collective-permute-start(bf16[64,512]{1,0:T(8,128)(2,1)S(1)} %shard_map.187), channel_id=1, source_target_pairs={{8,16},{24,32},{40,48},{56,64},{72,80},{88,96},{104,112},{120,0},{... | collective-permute-start | bytes 196616 | tf_op jit(solution)/shard_map/ppermute | solution.py:284
  43.3 4.1 %collective-permute-start.8 = (bf16[64,512]{1,0:T(8,128)(2,1)S(1)}, bf16[64,512]{1,0:T(8,128)(2,1)S(1)}, u32[]{:S(2)}, u32[]{:S(2)}) collective-permute-start(bf16[64,512]{1,0:T(8,128)(2,1)S(1)} %shard_map.187), channel_id=1, source_target_pairs={{0,8},{16,24},{32,40},{48,56},{64,72},{80,88},{96,104},{112,120},{... | collective-permute-start | bytes 196616 | tf_op jit(solution)/shard_map/ppermute | solution.py:284
  47.4 7.1 %copy-start.9 = (s32[1,9,512]{2,0,1:T(1,128)S(1)}, s32[1,9,512]{2,0,1:T(1,128)}, u32[]{:S(2)}) copy-start(s32[1,9,512]{2,0,1:T(1,128)} %param.22) | copy-start | bytes 55300
  47.4 7.1 %collective-permute-start.11 = (bf16[3,64,512]{2,1,0:T(8,128)(2,1)S(1)}, bf16[3,64,512]{2,1,0:T(8,128)(2,1)S(1)}, u32[]{:S(2)}, u32[]{:S(2)}) collective-permute-start(bf16[3,64,512]{2,1,0:T(8,128)(2,1)S(1)} %pad_maximum_fusion.1.own), channel_id=1, source_target_pairs={{1,2},{3,4},{5,6},{7,0},{2,1},{4,3},{6,5},{0,7},{9,10},{11,12},{13... | collective-permute-start | bytes 589832 | tf_op jit(solution)/shard_map/ppermute | solution.py:284
  50.1 4.4 %collective-permute-start.10 = (bf16[3,64,512]{2,1,0:T(8,128)(2,1)S(1)}, bf16[3,64,512]{2,1,0:T(8,128)(2,1)S(1)}, u32[]{:S(2)}, u32[]{:S(2)}) collective-permute-start(bf16[3,64,512]{2,1,0:T(8,128)(2,1)S(1)} %pad_maximum_fusion.1.own), channel_id=1, source_target_pairs={{0,1},{2,3},{4,5},{6,7},{1,0},{3,2},{5,4},{7,6},{8,9},{10,11},{12,... | collective-permute-start | bytes 589832 | tf_op jit(solution)/shard_map/ppermute | solution.py:284
  61.1 2.1 %collective-permute-start.12 = (bf16[3,64,512]{2,1,0:T(8,128)(2,1)S(1)}, bf16[3,64,512]{2,1,0:T(8,128)(2,1)S(1)}, u32[]{:S(2)}, u32[]{:S(2)}) collective-permute-start(bf16[3,64,512]{2,1,0:T(8,128)(2,1)S(1)} %get-tuple-element.35), channel_id=1, source_target_pairs={{0,1},{2,3},{4,5},{6,7},{1,0},{3,2},{5,4},{7,6},{8,9},{10,11},{12,... | collective-permute-start | bytes 589832 | tf_op jit(solution)/shard_map/ppermute | solution.py:284
  62.0 5.4 %collective-permute-start.13 = (bf16[3,64,512]{2,1,0:T(8,128)(2,1)S(1)}, bf16[3,64,512]{2,1,0:T(8,128)(2,1)S(1)}, u32[]{:S(2)}, u32[]{:S(2)}) collective-permute-start(bf16[3,64,512]{2,1,0:T(8,128)(2,1)S(1)} %get-tuple-element.36), channel_id=1, source_target_pairs={{1,2},{3,4},{5,6},{7,0},{2,1},{4,3},{6,5},{0,7},{9,10},{11,12},{13... | collective-permute-start | bytes 589832 | tf_op jit(solution)/shard_map/ppermute | solution.py:284
  67.5 8.8 %collective-permute-start.14 = (bf16[64,512]{1,0:T(8,128)(2,1)S(1)}, bf16[64,512]{1,0:T(8,128)(2,1)S(1)}, u32[]{:S(2)}, u32[]{:S(2)}) collective-permute-start(bf16[64,512]{1,0:T(8,128)(2,1)S(1)} %get-tuple-element.38), channel_id=1, source_target_pairs={{0,8},{16,24},{32,40},{48,56},{64,72},{80,88},{96,104},{112,120},{... | collective-permute-start | bytes 196616 | tf_op jit(solution)/shard_map/ppermute | solution.py:284
  70.1 6.4 %collective-permute-start.15 = (bf16[64,512]{1,0:T(8,128)(2,1)S(1)}, bf16[64,512]{1,0:T(8,128)(2,1)S(1)}, u32[]{:S(2)}, u32[]{:S(2)}) collective-permute-start(bf16[64,512]{1,0:T(8,128)(2,1)S(1)} %get-tuple-element.39), channel_id=1, source_target_pairs={{8,16},{24,32},{40,48},{56,64},{72,80},{88,96},{104,112},{120,0},{... | collective-permute-start | bytes 196616 | tf_op jit(solution)/shard_map/ppermute | solution.py:284
  77.0 6.5 %collective-permute-start.17 = (bf16[64,512]{1,0:T(8,128)(2,1)S(1)}, bf16[64,512]{1,0:T(8,128)(2,1)S(1)}, u32[]{:S(2)}, u32[]{:S(2)}) collective-permute-start(bf16[64,512]{1,0:T(8,128)(2,1)S(1)} %get-tuple-element.40), channel_id=1, source_target_pairs={{8,16},{24,32},{40,48},{56,64},{72,80},{88,96},{104,112},{120,0},{... | collective-permute-start | bytes 196616 | tf_op jit(solution)/shard_map/ppermute | solution.py:284
  79.7 3.9 %collective-permute-start.16 = (bf16[64,512]{1,0:T(8,128)(2,1)S(1)}, bf16[64,512]{1,0:T(8,128)(2,1)S(1)}, u32[]{:S(2)}, u32[]{:S(2)}) collective-permute-start(bf16[64,512]{1,0:T(8,128)(2,1)S(1)} %get-tuple-element.40), channel_id=1, source_target_pairs={{0,8},{16,24},{32,40},{48,56},{64,72},{80,88},{96,104},{112,120},{... | collective-permute-start | bytes 196616 | tf_op jit(solution)/shard_map/ppermute | solution.py:284
  83.6 7.4 %collective-permute-start.19 = (bf16[3,64,512]{2,1,0:T(8,128)(2,1)S(1)}, bf16[3,64,512]{2,1,0:T(8,128)(2,1)S(1)}, u32[]{:S(2)}, u32[]{:S(2)}) collective-permute-start(bf16[3,64,512]{2,1,0:T(8,128)(2,1)S(1)} %pad_maximum_fusion.2.own), channel_id=1, source_target_pairs={{1,2},{3,4},{5,6},{7,0},{2,1},{4,3},{6,5},{0,7},{9,10},{11,12},{13... | collective-permute-start | bytes 589832 | tf_op jit(solution)/shard_map/ppermute | solution.py:284
  87.1 3.8 %collective-permute-start.18 = (bf16[3,64,512]{2,1,0:T(8,128)(2,1)S(1)}, bf16[3,64,512]{2,1,0:T(8,128)(2,1)S(1)}, u32[]{:S(2)}, u32[]{:S(2)}) collective-permute-start(bf16[3,64,512]{2,1,0:T(8,128)(2,1)S(1)} %pad_maximum_fusion.2.own), channel_id=1, source_target_pairs={{0,1},{2,3},{4,5},{6,7},{1,0},{3,2},{5,4},{7,6},{8,9},{10,11},{12,... | collective-permute-start | bytes 589832 | tf_op jit(solution)/shard_map/ppermute | solution.py:284
  87.5 3.4 %copy-start.13 = (s32[1,9]{1,0:T(1,128)S(1)}, s32[1,9]{1,0:T(1,128)}, u32[]{:S(2)}) copy-start(s32[1,9]{1,0:T(1,128)} %counts.27) | copy-start | bytes 112
  93.6 9.9 %collective-permute-start.20 = (bf16[3,64,512]{2,1,0:T(8,128)(2,1)S(1)}, bf16[3,64,512]{2,1,0:T(8,128)(2,1)S(1)}, u32[]{:S(2)}, u32[]{:S(2)}) collective-permute-start(bf16[3,64,512]{2,1,0:T(8,128)(2,1)S(1)} %get-tuple-element.43), channel_id=1, source_target_pairs={{0,1},{2,3},{4,5},{6,7},{1,0},{3,2},{5,4},{7,6},{8,9},{10,11},{12,... | collective-permute-start | bytes 589832 | tf_op jit(solution)/shard_map/ppermute | solution.py:284
  96.5 5.1 %copy-start.11 = (s32[1,9,256]{2,0,1:T(1,128)S(1)}, s32[1,9,256]{2,0,1:T(1,128)}, u32[]{:S(2)}) copy-start(s32[1,9,256]{2,0,1:T(1,128)} %param.19) | copy-start | bytes 27652
  96.5 7.1 %collective-permute-start.21 = (bf16[3,64,512]{2,1,0:T(8,128)(2,1)S(1)}, bf16[3,64,512]{2,1,0:T(8,128)(2,1)S(1)}, u32[]{:S(2)}, u32[]{:S(2)}) collective-permute-start(bf16[3,64,512]{2,1,0:T(8,128)(2,1)S(1)} %get-tuple-element.44), channel_id=1, source_target_pairs={{1,2},{3,4},{5,6},{7,0},{2,1},{4,3},{6,5},{0,7},{9,10},{11,12},{13... | collective-permute-start | bytes 589832 | tf_op jit(solution)/shard_map/ppermute | solution.py:284
  101.5 6.4 %copy-start.5 = (bf16[512,512]{1,0:T(8,128)(2,1)S(1)}, bf16[512,512]{1,0:T(8,128)(2,1)}, u32[]{:S(2)}) copy-start(bf16[512,512]{1,0:T(8,128)(2,1)} %enc_weight.1) | copy-start | bytes 1572868
  103.6 8.5 %collective-permute-start.22 = (bf16[64,512]{1,0:T(8,128)(2,1)S(1)}, bf16[64,512]{1,0:T(8,128)(2,1)S(1)}, u32[]{:S(2)}, u32[]{:S(2)}) collective-permute-start(bf16[64,512]{1,0:T(8,128)(2,1)S(1)} %get-tuple-element.46), channel_id=1, source_target_pairs={{0,8},{16,24},{32,40},{48,56},{64,72},{80,88},{96,104},{112,120},{... | collective-permute-start | bytes 196616 | tf_op jit(solution)/shard_map/ppermute | solution.py:284
  105.0 7.1 %collective-permute-start.23 = (bf16[64,512]{1,0:T(8,128)(2,1)S(1)}, bf16[64,512]{1,0:T(8,128)(2,1)S(1)}, u32[]{:S(2)}, u32[]{:S(2)}) collective-permute-start(bf16[64,512]{1,0:T(8,128)(2,1)S(1)} %get-tuple-element.47), channel_id=1, source_target_pairs={{8,16},{24,32},{40,48},{56,64},{72,80},{88,96},{104,112},{120,0},{... | collective-permute-start | bytes 196616 | tf_op jit(solution)/shard_map/ppermute | solution.py:284

commit v3 on v2

--- a/solution.py
+++ b/solution.py
@@ -14,6 +14,7 @@
 CHUNK = 128
 GROUP = 4
 
+ANY = pl.BlockSpec(memory_space=pl.ANY)
 VMEM = pl.BlockSpec(memory_space=pltpu.VMEM)
 SMEM = pl.BlockSpec(memory_space=pltpu.SMEM)
 
@@ -53,18 +54,19 @@
     return 0.5 * jnp.tanh(0.5 * pre) + 0.5
 
 
-def list_chunks(counts, capacity, block, start, live):
+def list_chunks(counts, capacity, block, start, live, blocks=range(9)):
     found = jnp.int32(0)
-    for k in range(counts.shape[1]):
+    for k in blocks:
         count = counts[0, k]
         for at in range(0, capacity, CHUNK):
             block[found] = k
             start[found] = at
             live[found] = count - at
             found += (count > at).astype(jnp.int32)
+    last = jnp.maximum(found - 1, 0)
     for j in range(GROUP - 1):
-        block[found + j] = counts.shape[1] // 2
-        start[found + j] = 0
+        block[found + j] = block[last]
+        start[found + j] = start[last]
         live[found + j] = 0
     return lax.div(found + (GROUP - 1), GROUP)
 
@@ -102,9 +104,17 @@
     each_group(groups, chunk_list, body)
 
 
-def enc_gather_kernel(counts, send, feat, weight, out, table, *chunk_list):
-    table[...] = mm(feat[...], weight[...]).astype(BF16)
-    gather_slots(counts, send, table, out, chunk_list)
+def enc_gather_kernel(
+    counts, send, feat, weight, out, table, send_in, feat_in, weight_in, sems, *chunk_list
+):
+    pairs = ((feat, feat_in), (weight, weight_in), (send, send_in))
+    copies = [pltpu.make_async_copy(a, b, sems.at[i]) for i, (a, b) in enumerate(pairs)]
+    for copy in copies:
+        copy.start()
+    for copy in copies:
+        copy.wait()
+    table[...] = mm(feat_in[...], weight_in[...]).astype(BF16)
+    gather_slots(counts, send_in, table, out, chunk_list)
 
 
 def side_gather_kernel(cols, counts, recv, feat, weight, bias, out, table, *chunk_list):
@@ -125,11 +135,13 @@
 
 def edge_groups(counts, index_ref, flips, side, total, outs, chunk_list, edges):
     rows = total.shape[1]
-    groups = list_chunks(counts, index_ref.shape[2], *chunk_list)
+    ours = len(outs) == 1
+    blocks = [k for k in range(9) if (k % 3 == 1) == ours]
+    groups = list_chunks(counts, index_ref.shape[2], *chunk_list, blocks=blocks)
     total[...] = jnp.zeros(total.shape, F32)
 
     def body(chunks):
-        places = [place_of(k, flips) for k, _, _ in chunks]
+        places = [place_of(k, flips) - (0 if ours else 3) for k, _, _ in chunks]
         index_rows = [rows_of(index_ref, chunk) for chunk in chunks]
 
         def gather(j):
@@ -147,12 +159,16 @@
         out[...] = total[3 * place : 3 * place + 3].astype(BF16)
 
 
-def enc_forward_kernel(
-    counts, flips, recv, own, first, second, weight, bias, sent,
-    out_own, out_first, out_second, slope, side, total, *chunk_list,
-):
-    rows = own.shape[1]
-    for place, near in enumerate((own, first, second)):
+def stack_near(nears, side):
+    for place, tiles in enumerate(nears):
+        side[3 * place : 3 * place + 3] = tiles[...]
+
+
+def enc_forward_kernel(n, counts, flips, recv, *refs):
+    nears, (weight, bias, sent), refs = refs[:n], refs[n : n + 3], refs[n + 3 + (n == 1) :]
+    outs, (slope, side, total, *chunk_list) = refs[:n], refs[n:]
+    rows = total.shape[1]
+    for place, near in enumerate(nears):
         feats = near[...].reshape(3 * rows, near.shape[2])
         exact = mm(feats, weight[...]) + bias[...]
         high = exact.astype(BF16)
@@ -168,7 +184,6 @@
         slope[k, pl.ds(at, CHUNK), :] = (squashed + message * (1.0 - squashed)).astype(BF16)
         return message.astype(BF16)
 
-    outs = (out_own, out_first, out_second)
     edge_groups(counts, recv, flips, side, total, outs, chunk_list, edges)
 
 
@@ -176,35 +191,30 @@
     return jnp.concatenate([lower[at], upper[at]], axis=1).astype(F32)
 
 
-def dec_kernel(
-    counts, flips, send, own, first, second, side_a, side_b, back_a, back_b,
-    out_own, out_first, out_second, messages, grads, near, total, *chunk_list,
-):
-    for place, tiles in enumerate((own, first, second)):
-        near[3 * place : 3 * place + 3] = tiles[...]
+def dec_kernel(n, counts, flips, send, *refs):
+    nears, tables, refs = refs[:n], refs[n : n + 4], refs[n + 4 + 2 * (n == 1) :]
+    outs, (messages, grads, near, total, *chunk_list) = refs[:n], refs[n:]
+    stack_near(nears, near)
 
     def edges(chunk, received):
         k, at, _ = chunk
         here = (k, pl.ds(at, CHUNK), slice(None))
-        pre = halves(side_a, side_b, here) + received
+        pre = halves(*tables[:2], here) + received
         squashed = gate(pre)
         message = pre * squashed
         messages[here] = message.astype(BF16)
         slope = squashed + message * (1.0 - squashed)
-        grad = (halves(back_a, back_b, here) * slope).astype(BF16)
+        grad = (halves(*tables[2:], here) * slope).astype(BF16)
         grads[here] = grad
         return grad
 
-    outs = (out_own, out_first, out_second)
     edge_groups(counts, send, flips, near, total, outs, chunk_list, edges)
 
 
-def enc_backward_kernel(
-    counts, flips, recv, own, first, second, slope,
-    out_own, out_first, out_second, grads, near, total, *chunk_list,
-):
-    for place, tiles in enumerate((own, first, second)):
-        near[3 * place : 3 * place + 3] = tiles[...]
+def enc_backward_kernel(n, counts, flips, recv, *refs):
+    nears, slope, refs = refs[:n], refs[n], refs[n + 1 + (n == 1) :]
+    outs, (grads, near, total, *chunk_list) = refs[:n], refs[n:]
+    stack_near(nears, near)
 
     def edges(chunk, received):
         k, at, _ = chunk
@@ -213,7 +223,6 @@
         grads[here] = grad
         return grad
 
-    outs = (out_own, out_first, out_second)
     edge_groups(counts, recv, flips, near, total, outs, chunk_list, edges)
 
 
@@ -243,16 +252,20 @@
     out[...] = (feat[...].astype(F32) + update).astype(BF16)
 
 
-def grid_grad_kernel(
-    cols, counts, send, grads, cot, dec_lower, dec_upper, lower, dec_weight, enc_weight,
-    out, total, *chunk_list,
+def dec_grid_kernel(
+    cols, counts, recv, grads, cot, lower, weight, out, total, *chunk_list
 ):
-    scatter_slots(counts, send, grads, total, chunk_list, cols)
+    scatter_slots(counts, recv, grads, total, chunk_list, cols)
     half = lower.shape[1]
-    back = mm_nt(dec_lower[...], dec_weight[:, :half]) + mm_nt(dec_upper[...], dec_weight[:, half:])
-    back += mm_nt(lower[...], enc_weight[:, :half])
-    back += mm_nt(total[...].astype(BF16), enc_weight[:, half:])
-    out[...] = (cot[...].astype(F32) + back).astype(BF16)
+    back = mm_nt(lower[...], weight[:, :half])
+    back += mm_nt(total[...].astype(BF16), weight[:, half:])
+    out[...] = cot[...].astype(F32) + back
+
+
+def grid_grad_kernel(counts, send, grads, partial, weight, out, total, *chunk_list):
+    scatter_slots(counts, send, grads, total, chunk_list)
+    back = mm_nt(total[...].astype(BF16), weight[...])
+    out[...] = (partial[...] + back).astype(BF16)
 
 
 def fold_kernel(own, east, west, kept, to_first, to_second):
@@ -315,11 +328,12 @@
         )
         return kept, lat_first(to_first), lat_second(to_second)
 
-    def kernel(body, outs, scratch, *args, smem=1, mib=12, work=0):
+    def kernel(body, outs, scratch, *args, smem=1, mib=12, work=0, specs=None, alias=()):
         return pl.pallas_call(
             body,
             out_shape=outs,
-            in_specs=[SMEM] * smem + [VMEM] * (len(args) - smem),
+            in_specs=specs or [SMEM] * smem + [VMEM] * (len(args) - smem),
+            input_output_aliases=dict(alias),
             out_specs=[VMEM] * len(outs),
             scratch_shapes=scratch,
             compiler_params=pltpu.CompilerParams(vmem_limit_bytes=mib * 1024 * 1024),
@@ -342,9 +356,9 @@
     rounded_half = [pltpu.VMEM((grid_rows, width // 2), BF16)] + chunk_list
     exact_half = [pltpu.VMEM((grid_rows, width // 2), F32)] + chunk_list
     rounded_grid = [pltpu.VMEM((grid_rows, width), BF16)] + chunk_list
-    near = pltpu.VMEM((9, mesh_rows, width), BF16)
-    near_split = pltpu.VMEM((9, 2 * mesh_rows, width), BF16)
-    near_total = pltpu.VMEM((9, mesh_rows, width), F32)
+    near = (mesh_rows, width), BF16
+    near_split = (2 * mesh_rows, width), BF16
+    near_total = (mesh_rows, width), F32
     enc_work = 2 * grid_rows * width * 9 * cap_e
     dec_work = 2 * grid_rows * width * 9 * cap_d
 
@@ -354,8 +368,17 @@
 
     near_feat = spread(mesh_feat)
     (sent,) = kernel(
-        enc_gather_kernel, enc_slots, rounded_grid,
-        enc_count, enc_send, grid_feat, enc_src, work=enc_work,
+        enc_gather_kernel, enc_slots,
+        [
+            rounded_grid[0],
+            pltpu.VMEM((9, 1, cap_e), jnp.int32),
+            pltpu.VMEM((grid_rows, width), BF16),
+            pltpu.VMEM((width, width), BF16),
+            pltpu.SemaphoreType.DMA((3,)),
+            *chunk_list,
+        ],
+        enc_count, enc_send, grid_feat, enc_src,
+        work=enc_work, specs=[SMEM, ANY, ANY, ANY],
     )
     back_at = [
         kernel(
@@ -373,21 +396,35 @@
         for cols in (lower, upper)
     ]
 
-    *enc_partial, slope = kernel(
-        enc_forward_kernel, three + enc_slots,
-        [near_split, near_total] + chunk_list,
-        enc_count, flips, enc_recv, *near_feat, enc_dst, enc_bias.reshape(1, width), sent,
-        smem=2, work=enc_work // 4,
+    def edges(body, counts, index, nears, extra, slots, scratch, work):
+        outs = []
+        fill = []
+        for n in (2, 1):
+            args = (counts, flips, index, *(nears[1:] if n == 2 else nears[:1]), *extra, *fill)
+            base = len(args) - len(fill)
+            made = kernel(
+                functools.partial(body, n), three[:n] + slots,
+                [pltpu.VMEM((3 * n,) + shape, kind) for shape, kind in scratch] + chunk_list,
+                *args, smem=2, work=n * work // 3,
+                alias=[(base + i, n + i) for i in range(len(fill))],
+            )
+            outs = list(made[:n]) + outs
+            fill = made[n:]
+        return outs, fill
+
+    enc_partial, (slope,) = edges(
+        enc_forward_kernel, enc_count, enc_recv, near_feat,
+        (enc_dst, enc_bias.reshape(1, width), sent), enc_slots, [near_split, near_total],
+        enc_work // 4,
     )
     (dec_proj,) = kernel(
         mesh_new_kernel, [tile], [],
         *fold(*enc_partial), mesh_feat, enc_out, dec_src, smem=0,
     )
 
-    *dec_partial, messages, dec_grads = kernel(
-        dec_kernel, three + dec_slots * 2, [near, near_total] + chunk_list,
-        dec_count, flips, dec_send, *spread(dec_proj), *side_at, *back_at,
-        smem=2, work=dec_work // 4,
+    dec_partial, (messages, dec_grads) = edges(
+        dec_kernel, dec_count, dec_send, spread(dec_proj),
+        (*side_at, *back_at), dec_slots * 2, [near, near_total], dec_work // 4,
     )
     mesh_back, enc_back = kernel(
         mesh_back_kernel, [exact_tile, tile], [],
@@ -402,32 +439,29 @@
         functools.partial(grid_new_kernel, upper), grid_tile, exact_half,
         dec_count, dec_recv, messages, grid_feat, sum_lower, dec_out, work=dec_work // 2,
     )
-    dec_local = [
-        kernel(
-            functools.partial(scatter_kernel, cols), half_grid, exact_half,
-            dec_count, dec_recv, dec_grads, work=dec_work // 2,
-        )[0]
-        for cols in (lower, upper)
-    ]
-
-    *grad_partial, grads = kernel(
-        enc_backward_kernel, three + enc_slots, [near, near_total] + chunk_list,
-        enc_count, flips, enc_recv, *spread(enc_back), slope,
-        smem=2, work=enc_work // 4,
+    (local_lower,) = kernel(
+        functools.partial(scatter_kernel, lower), half_grid, exact_half,
+        dec_count, dec_recv, dec_grads, work=dec_work // 2,
+    )
+    (dec_grid,) = kernel(
+        functools.partial(dec_grid_kernel, upper),
+        [jax.ShapeDtypeStruct((grid_rows, width), F32)], exact_half,
+        dec_count, dec_recv, dec_grads, grid_cot, local_lower, dec_dst, work=dec_work // 2,
+    )
+
+    grad_partial, (grads,) = edges(
+        enc_backward_kernel, enc_count, enc_recv, spread(enc_back),
+        (slope,), enc_slots, [near, near_total], enc_work // 4,
     )
     (mesh_grad,) = kernel(
         mesh_grad_kernel, [tile], [],
         *fold(*grad_partial), mesh_back, enc_dst, smem=0,
     )
 
-    (total_lower,) = kernel(
-        functools.partial(scatter_kernel, lower), half_grid, exact_half,
-        enc_count, enc_send, grads, work=enc_work // 2,
-    )
     (grid_grad,) = kernel(
-        functools.partial(grid_grad_kernel, upper), grid_tile, exact_half,
-        enc_count, enc_send, grads, grid_cot, *dec_local, total_lower, dec_dst, enc_src,
-        work=enc_work // 2,
+        grid_grad_kernel, grid_tile,
+        [pltpu.VMEM((grid_rows, width), F32)] + chunk_list,
+        enc_count, enc_send, grads, dec_grid, enc_src, work=enc_work,
     )
     return grid_new, mesh_grad, grid_grad
 

time: 114 us -> 112 us (0.982)
  waiting for transfers between devices: 8.12 us -> 5.06 us
    ppermute x24, waiting for transfers between devices: 8.12 us -> 5.06 us  [along(): return lambda value: lax.ppermute(value, axis, pairs)]
    pallas_call x20 -> x22, Pallas kernels: 56.3 us -> 57.3 us  [kernel(): pl.pallas_call(body, out_shape=outs, in_specs=specs or [SMEM] * smem + [V...]
  transfers between devices with their start and end apart: 24 -> 24, of which waited for: 7 -> 3; matrix products, arithmetic and copies ran while one was open for 0% -> 0% of each run, Pallas kernels for 37% -> 41%
where the time goes in v3:
time: 112 us
  Pallas kernels  57.3 us (51%)
  starting transfers between devices  43.5 us (39%)
  waiting for transfers between devices  5.06 us (5%)
  local copies, waits for them, and re-layouts  3.72 us (3%)
  between operations  1.12 us (1%)
    pallas_call x22, Pallas kernels, kernel(): pl.pallas_call(body, out_shape=outs, in_specs=specs or [SMEM] * smem + [V...  57.3 us
    ppermute x24, starting transfers between devices, along(): return lambda value: lax.ppermute(value, axis, pairs)  43.5 us
    ppermute x24, waiting for transfers between devices, along(): return lambda value: lax.ppermute(value, axis, pairs)  5.06 us
    unnamed x42, local copies, waits for them, and re-layouts  3.72 us
  transfers between devices with their start and end apart: 24, of which 3 were waited for; matrix products, arithmetic and copies ran while one was open for 0% of the time, Pallas kernels for 41%

profile of v3, /device:TPU:1, one launch (start us, length us, event | category | flops | bytes accessed | tf_op | source)
XLA Modules:
  0.0 111.6 jit_solution(13923425634097751194)
XLA Ops:
  0.6 2.2 %collective-permute-start = (bf16[64,512]{1,0:T(8,128)(2,1)}, bf16[64,512]{1,0:T(8,128)(2,1)S(1)}, u32[]{:S(2)}, u32[]{:S(2)}) collective-permute-start(bf16[64,512]{1,0:T(8,128)(2,1)} %feat.6), channel_id=1, source_target_pairs={{0,8},{16,24},{32,40},{48,56},{64,72},{80,88},{96,104},{112,120},{... | collective-permute-start | bytes 196616 | tf_op jit(solution)/shard_map/ppermute | solution.py:297
  2.8 5.4 %collective-permute-start.1 = (bf16[64,512]{1,0:T(8,128)(2,1)}, bf16[64,512]{1,0:T(8,128)(2,1)S(1)}, u32[]{:S(2)}, u32[]{:S(2)}) collective-permute-start(bf16[64,512]{1,0:T(8,128)(2,1)} %feat.6), channel_id=1, source_target_pairs={{8,16},{24,32},{40,48},{56,64},{72,80},{88,96},{104,112},{120,0},{... | collective-permute-start | bytes 196616 | tf_op jit(solution)/shard_map/ppermute | solution.py:297
  8.2 0.1 pad_add_fusion.flips
  8.3 1.8 %collective-permute-done.1 = bf16[64,512]{1,0:T(8,128)(2,1)S(1)} collective-permute-done((bf16[64,512]{1,0:T(8,128)(2,1)}, bf16[64,512]{1,0:T(8,128)(2,1)S(1)}, u32[]{:S(2)}, u32[]{:S(2)}) %collective-permute-start.1) | collective-permute-done | bytes 65568 | tf_op jit(solution)/shard_map/ppermute | solution.py:297
  10.1 0.9 pad_maximum_fusion.refs_0_
  11.0 3.0 %collective-permute-start.3 = (bf16[3,64,512]{2,1,0:T(8,128)(2,1)S(1)}, bf16[3,64,512]{2,1,0:T(8,128)(2,1)S(1)}, u32[]{:S(2)}, u32[]{:S(2)}) collective-permute-start(bf16[3,64,512]{2,1,0:T(8,128)(2,1)S(1)} %pad_maximum_fusion.refs_0_), channel_id=1, source_target_pairs={{1,2},{3,4},{5,6},{7,0},{2,1},{4,3},{6,5},{0,7},{9,10},{11,12},{13... | collective-permute-start | bytes 589832 | tf_op jit(solution)/shard_map/ppermute | solution.py:297
  14.0 0.7 copy-done.7
  14.6 1.2 %copy-done.10 = bf16[1024,512]{1,0:T(8,128)(2,1)S(1)} copy-done((bf16[1024,512]{1,0:T(8,128)(2,1)S(1)}, bf16[1024,512]{1,0:T(8,128)(2,1)}, u32[]{:S(2)}) %copy-start.10) | copy-done | bytes 1048600
  15.8 1.0 copy-done.15
  16.9 0.7 copy-done.18
  17.6 3.7 %shard_map.184.refs_4_.refs_3_ = bf16[9,256,512]{2,1,0:T(8,128)(2,1)S(1)} custom-call(s32[1,9]{1,0:T(1,128)S(1)} %copy-done.7, s32[9,1,256]{2,1,0:T(1,128)S(1)} %bitcast.36, bf16[1024,512]{1,0:T(8,128)(2,1)S(1)} %copy-done.10, bf16[512,512]{1,0:T(8,128)(2,1)S(1)} %copy-done.15), custom_call_target="tpu_custom_call" | custom-call | flops 2415919104 | tf_op jit(solution)/shard_map/pallas_call | solution.py:332
  21.3 0.0 copy-start.9
  21.3 0.0 copy-start.12
  21.3 0.0 copy-start.13
  21.3 0.0 copy-start.17
  21.4 2.7 %shard_map.185 = (bf16[3,64,512]{2,1,0:T(8,128)(2,1)S(1)}, bf16[3,64,512]{2,1,0:T(8,128)(2,1)S(1)}, bf16[9,256,512]{2,1,0:T(8,128)(2,1)S(1)}) custom-call(s32[1,9]{1,0:T(1,128)S(1)} %copy-done.7, s32[2]{0:T(128)S(1)} %pad_add_fusion.flips, s32[9,1,256]{2,1,0:T(1,128)S(1)} %bitcast.19, bf16[3,64,512]{2,1,0:T(8,128)(2,1)S(1)} %collective-permute-done.2.refs_0_, ...), custom_call_target="tpu_custom_call" | custom-call | flops 402653184 | tf_op jit(solution)/shard_map/pallas_call | solution.py:332
  24.1 0.6 collective-permute-start.4
  24.7 1.2 %collective-permute-start.5 = (bf16[3,64,512]{2,1,0:T(8,128)(2,1)S(1)}, bf16[3,64,512]{2,1,0:T(8,128)(2,1)S(1)}, u32[]{:S(2)}, u32[]{:S(2)}) collective-permute-start(bf16[3,64,512]{2,1,0:T(8,128)(2,1)S(1)} %get-tuple-element.34), channel_id=1, source_target_pairs={{1,2},{3,4},{5,6},{7,0},{2,1},{4,3},{6,5},{0,7},{9,10},{11,12},{13... | collective-permute-start | bytes 589832 | tf_op jit(solution)/shard_map/ppermute | solution.py:297
  25.9 0.0 copy-start.8
  25.9 4.1 %shard_map.192.refs_5_.refs_4_ = bf16[9,512,256]{2,1,0:T(8,128)(2,1)S(1)} custom-call(s32[1,9]{1,0:T(1,128)S(1)} %copy-done.9, s32[9,1,512]{2,1,0:T(1,128)S(1)} %bitcast.28, bf16[1024,512]{1,0:T(8,128)(2,1)S(1)} %copy-done.12, bf16[512,512]{1,0:T(8,128)(2,1)S(1)} %copy-done.13), custom_call_target="tpu_custom_call" | custom-call | flops 2415919104 | tf_op jit(solution)/shard_map/pallas_call | solution.py:332
  30.0 1.7 %shard_map.186 = (bf16[3,64,512]{2,1,0:T(8,128)(2,1)S(1)}, bf16[9,256,512]{2,1,0:T(8,128)(2,1)S(1)}) custom-call(s32[1,9]{1,0:T(1,128)S(1)} %copy-done.8, s32[2]{0:T(128)S(1)} %pad_add_fusion.flips, s32[9,1,256]{2,1,0:T(1,128)S(1)} %bitcast.20, bf16[3,64,512]{2,1,0:T(8,128)(2,1)S(1)} %pad_maximum_fusion.refs_0_, ...), custom_call_target="tpu_custom_call", output_to_operand_aliasing={{1}: (7, {})} | custom-call | flops 201326592 | tf_op jit(solution)/shard_map/pallas_call | solution.py:332
  31.8 0.1 shard_map.187
  31.8 0.1 collective-permute-start.6
  31.9 0.0 copy-start.1
  31.9 0.0 copy-start.2
  32.0 0.0 copy-start.3
  32.0 0.0 copy-start.11
  32.0 0.0 copy-start.20
  32.0 5.3 %collective-permute-start.7 = (bf16[64,512]{1,0:T(8,128)(2,1)S(1)}, bf16[64,512]{1,0:T(8,128)(2,1)S(1)}, u32[]{:S(2)}, u32[]{:S(2)}) collective-permute-start(bf16[64,512]{1,0:T(8,128)(2,1)S(1)} %get-tuple-element.37), channel_id=1, source_target_pairs={{8,16},{24,32},{40,48},{56,64},{72,80},{88,96},{104,112},{120,0},{... | collective-permute-start | bytes 196616 | tf_op jit(solution)/shard_map/ppermute | solution.py:297
  37.3 4.1 %shard_map.191.refs_4_.refs_3_ = bf16[9,512,256]{2,1,0:T(8,128)(2,1)S(1)} custom-call(s32[1,9]{1,0:T(1,128)S(1)} %copy-done.9, s32[9,1,512]{2,1,0:T(1,128)S(1)} %bitcast.29, bf16[1024,512]{1,0:T(8,128)(2,1)S(1)} %copy-done.12, bf16[512,512]{1,0:T(8,128)(2,1)S(1)} %copy-done.13), custom_call_target="tpu_custom_call" | custom-call | flops 2415919104 | tf_op jit(solution)/shard_map/pallas_call | solution.py:332
  41.4 0.4 shard_map.188
  41.8 2.4 %collective-permute-start.9 = (bf16[64,512]{1,0:T(8,128)(2,1)S(1)}, bf16[64,512]{1,0:T(8,128)(2,1)S(1)}, u32[]{:S(2)}, u32[]{:S(2)}) collective-permute-start(bf16[64,512]{1,0:T(8,128)(2,1)S(1)} %shard_map.188), channel_id=1, source_target_pairs={{8,16},{24,32},{40,48},{56,64},{72,80},{88,96},{104,112},{120,0},{... | collective-permute-start | bytes 196616 | tf_op jit(solution)/shard_map/ppermute | solution.py:297
  44.2 4.0 %shard_map.190.refs_3_.refs_2_ = bf16[9,512,256]{2,1,0:T(8,128)(2,1)S(1)} custom-call(s32[1,9]{1,0:T(1,128)S(1)} %copy-done.9, s32[9,1,512]{2,1,0:T(1,128)S(1)} %bitcast.30, bf16[1024,512]{1,0:T(8,128)(2,1)S(1)} %copy-done.11, bf16[512,512]{1,0:T(8,128)(2,1)S(1)} %copy-done.14, f32[1,512]{1,0:T(1,128)S(1)} %bitcast.38), custom_call_target="tpu_custom_call" | custom-call | flops 2415919104 | tf_op jit(solution)/shard_map/pallas_call | solution.py:332
  48.2 0.0 collective-permute-done.9
  48.3 2.6 %collective-permute-start.11 = (bf16[3,64,512]{2,1,0:T(8,128)(2,1)S(1)}, bf16[3,64,512]{2,1,0:T(8,128)(2,1)S(1)}, u32[]{:S(2)}, u32[]{:S(2)}) collective-permute-start(bf16[3,64,512]{2,1,0:T(8,128)(2,1)S(1)} %pad_maximum_fusion.1.refs_0_), channel_id=1, source_target_pairs={{1,2},{3,4},{5,6},{7,0},{2,1},{4,3},{6,5},{0,7},{9,10},{11,12},{13... | collective-permute-start | bytes 589832 | tf_op jit(solution)/shard_map/ppermute | solution.py:297
  50.9 0.3 collective-permute-start.10
  51.1 4.0 %shard_map.189.refs_2_.refs_1_ = bf16[9,512,256]{2,1,0:T(8,128)(2,1)S(1)} custom-call(s32[1,9]{1,0:T(1,128)S(1)} %copy-done.9, s32[9,1,512]{2,1,0:T(1,128)S(1)} %bitcast.31, bf16[1024,512]{1,0:T(8,128)(2,1)S(1)} %copy-done.11, bf16[512,512]{1,0:T(8,128)(2,1)S(1)} %copy-done.14, f32[1,512]{1,0:T(1,128)S(1)} %bitcast.39), custom_call_target="tpu_custom_call" | custom-call | flops 2415919104 | tf_op jit(solution)/shard_map/pallas_call | solution.py:332
  55.2 4.5 %shard_map.193 = (bf16[3,64,512]{2,1,0:T(8,128)(2,1)S(1)}, bf16[3,64,512]{2,1,0:T(8,128)(2,1)S(1)}, bf16[9,512,512]{2,1,0:T(8,128)(2,1)S(1)}, bf16[9,512,512]{2,1,0:T(8,128)(2,1)S(1)}) custom-call(s32[1,9]{1,0:T(1,128)S(1)} %copy-done.9, s32[2]{0:T(128)S(1)} %pad_add_fusion.flips, s32[9,1,512]{2,1,0:T(1,128)S(1)} %bitcast.23, ...), custom_call_target="tpu_custom_call" | custom-call | flops 805306368 | tf_op jit(solution)/shard_map/pallas_call | solution.py:332
  59.8 1.3 %collective-permute-start.12 = (bf16[3,64,512]{2,1,0:T(8,128)(2,1)S(1)}, bf16[3,64,512]{2,1,0:T(8,128)(2,1)S(1)}, u32[]{:S(2)}, u32[]{:S(2)}) collective-permute-start(bf16[3,64,512]{2,1,0:T(8,128)(2,1)S(1)} %get-tuple-element.42), channel_id=1, source_target_pairs={{0,1},{2,3},{4,5},{6,7},{1,0},{3,2},{5,4},{7,6},{8,9},{10,11},{12,... | collective-permute-start | bytes 589832 | tf_op jit(solution)/shard_map/ppermute | solution.py:297
  61.0 2.7 %shard_map.194 = (bf16[3,64,512]{2,1,0:T(8,128)(2,1)S(1)}, bf16[9,512,512]{2,1,0:T(8,128)(2,1)S(1)}, bf16[9,512,512]{2,1,0:T(8,128)(2,1)S(1)}) custom-call(s32[1,9]{1,0:T(1,128)S(1)} %copy-done.9, s32[2]{0:T(128)S(1)} %pad_add_fusion.flips, s32[9,1,512]{2,1,0:T(1,128)S(1)} %bitcast.24, ...), custom_call_target="tpu_custom_call", output_to_operand_aliasing={{1}: (8, {}), {2}: (9, {})} | custom-call | flops 402653184 | tf_op jit(solution)/shard_map/pallas_call | solution.py:332
  63.8 2.6 %collective-permute-done.13.west = bf16[3,64,512]{2,1,0:T(8,128)(2,1)S(1)} collective-permute-done((bf16[3,64,512]{2,1,0:T(8,128)(2,1)S(1)}, bf16[3,64,512]{2,1,0:T(8,128)(2,1)S(1)}, u32[]{:S(2)}, u32[]{:S(2)}) %collective-permute-start.13) | collective-permute-done | bytes 196640 | tf_op jit(solution)/shard_map/ppermute | solution.py:297
  66.4 0.1 shard_map.197
  66.5 2.6 %collective-permute-start.14 = (bf16[64,512]{1,0:T(8,128)(2,1)S(1)}, bf16[64,512]{1,0:T(8,128)(2,1)S(1)}, u32[]{:S(2)}, u32[]{:S(2)}) collective-permute-start(bf16[64,512]{1,0:T(8,128)(2,1)S(1)} %get-tuple-element.45), channel_id=1, source_target_pairs={{0,8},{16,24},{32,40},{48,56},{64,72},{80,88},{96,104},{112,120},{... | collective-permute-start | bytes 196616 | tf_op jit(solution)/shard_map/ppermute | solution.py:297
  69.1 2.5 %collective-permute-start.15 = (bf16[64,512]{1,0:T(8,128)(2,1)S(1)}, bf16[64,512]{1,0:T(8,128)(2,1)S(1)}, u32[]{:S(2)}, u32[]{:S(2)}) collective-permute-start(bf16[64,512]{1,0:T(8,128)(2,1)S(1)} %get-tuple-element.46), channel_id=1, source_target_pairs={{8,16},{24,32},{40,48},{56,64},{72,80},{88,96},{104,112},{120,0},{... | collective-permute-start | bytes 196616 | tf_op jit(solution)/shard_map/ppermute | solution.py:297
  71.6 3.4 %shard_map.195.lower = bf16[1024,256]{1,0:T(8,128)(2,1)S(1)} custom-call(s32[1,9]{1,0:T(1,128)S(1)} %copy-done.9, s32[9,1,512]{2,1,0:T(1,128)S(1)} %bitcast.32, bf16[9,512,512]{2,1,0:T(8,128)(2,1)S(1)} %get-tuple-element.40.values.messages), custom_call_target="tpu_custom_call" | custom-call | flops 2415919104 | tf_op jit(solution)/shard_map/pallas_call | solution.py:332
  75.1 0.5 collective-permute-done.15.second
  75.5 0.5 shard_map.198
  76.0 2.6 %collective-permute-start.17 = (bf16[64,512]{1,0:T(8,128)(2,1)S(1)}, bf16[64,512]{1,0:T(8,128)(2,1)S(1)}, u32[]{:S(2)}, u32[]{:S(2)}) collective-permute-start(bf16[64,512]{1,0:T(8,128)(2,1)S(1)} %get-tuple-element.47), channel_id=1, source_target_pairs={{8,16},{24,32},{40,48},{56,64},{72,80},{88,96},{104,112},{120,0},{... | collective-permute-start | bytes 196616 | tf_op jit(solution)/shard_map/ppermute | solution.py:297
  78.6 5.1 %shard_map.196 = bf16[1024,512]{1,0:T(8,128)(2,1)} custom-call(s32[1,9]{1,0:T(1,128)S(1)} %copy-done.9, s32[9,1,512]{2,1,0:T(1,128)S(1)} %bitcast.33, bf16[9,512,512]{2,1,0:T(8,128)(2,1)S(1)} %get-tuple-element.40.values.messages, bf16[1024,512]{1,0:T(8,128)(2,1)S(1)} %copy-done.11, bf16[1024,256]{1,0:T(8,128)(2,1)S(1)} %shard_map.195.lower, ...), custom_call_target="tpu_custom_call" | custom-call | flops 2415919104 | tf_op jit(solution)/shard_map/pallas_call | solution.py:332
  83.7 1.6 %collective-permute-start.19 = (bf16[3,64,512]{2,1,0:T(8,128)(2,1)S(1)}, bf16[3,64,512]{2,1,0:T(8,128)(2,1)S(1)}, u32[]{:S(2)}, u32[]{:S(2)}) collective-permute-start(bf16[3,64,512]{2,1,0:T(8,128)(2,1)S(1)} %pad_maximum_fusion.2.refs_0_), channel_id=1, source_target_pairs={{1,2},{3,4},{5,6},{7,0},{2,1},{4,3},{6,5},{0,7},{9,10},{11,12},{13... | collective-permute-start | bytes 589832 | tf_op jit(solution)/shard_map/ppermute | solution.py:297
  85.3 1.0 collective-permute-start.18
  86.3 3.4 %shard_map.203.lower = bf16[1024,256]{1,0:T(8,128)(2,1)S(1)} custom-call(s32[1,9]{1,0:T(1,128)S(1)} %copy-done.9, s32[9,1,512]{2,1,0:T(1,128)S(1)} %bitcast.34, bf16[9,512,512]{2,1,0:T(8,128)(2,1)S(1)} %get-tuple-element.58.values.grads), custom_call_target="tpu_custom_call" | custom-call | flops 2415919104 | tf_op jit(solution)/shard_map/pallas_call | solution.py:332
  89.8 1.9 %shard_map.199 = (bf16[3,64,512]{2,1,0:T(8,128)(2,1)S(1)}, bf16[3,64,512]{2,1,0:T(8,128)(2,1)S(1)}, bf16[9,256,512]{2,1,0:T(8,128)(2,1)S(1)}) custom-call(s32[1,9]{1,0:T(1,128)S(1)} %copy-done.8, s32[2]{0:T(128)S(1)} %pad_add_fusion.flips, s32[9,1,256]{2,1,0:T(1,128)S(1)} %bitcast.21, bf16[3,64,512]{2,1,0:T(8,128)(2,1)S(1)} %collective-permute-done.18.refs_0_, ...), custom_call_target="tpu_custom_call" | custom-call | flops 402653184 | tf_op jit(solution)/shard_map/pallas_call | solution.py:332
  91.7 2.9 %collective-permute-start.20 = (bf16[3,64,512]{2,1,0:T(8,128)(2,1)S(1)}, bf16[3,64,512]{2,1,0:T(8,128)(2,1)S(1)}, u32[]{:S(2)}, u32[]{:S(2)}) collective-permute-start(bf16[3,64,512]{2,1,0:T(8,128)(2,1)S(1)} %get-tuple-element.51), channel_id=1, source_target_pairs={{0,1},{2,3},{4,5},{6,7},{1,0},{3,2},{5,4},{7,6},{8,9},{10,11},{12,... | collective-permute-start | bytes 589832 | tf_op jit(solution)/shard_map/ppermute | solution.py:297
  94.6 4.1 %shard_map.204.partial = f32[1024,512]{1,0:T(8,128)S(1)} custom-call(s32[1,9]{1,0:T(1,128)S(1)} %copy-done.9, s32[9,1,512]{2,1,0:T(1,128)S(1)} %bitcast.35, bf16[9,512,512]{2,1,0:T(8,128)(2,1)S(1)} %get-tuple-element.58.values.grads, bf16[1024,512]{1,0:T(8,128)(2,1)S(1)} %copy-done.12, bf16[1024,256]{1,0:T(8,128)(2,1)S(1)} %shard_map.203.lower, ...), custom_call_target="tpu_custom_call" | custom-call | flops 2415919104 | tf_op jit(solution)/shard_map/pallas_call | solution.py:332
  98.7 0.0 copy-start.16
  98.7 0.0 copy-start.19
  98.7 1.2 %shard_map.200 = (bf16[3,64,512]{2,1,0:T(8,128)(2,1)S(1)}, bf16[9,256,512]{2,1,0:T(8,128)(2,1)S(1)}) custom-call(s32[1,9]{1,0:T(1,128)S(1)} %copy-done.8, s32[2]{0:T(128)S(1)} %pad_add_fusion.flips, s32[9,1,256]{2,1,0:T(1,128)S(1)} %bitcast.22, bf16[3,64,512]{2,1,0:T(8,128)(2,1)S(1)} %pad_maximum_fusion.2.refs_0_, ...), custom_call_target="tpu_custom_call", output_to_operand_aliasing={{1}: (5, {})} | custom-call | flops 201326592 | tf_op jit(solution)/shard_map/pallas_call | solution.py:332
  100.0 0.1 shard_map.201
  100.1 3.8 %collective-permute-start.22 = (bf16[64,512]{1,0:T(8,128)(2,1)S(1)}, bf16[64,512]{1,0:T(8,128)(2,1)S(1)}, u32[]{:S(2)}, u32[]{:S(2)}) collective-permute-start(bf16[64,512]{1,0:T(8,128)(2,1)S(1)} %get-tuple-element.54), channel_id=1, source_target_pairs={{0,8},{16,24},{32,40},{48,56},{64,72},{80,88},{96,104},{112,120},{... | collective-permute-start | bytes 196616 | tf_op jit(solution)/shard_map/ppermute | solution.py:297
  103.9 2.2 %collective-permute-start.23 = (bf16[64,512]{1,0:T(8,128)(2,1)S(1)}, bf16[64,512]{1,0:T(8,128)(2,1)S(1)}, u32[]{:S(2)}, u32[]{:S(2)}) collective-permute-start(bf16[64,512]{1,0:T(8,128)(2,1)S(1)} %get-tuple-element.55), channel_id=1, source_target_pairs={{8,16},{24,32},{40,48},{56,64},{72,80},{88,96},{104,112},{120,0},{... | collective-permute-start | bytes 196616 | tf_op jit(solution)/shard_map/ppermute | solution.py:297
  106.1 4.5 %shard_map.205 = bf16[1024,512]{1,0:T(8,128)(2,1)} custom-call(s32[1,9]{1,0:T(1,128)S(1)} %copy-done.8, s32[9,1,256]{2,1,0:T(1,128)S(1)} %bitcast.37, bf16[9,256,512]{2,1,0:T(8,128)(2,1)S(1)} %get-tuple-element.57.grads, f32[1024,512]{1,0:T(8,128)S(1)} %shard_map.204.partial, bf16[512,512]{1,0:T(8,128)(2,1)S(1)} %copy-done.16), custom_call_target="tpu_custom_call" | custom-call | flops 2415919104 | tf_op jit(solution)/shard_map/pallas_call | solution.py:332
  110.7 0.0 collective-permute-done.23.second
  110.7 0.9 shard_map.202
  (52 shorter events, 0.2 us)
Async XLA Ops:
  0.6 7.6 %collective-permute-start = (bf16[64,512]{1,0:T(8,128)(2,1)}, bf16[64,512]{1,0:T(8,128)(2,1)S(1)}, u32[]{:S(2)}, u32[]{:S(2)}) collective-permute-start(bf16[64,512]{1,0:T(8,128)(2,1)} %feat.6), channel_id=1, source_target_pairs={{0,8},{16,24},{32,40},{48,56},{64,72},{80,88},{96,104},{112,120},{... | collective-permute-start | bytes 196616 | tf_op jit(solution)/shard_map/ppermute | solution.py:297
  2.8 7.3 %collective-permute-start.1 = (bf16[64,512]{1,0:T(8,128)(2,1)}, bf16[64,512]{1,0:T(8,128)(2,1)S(1)}, u32[]{:S(2)}, u32[]{:S(2)}) collective-permute-start(bf16[64,512]{1,0:T(8,128)(2,1)} %feat.6), channel_id=1, source_target_pairs={{8,16},{24,32},{40,48},{56,64},{72,80},{88,96},{104,112},{120,0},{... | collective-permute-start | bytes 196616 | tf_op jit(solution)/shard_map/ppermute | solution.py:297
  11.0 10.4 %collective-permute-start.3 = (bf16[3,64,512]{2,1,0:T(8,128)(2,1)S(1)}, bf16[3,64,512]{2,1,0:T(8,128)(2,1)S(1)}, u32[]{:S(2)}, u32[]{:S(2)}) collective-permute-start(bf16[3,64,512]{2,1,0:T(8,128)(2,1)S(1)} %pad_maximum_fusion.refs_0_), channel_id=1, source_target_pairs={{1,2},{3,4},{5,6},{7,0},{2,1},{4,3},{6,5},{0,7},{9,10},{11,12},{13... | collective-permute-start | bytes 589832 | tf_op jit(solution)/shard_map/ppermute | solution.py:297
  14.0 7.4 %collective-permute-start.2 = (bf16[3,64,512]{2,1,0:T(8,128)(2,1)S(1)}, bf16[3,64,512]{2,1,0:T(8,128)(2,1)S(1)}, u32[]{:S(2)}, u32[]{:S(2)}) collective-permute-start(bf16[3,64,512]{2,1,0:T(8,128)(2,1)S(1)} %pad_maximum_fusion.refs_0_), channel_id=1, source_target_pairs={{0,1},{2,3},{4,5},{6,7},{1,0},{3,2},{5,4},{7,6},{8,9},{10,11},{12,... | collective-permute-start | bytes 589832 | tf_op jit(solution)/shard_map/ppermute | solution.py:297
  14.0 0.7 copy-start.7
  14.6 1.2 %copy-start.10 = (bf16[1024,512]{1,0:T(8,128)(2,1)S(1)}, bf16[1024,512]{1,0:T(8,128)(2,1)}, u32[]{:S(2)}) copy-start(bf16[1024,512]{1,0:T(8,128)(2,1)} %feat.9) | copy-start | bytes 3145732
  15.8 1.0 copy-start.15
  16.9 0.7 copy-start.18
  17.6 3.8 %copy-start = (bf16[512,512]{1,0:T(8,128)(2,1)S(1)}, bf16[512,512]{1,0:T(8,128)(2,1)}, u32[]{:S(2)}) copy-start(bf16[512,512]{1,0:T(8,128)(2,1)} %weight.19) | copy-start | bytes 1572868
  17.6 3.8 %copy-start.4 = (s32[1,9,256]{2,0,1:T(1,128)S(1)}, s32[1,9,256]{2,0,1:T(1,128)}, u32[]{:S(2)}) copy-start(s32[1,9,256]{2,0,1:T(1,128)} %param.20) | copy-start | bytes 27652
  17.6 3.8 %copy-start.6 = (f32[512]{0:T(512)S(1)}, f32[512]{0:T(512)}, u32[]{:S(2)}) copy-start(f32[512]{0:T(512)} %param.27) | copy-start | bytes 6148
  21.3 4.6 %copy-start.9 = (s32[1,9]{1,0:T(1,128)S(1)}, s32[1,9]{1,0:T(1,128)}, u32[]{:S(2)}) copy-start(s32[1,9]{1,0:T(1,128)} %counts.30) | copy-start | bytes 112
  21.3 4.6 %copy-start.12 = (bf16[1024,512]{1,0:T(8,128)(2,1)S(1)}, bf16[1024,512]{1,0:T(8,128)(2,1)}, u32[]{:S(2)}) copy-start(bf16[1024,512]{1,0:T(8,128)(2,1)} %cot.5) | copy-start | bytes 3145732
  21.3 4.6 %copy-start.13 = (bf16[512,512]{1,0:T(8,128)(2,1)S(1)}, bf16[512,512]{1,0:T(8,128)(2,1)}, u32[]{:S(2)}) copy-start(bf16[512,512]{1,0:T(8,128)(2,1)} %weight.17) | copy-start | bytes 1572868
  21.3 4.6 %copy-start.17 = (s32[1,9,512]{2,0,1:T(1,128)S(1)}, s32[1,9,512]{2,0,1:T(1,128)}, u32[]{:S(2)}) copy-start(s32[1,9,512]{2,0,1:T(1,128)} %param.23) | copy-start | bytes 55300
  24.1 7.6 %collective-permute-start.4 = (bf16[3,64,512]{2,1,0:T(8,128)(2,1)S(1)}, bf16[3,64,512]{2,1,0:T(8,128)(2,1)S(1)}, u32[]{:S(2)}, u32[]{:S(2)}) collective-permute-start(bf16[3,64,512]{2,1,0:T(8,128)(2,1)S(1)} %get-tuple-element.33), channel_id=1, source_target_pairs={{0,1},{2,3},{4,5},{6,7},{1,0},{3,2},{5,4},{7,6},{8,9},{10,11},{12,... | collective-permute-start | bytes 589832 | tf_op jit(solution)/shard_map/ppermute | solution.py:297
  24.7 7.0 %collective-permute-start.5 = (bf16[3,64,512]{2,1,0:T(8,128)(2,1)S(1)}, bf16[3,64,512]{2,1,0:T(8,128)(2,1)S(1)}, u32[]{:S(2)}, u32[]{:S(2)}) collective-permute-start(bf16[3,64,512]{2,1,0:T(8,128)(2,1)S(1)} %get-tuple-element.34), channel_id=1, source_target_pairs={{1,2},{3,4},{5,6},{7,0},{2,1},{4,3},{6,5},{0,7},{9,10},{11,12},{13... | collective-permute-start | bytes 589832 | tf_op jit(solution)/shard_map/ppermute | solution.py:297
  25.9 4.1 %copy-start.8 = (s32[1,9]{1,0:T(1,128)S(1)}, s32[1,9]{1,0:T(1,128)}, u32[]{:S(2)}) copy-start(s32[1,9]{1,0:T(1,128)} %counts.31) | copy-start | bytes 112
  31.8 9.5 %collective-permute-start.6 = (bf16[64,512]{1,0:T(8,128)(2,1)S(1)}, bf16[64,512]{1,0:T(8,128)(2,1)S(1)}, u32[]{:S(2)}, u32[]{:S(2)}) collective-permute-start(bf16[64,512]{1,0:T(8,128)(2,1)S(1)} %get-tuple-element.36), channel_id=1, source_target_pairs={{0,8},{16,24},{32,40},{48,56},{64,72},{80,88},{96,104},{112,120},{... | collective-permute-start | bytes 196616 | tf_op jit(solution)/shard_map/ppermute | solution.py:297
  31.9 9.4 %copy-start.1 = (bf16[512,512]{1,0:T(8,128)(2,1)S(1)}, bf16[512,512]{1,0:T(8,128)(2,1)}, u32[]{:S(2)}) copy-start(bf16[512,512]{1,0:T(8,128)(2,1)} %out_weight.3) | copy-start | bytes 1572868
  31.9 9.4 %copy-start.2 = (bf16[512,512]{1,0:T(8,128)(2,1)S(1)}, bf16[512,512]{1,0:T(8,128)(2,1)}, u32[]{:S(2)}) copy-start(bf16[512,512]{1,0:T(8,128)(2,1)} %weight.18) | copy-start | bytes 1572868
  32.0 9.4 %copy-start.3 = (bf16[64,512]{1,0:T(8,128)(2,1)S(1)}, bf16[64,512]{1,0:T(8,128)(2,1)}, u32[]{:S(2)}) copy-start(bf16[64,512]{1,0:T(8,128)(2,1)} %feat.6) | copy-start | bytes 196612
  32.0 12.2 %copy-start.11 = (bf16[1024,512]{1,0:T(8,128)(2,1)S(1)}, bf16[1024,512]{1,0:T(8,128)(2,1)}, u32[]{:S(2)}) copy-start(bf16[1024,512]{1,0:T(8,128)(2,1)} %feat.9) | copy-start | bytes 3145732
  32.0 12.2 %copy-start.14 = (bf16[512,512]{1,0:T(8,128)(2,1)S(1)}, bf16[512,512]{1,0:T(8,128)(2,1)}, u32[]{:S(2)}) copy-start(bf16[512,512]{1,0:T(8,128)(2,1)} %weight.20) | copy-start | bytes 1572868
  32.0 12.2 %copy-start.20 = (f32[512]{0:T(512)S(1)}, f32[512]{0:T(512)}, u32[]{:S(2)}) copy-start(f32[512]{0:T(512)} %param.31) | copy-start | bytes 6148
  32.0 9.3 %collective-permute-start.7 = (bf16[64,512]{1,0:T(8,128)(2,1)S(1)}, bf16[64,512]{1,0:T(8,128)(2,1)S(1)}, u32[]{:S(2)}, u32[]{:S(2)}) collective-permute-start(bf16[64,512]{1,0:T(8,128)(2,1)S(1)} %get-tuple-element.37), channel_id=1, source_target_pairs={{8,16},{24,32},{40,48},{56,64},{72,80},{88,96},{104,112},{120,0},{... | collective-permute-start | bytes 196616 | tf_op jit(solution)/shard_map/ppermute | solution.py:297
  41.8 6.5 %collective-permute-start.9 = (bf16[64,512]{1,0:T(8,128)(2,1)S(1)}, bf16[64,512]{1,0:T(8,128)(2,1)S(1)}, u32[]{:S(2)}, u32[]{:S(2)}) collective-permute-start(bf16[64,512]{1,0:T(8,128)(2,1)S(1)} %shard_map.188), channel_id=1, source_target_pairs={{8,16},{24,32},{40,48},{56,64},{72,80},{88,96},{104,112},{120,0},{... | collective-permute-start | bytes 196616 | tf_op jit(solution)/shard_map/ppermute | solution.py:297
  44.2 4.1 %collective-permute-start.8 = (bf16[64,512]{1,0:T(8,128)(2,1)S(1)}, bf16[64,512]{1,0:T(8,128)(2,1)S(1)}, u32[]{:S(2)}, u32[]{:S(2)}) collective-permute-start(bf16[64,512]{1,0:T(8,128)(2,1)S(1)} %shard_map.188), channel_id=1, source_target_pairs={{0,8},{16,24},{32,40},{48,56},{64,72},{80,88},{96,104},{112,120},{... | collective-permute-start | bytes 196616 | tf_op jit(solution)/shard_map/ppermute | solution.py:297
  48.3 6.9 %copy-start.5 = (s32[1,9,512]{2,0,1:T(1,128)S(1)}, s32[1,9,512]{2,0,1:T(1,128)}, u32[]{:S(2)}) copy-start(s32[1,9,512]{2,0,1:T(1,128)} %param.22) | copy-start | bytes 55300
  48.3 6.9 %collective-permute-start.11 = (bf16[3,64,512]{2,1,0:T(8,128)(2,1)S(1)}, bf16[3,64,512]{2,1,0:T(8,128)(2,1)S(1)}, u32[]{:S(2)}, u32[]{:S(2)}) collective-permute-start(bf16[3,64,512]{2,1,0:T(8,128)(2,1)S(1)} %pad_maximum_fusion.1.refs_0_), channel_id=1, source_target_pairs={{1,2},{3,4},{5,6},{7,0},{2,1},{4,3},{6,5},{0,7},{9,10},{11,12},{13... | collective-permute-start | bytes 589832 | tf_op jit(solution)/shard_map/ppermute | solution.py:297
  50.9 4.3 %collective-permute-start.10 = (bf16[3,64,512]{2,1,0:T(8,128)(2,1)S(1)}, bf16[3,64,512]{2,1,0:T(8,128)(2,1)S(1)}, u32[]{:S(2)}, u32[]{:S(2)}) collective-permute-start(bf16[3,64,512]{2,1,0:T(8,128)(2,1)S(1)} %pad_maximum_fusion.1.refs_0_), channel_id=1, source_target_pairs={{0,1},{2,3},{4,5},{6,7},{1,0},{3,2},{5,4},{7,6},{8,9},{10,11},{12,... | collective-permute-start | bytes 589832 | tf_op jit(solution)/shard_map/ppermute | solution.py:297
  59.8 4.0 %collective-permute-start.12 = (bf16[3,64,512]{2,1,0:T(8,128)(2,1)S(1)}, bf16[3,64,512]{2,1,0:T(8,128)(2,1)S(1)}, u32[]{:S(2)}, u32[]{:S(2)}) collective-permute-start(bf16[3,64,512]{2,1,0:T(8,128)(2,1)S(1)} %get-tuple-element.42), channel_id=1, source_target_pairs={{0,1},{2,3},{4,5},{6,7},{1,0},{3,2},{5,4},{7,6},{8,9},{10,11},{12,... | collective-permute-start | bytes 589832 | tf_op jit(solution)/shard_map/ppermute | solution.py:297
  61.0 5.4 %collective-permute-start.13 = (bf16[3,64,512]{2,1,0:T(8,128)(2,1)S(1)}, bf16[3,64,512]{2,1,0:T(8,128)(2,1)S(1)}, u32[]{:S(2)}, u32[]{:S(2)}) collective-permute-start(bf16[3,64,512]{2,1,0:T(8,128)(2,1)S(1)} %get-tuple-element.43), channel_id=1, source_target_pairs={{1,2},{3,4},{5,6},{7,0},{2,1},{4,3},{6,5},{0,7},{9,10},{11,12},{13... | collective-permute-start | bytes 589832 | tf_op jit(solution)/shard_map/ppermute | solution.py:297
  66.5 8.6 %collective-permute-start.14 = (bf16[64,512]{1,0:T(8,128)(2,1)S(1)}, bf16[64,512]{1,0:T(8,128)(2,1)S(1)}, u32[]{:S(2)}, u32[]{:S(2)}) collective-permute-start(bf16[64,512]{1,0:T(8,128)(2,1)S(1)} %get-tuple-element.45), channel_id=1, source_target_pairs={{0,8},{16,24},{32,40},{48,56},{64,72},{80,88},{96,104},{112,120},{... | collective-permute-start | bytes 196616 | tf_op jit(solution)/shard_map/ppermute | solution.py:297
  69.1 6.4 %collective-permute-start.15 = (bf16[64,512]{1,0:T(8,128)(2,1)S(1)}, bf16[64,512]{1,0:T(8,128)(2,1)S(1)}, u32[]{:S(2)}, u32[]{:S(2)}) collective-permute-start(bf16[64,512]{1,0:T(8,128)(2,1)S(1)} %get-tuple-element.46), channel_id=1, source_target_pairs={{8,16},{24,32},{40,48},{56,64},{72,80},{88,96},{104,112},{120,0},{... | collective-permute-start | bytes 196616 | tf_op jit(solution)/shard_map/ppermute | solution.py:297
  76.0 7.7 %collective-permute-start.17 = (bf16[64,512]{1,0:T(8,128)(2,1)S(1)}, bf16[64,512]{1,0:T(8,128)(2,1)S(1)}, u32[]{:S(2)}, u32[]{:S(2)}) collective-permute-start(bf16[64,512]{1,0:T(8,128)(2,1)S(1)} %get-tuple-element.47), channel_id=1, source_target_pairs={{8,16},{24,32},{40,48},{56,64},{72,80},{88,96},{104,112},{120,0},{... | collective-permute-start | bytes 196616 | tf_op jit(solution)/shard_map/ppermute | solution.py:297
  78.6 5.1 %collective-permute-start.16 = (bf16[64,512]{1,0:T(8,128)(2,1)S(1)}, bf16[64,512]{1,0:T(8,128)(2,1)S(1)}, u32[]{:S(2)}, u32[]{:S(2)}) collective-permute-start(bf16[64,512]{1,0:T(8,128)(2,1)S(1)} %get-tuple-element.47), channel_id=1, source_target_pairs={{0,8},{16,24},{32,40},{48,56},{64,72},{80,88},{96,104},{112,120},{... | collective-permute-start | bytes 196616 | tf_op jit(solution)/shard_map/ppermute | solution.py:297
  83.7 6.0 %collective-permute-start.19 = (bf16[3,64,512]{2,1,0:T(8,128)(2,1)S(1)}, bf16[3,64,512]{2,1,0:T(8,128)(2,1)S(1)}, u32[]{:S(2)}, u32[]{:S(2)}) collective-permute-start(bf16[3,64,512]{2,1,0:T(8,128)(2,1)S(1)} %pad_maximum_fusion.2.refs_0_), channel_id=1, source_target_pairs={{1,2},{3,4},{5,6},{7,0},{2,1},{4,3},{6,5},{0,7},{9,10},{11,12},{13... | collective-permute-start | bytes 589832 | tf_op jit(solution)/shard_map/ppermute | solution.py:297
  85.3 4.4 %collective-permute-start.18 = (bf16[3,64,512]{2,1,0:T(8,128)(2,1)S(1)}, bf16[3,64,512]{2,1,0:T(8,128)(2,1)S(1)}, u32[]{:S(2)}, u32[]{:S(2)}) collective-permute-start(bf16[3,64,512]{2,1,0:T(8,128)(2,1)S(1)} %pad_maximum_fusion.2.refs_0_), channel_id=1, source_target_pairs={{0,1},{2,3},{4,5},{6,7},{1,0},{3,2},{5,4},{7,6},{8,9},{10,11},{12,... | collective-permute-start | bytes 589832 | tf_op jit(solution)/shard_map/ppermute | solution.py:297
  91.7 8.3 %collective-permute-start.20 = (bf16[3,64,512]{2,1,0:T(8,128)(2,1)S(1)}, bf16[3,64,512]{2,1,0:T(8,128)(2,1)S(1)}, u32[]{:S(2)}, u32[]{:S(2)}) collective-permute-start(bf16[3,64,512]{2,1,0:T(8,128)(2,1)S(1)} %get-tuple-element.51), channel_id=1, source_target_pairs={{0,1},{2,3},{4,5},{6,7},{1,0},{3,2},{5,4},{7,6},{8,9},{10,11},{12,... | collective-permute-start | bytes 589832 | tf_op jit(solution)/shard_map/ppermute | solution.py:297
  94.6 5.4 %collective-permute-start.21 = (bf16[3,64,512]{2,1,0:T(8,128)(2,1)S(1)}, bf16[3,64,512]{2,1,0:T(8,128)(2,1)S(1)}, u32[]{:S(2)}, u32[]{:S(2)}) collective-permute-start(bf16[3,64,512]{2,1,0:T(8,128)(2,1)S(1)} %get-tuple-element.52), channel_id=1, source_target_pairs={{1,2},{3,4},{5,6},{7,0},{2,1},{4,3},{6,5},{0,7},{9,10},{11,12},{13... | collective-permute-start | bytes 589832 | tf_op jit(solution)/shard_map/ppermute | solution.py:297
  98.7 7.4 %copy-start.16 = (bf16[512,512]{1,0:T(8,128)(2,1)S(1)}, bf16[512,512]{1,0:T(8,128)(2,1)}, u32[]{:S(2)}) copy-start(bf16[512,512]{1,0:T(8,128)(2,1)} %weight.21) | copy-start | bytes 1572868
  98.7 7.4 %copy-start.19 = (s32[1,9,256]{2,0,1:T(1,128)S(1)}, s32[1,9,256]{2,0,1:T(1,128)}, u32[]{:S(2)}) copy-start(s32[1,9,256]{2,0,1:T(1,128)} %param.19) | copy-start | bytes 27652
  100.1 10.6 %collective-permute-start.22 = (bf16[64,512]{1,0:T(8,128)(2,1)S(1)}, bf16[64,512]{1,0:T(8,128)(2,1)S(1)}, u32[]{:S(2)}, u32[]{:S(2)}) collective-permute-start(bf16[64,512]{1,0:T(8,128)(2,1)S(1)} %get-tuple-element.54), channel_id=1, source_target_pairs={{0,8},{16,24},{32,40},{48,56},{64,72},{80,88},{96,104},{112,120},{... | collective-permute-start | bytes 196616 | tf_op jit(solution)/shard_map/ppermute | solution.py:297
  103.9 6.8 %collective-permute-start.23 = (bf16[64,512]{1,0:T(8,128)(2,1)S(1)}, bf16[64,512]{1,0:T(8,128)(2,1)S(1)}, u32[]{:S(2)}, u32[]{:S(2)}) collective-permute-start(bf16[64,512]{1,0:T(8,128)(2,1)S(1)} %get-tuple-element.55), channel_id=1, source_target_pairs={{8,16},{24,32},{40,48},{56,64},{72,80},{88,96},{104,112},{120,0},{... | collective-permute-start | bytes 196616 | tf_op jit(solution)/shard_map/ppermute | solution.py:297

commit v4 on v3

--- a/solution.py
+++ b/solution.py
@@ -14,7 +14,7 @@
 CHUNK = 128
 GROUP = 4
 
-ANY = pl.BlockSpec(memory_space=pl.ANY)
+HBM = pl.BlockSpec(memory_space=pltpu.HBM)
 VMEM = pl.BlockSpec(memory_space=pltpu.VMEM)
 SMEM = pl.BlockSpec(memory_space=pltpu.SMEM)
 
@@ -377,8 +377,11 @@
             pltpu.SemaphoreType.DMA((3,)),
             *chunk_list,
         ],
-        enc_count, enc_send, grid_feat, enc_src,
-        work=enc_work, specs=[SMEM, ANY, ANY, ANY],
+        *(
+            pltpu.with_memory_space_constraint(a, pltpu.HBM)
+            for a in (enc_count, enc_send, grid_feat, enc_src)
+        ),
+        work=enc_work, specs=[SMEM, HBM, HBM, HBM],
     )
     back_at = [
         kernel(

time: 112 us -> 110 us (0.982)
  local copies, waits for them, and re-layouts: 3.72 us -> 0.1 us
  Pallas kernels: 57.3 us -> 58.8 us
    unnamed x42 -> x34, local copies, waits for them, and re-layouts: 3.72 us -> 0.1 us
    pallas_call x22, Pallas kernels: 57.3 us -> 58.8 us  [kernel(): pl.pallas_call(body, out_shape=outs, in_specs=specs or [SMEM] * smem + [V...]
  transfers between devices with their start and end apart: 24 -> 24, of which waited for: 3 -> 3; matrix products, arithmetic and copies ran while one was open for 0% -> 0% of each run, Pallas kernels for 41% -> 43%
where the time goes in v4:
time: 110 us; the launch traced here: 109 us
  Pallas kernels  58.8 us (53%)
  starting transfers between devices  43.4 us (39%)
  waiting for transfers between devices  5.06 us (5%)
  between operations  1.12 us (1%)
    pallas_call x22, Pallas kernels, kernel(): pl.pallas_call(body, out_shape=outs, in_specs=specs or [SMEM] * smem + [V...  58.8 us
    ppermute x24, starting transfers between devices, along(): return lambda value: lax.ppermute(value, axis, pairs)  43.4 us
    ppermute x24, waiting for transfers between devices, along(): return lambda value: lax.ppermute(value, axis, pairs)  5.06 us
  transfers between devices with their start and end apart: 24, of which 3 were waited for; matrix products, arithmetic and copies ran while one was open for 0% of the time, Pallas kernels for 43%

profile of v4, /device:TPU:1, one launch (start us, length us, event | category | flops | bytes accessed | tf_op | source)
XLA Modules:
  0.0 109.5 jit_solution(15822711010501689501)
XLA Ops:
  0.6 2.2 %collective-permute-start = (bf16[64,512]{1,0:T(8,128)(2,1)}, bf16[64,512]{1,0:T(8,128)(2,1)S(1)}, u32[]{:S(2)}, u32[]{:S(2)}) collective-permute-start(bf16[64,512]{1,0:T(8,128)(2,1)} %feat.6), channel_id=1, source_target_pairs={{0,8},{16,24},{32,40},{48,56},{64,72},{80,88},{96,104},{112,120},{... | collective-permute-start | bytes 196616 | tf_op jit(solution)/shard_map/ppermute | solution.py:297
  2.8 5.4 %collective-permute-start.1 = (bf16[64,512]{1,0:T(8,128)(2,1)}, bf16[64,512]{1,0:T(8,128)(2,1)S(1)}, u32[]{:S(2)}, u32[]{:S(2)}) collective-permute-start(bf16[64,512]{1,0:T(8,128)(2,1)} %feat.6), channel_id=1, source_target_pairs={{8,16},{24,32},{40,48},{56,64},{72,80},{88,96},{104,112},{120,0},{... | collective-permute-start | bytes 196616 | tf_op jit(solution)/shard_map/ppermute | solution.py:297
  8.2 0.1 pad_add_fusion.flips
  8.3 1.8 %collective-permute-done.1 = bf16[64,512]{1,0:T(8,128)(2,1)S(1)} collective-permute-done((bf16[64,512]{1,0:T(8,128)(2,1)}, bf16[64,512]{1,0:T(8,128)(2,1)S(1)}, u32[]{:S(2)}, u32[]{:S(2)}) %collective-permute-start.1) | collective-permute-done | bytes 65568 | tf_op jit(solution)/shard_map/ppermute | solution.py:297
  10.1 0.9 pad_maximum_fusion.refs_0_
  11.0 3.0 %collective-permute-start.3 = (bf16[3,64,512]{2,1,0:T(8,128)(2,1)S(1)}, bf16[3,64,512]{2,1,0:T(8,128)(2,1)S(1)}, u32[]{:S(2)}, u32[]{:S(2)}) collective-permute-start(bf16[3,64,512]{2,1,0:T(8,128)(2,1)S(1)} %pad_maximum_fusion.refs_0_), channel_id=1, source_target_pairs={{1,2},{3,4},{5,6},{7,0},{2,1},{4,3},{6,5},{0,7},{9,10},{11,12},{13... | collective-permute-start | bytes 589832 | tf_op jit(solution)/shard_map/ppermute | solution.py:297
  14.0 0.0 copy-start.7
  14.0 5.2 %shard_map.184.refs_4_.refs_3_ = bf16[9,256,512]{2,1,0:T(8,128)(2,1)S(1)} custom-call(s32[1,9]{1,0:T(1,128)} %counts.31, s32[9,1,256]{2,1,0:T(1,128)} %bitcast.36, bf16[1024,512]{1,0:T(8,128)(2,1)} %feat.9, bf16[512,512]{1,0:T(8,128)(2,1)} %weight.21), custom_call_target="tpu_custom_call" | custom-call | flops 2415919104 | tf_op jit(solution)/shard_map/pallas_call | solution.py:332
  19.2 0.0 copy-start.8
  19.2 0.0 copy-start.10
  19.2 0.0 copy-start.11
  19.2 0.0 copy-start.14
  19.2 0.0 collective-permute-done.3.refs_1_
  19.3 2.7 %shard_map.185 = (bf16[3,64,512]{2,1,0:T(8,128)(2,1)S(1)}, bf16[3,64,512]{2,1,0:T(8,128)(2,1)S(1)}, bf16[9,256,512]{2,1,0:T(8,128)(2,1)S(1)}) custom-call(s32[1,9]{1,0:T(1,128)S(1)} %copy-done.7, s32[2]{0:T(128)S(1)} %pad_add_fusion.flips, s32[9,1,256]{2,1,0:T(1,128)S(1)} %bitcast.19, bf16[3,64,512]{2,1,0:T(8,128)(2,1)S(1)} %collective-permute-done.2.refs_0_, ...), custom_call_target="tpu_custom_call" | custom-call | flops 402653184 | tf_op jit(solution)/shard_map/pallas_call | solution.py:332
  22.0 0.6 collective-permute-start.4
  22.6 1.2 %collective-permute-start.5 = (bf16[3,64,512]{2,1,0:T(8,128)(2,1)S(1)}, bf16[3,64,512]{2,1,0:T(8,128)(2,1)S(1)}, u32[]{:S(2)}, u32[]{:S(2)}) collective-permute-start(bf16[3,64,512]{2,1,0:T(8,128)(2,1)S(1)} %get-tuple-element.34), channel_id=1, source_target_pairs={{1,2},{3,4},{5,6},{7,0},{2,1},{4,3},{6,5},{0,7},{9,10},{11,12},{13... | collective-permute-start | bytes 589832 | tf_op jit(solution)/shard_map/ppermute | solution.py:297
  23.8 4.1 %shard_map.192.refs_5_.refs_4_ = bf16[9,512,256]{2,1,0:T(8,128)(2,1)S(1)} custom-call(s32[1,9]{1,0:T(1,128)S(1)} %copy-done.8, s32[9,1,512]{2,1,0:T(1,128)S(1)} %bitcast.28, bf16[1024,512]{1,0:T(8,128)(2,1)S(1)} %copy-done.10, bf16[512,512]{1,0:T(8,128)(2,1)S(1)} %copy-done.11), custom_call_target="tpu_custom_call" | custom-call | flops 2415919104 | tf_op jit(solution)/shard_map/pallas_call | solution.py:332
  27.9 1.7 %shard_map.186 = (bf16[3,64,512]{2,1,0:T(8,128)(2,1)S(1)}, bf16[9,256,512]{2,1,0:T(8,128)(2,1)S(1)}) custom-call(s32[1,9]{1,0:T(1,128)S(1)} %copy-done.7, s32[2]{0:T(128)S(1)} %pad_add_fusion.flips, s32[9,1,256]{2,1,0:T(1,128)S(1)} %bitcast.20, bf16[3,64,512]{2,1,0:T(8,128)(2,1)S(1)} %pad_maximum_fusion.refs_0_, ...), custom_call_target="tpu_custom_call", output_to_operand_aliasing={{1}: (7, {})} | custom-call | flops 201326592 | tf_op jit(solution)/shard_map/pallas_call | solution.py:332
  29.6 0.0 collective-permute-done.4.east
  29.6 0.1 shard_map.187
  29.7 0.1 collective-permute-start.6
  29.8 0.0 copy-start.1
  29.8 0.0 copy-start.2
  29.8 0.0 copy-start.3
  29.8 0.0 copy-start.9
  29.9 0.0 copy-start.12
  29.9 0.0 copy-start.16
  29.9 5.3 %collective-permute-start.7 = (bf16[64,512]{1,0:T(8,128)(2,1)S(1)}, bf16[64,512]{1,0:T(8,128)(2,1)S(1)}, u32[]{:S(2)}, u32[]{:S(2)}) collective-permute-start(bf16[64,512]{1,0:T(8,128)(2,1)S(1)} %get-tuple-element.37), channel_id=1, source_target_pairs={{8,16},{24,32},{40,48},{56,64},{72,80},{88,96},{104,112},{120,0},{... | collective-permute-start | bytes 196616 | tf_op jit(solution)/shard_map/ppermute | solution.py:297
  35.1 4.1 %shard_map.191.refs_4_.refs_3_ = bf16[9,512,256]{2,1,0:T(8,128)(2,1)S(1)} custom-call(s32[1,9]{1,0:T(1,128)S(1)} %copy-done.8, s32[9,1,512]{2,1,0:T(1,128)S(1)} %bitcast.29, bf16[1024,512]{1,0:T(8,128)(2,1)S(1)} %copy-done.10, bf16[512,512]{1,0:T(8,128)(2,1)S(1)} %copy-done.11), custom_call_target="tpu_custom_call" | custom-call | flops 2415919104 | tf_op jit(solution)/shard_map/pallas_call | solution.py:332
  39.3 0.4 shard_map.188
  39.6 2.4 %collective-permute-start.9 = (bf16[64,512]{1,0:T(8,128)(2,1)S(1)}, bf16[64,512]{1,0:T(8,128)(2,1)S(1)}, u32[]{:S(2)}, u32[]{:S(2)}) collective-permute-start(bf16[64,512]{1,0:T(8,128)(2,1)S(1)} %shard_map.188), channel_id=1, source_target_pairs={{8,16},{24,32},{40,48},{56,64},{72,80},{88,96},{104,112},{120,0},{... | collective-permute-start | bytes 196616 | tf_op jit(solution)/shard_map/ppermute | solution.py:297
  42.1 4.0 %shard_map.190.refs_3_.refs_2_ = bf16[9,512,256]{2,1,0:T(8,128)(2,1)S(1)} custom-call(s32[1,9]{1,0:T(1,128)S(1)} %copy-done.8, s32[9,1,512]{2,1,0:T(1,128)S(1)} %bitcast.30, bf16[1024,512]{1,0:T(8,128)(2,1)S(1)} %copy-done.9, bf16[512,512]{1,0:T(8,128)(2,1)S(1)} %copy-done.12, f32[1,512]{1,0:T(1,128)S(1)} %bitcast.38), custom_call_target="tpu_custom_call" | custom-call | flops 2415919104 | tf_op jit(solution)/shard_map/pallas_call | solution.py:332
  46.1 0.0 collective-permute-done.9
  46.2 0.0 copy-start.5
  46.2 2.5 %collective-permute-start.11 = (bf16[3,64,512]{2,1,0:T(8,128)(2,1)S(1)}, bf16[3,64,512]{2,1,0:T(8,128)(2,1)S(1)}, u32[]{:S(2)}, u32[]{:S(2)}) collective-permute-start(bf16[3,64,512]{2,1,0:T(8,128)(2,1)S(1)} %pad_maximum_fusion.1.refs_0_), channel_id=1, source_target_pairs={{1,2},{3,4},{5,6},{7,0},{2,1},{4,3},{6,5},{0,7},{9,10},{11,12},{13... | collective-permute-start | bytes 589832 | tf_op jit(solution)/shard_map/ppermute | solution.py:297
  48.7 0.2 collective-permute-start.10
  49.0 4.0 %shard_map.189.refs_2_.refs_1_ = bf16[9,512,256]{2,1,0:T(8,128)(2,1)S(1)} custom-call(s32[1,9]{1,0:T(1,128)S(1)} %copy-done.8, s32[9,1,512]{2,1,0:T(1,128)S(1)} %bitcast.31, bf16[1024,512]{1,0:T(8,128)(2,1)S(1)} %copy-done.9, bf16[512,512]{1,0:T(8,128)(2,1)S(1)} %copy-done.12, f32[1,512]{1,0:T(1,128)S(1)} %bitcast.39), custom_call_target="tpu_custom_call" | custom-call | flops 2415919104 | tf_op jit(solution)/shard_map/pallas_call | solution.py:332
  53.1 4.6 %shard_map.193 = (bf16[3,64,512]{2,1,0:T(8,128)(2,1)S(1)}, bf16[3,64,512]{2,1,0:T(8,128)(2,1)S(1)}, bf16[9,512,512]{2,1,0:T(8,128)(2,1)S(1)}, bf16[9,512,512]{2,1,0:T(8,128)(2,1)S(1)}) custom-call(s32[1,9]{1,0:T(1,128)S(1)} %copy-done.8, s32[2]{0:T(128)S(1)} %pad_add_fusion.flips, s32[9,1,512]{2,1,0:T(1,128)S(1)} %bitcast.23, ...), custom_call_target="tpu_custom_call" | custom-call | flops 805306368 | tf_op jit(solution)/shard_map/pallas_call | solution.py:332
  57.6 1.2 %collective-permute-start.12 = (bf16[3,64,512]{2,1,0:T(8,128)(2,1)S(1)}, bf16[3,64,512]{2,1,0:T(8,128)(2,1)S(1)}, u32[]{:S(2)}, u32[]{:S(2)}) collective-permute-start(bf16[3,64,512]{2,1,0:T(8,128)(2,1)S(1)} %get-tuple-element.42), channel_id=1, source_target_pairs={{0,1},{2,3},{4,5},{6,7},{1,0},{3,2},{5,4},{7,6},{8,9},{10,11},{12,... | collective-permute-start | bytes 589832 | tf_op jit(solution)/shard_map/ppermute | solution.py:297
  58.9 2.7 %shard_map.194 = (bf16[3,64,512]{2,1,0:T(8,128)(2,1)S(1)}, bf16[9,512,512]{2,1,0:T(8,128)(2,1)S(1)}, bf16[9,512,512]{2,1,0:T(8,128)(2,1)S(1)}) custom-call(s32[1,9]{1,0:T(1,128)S(1)} %copy-done.8, s32[2]{0:T(128)S(1)} %pad_add_fusion.flips, s32[9,1,512]{2,1,0:T(1,128)S(1)} %bitcast.24, ...), custom_call_target="tpu_custom_call", output_to_operand_aliasing={{1}: (8, {}), {2}: (9, {})} | custom-call | flops 402653184 | tf_op jit(solution)/shard_map/pallas_call | solution.py:332
  61.6 2.6 %collective-permute-done.13.west = bf16[3,64,512]{2,1,0:T(8,128)(2,1)S(1)} collective-permute-done((bf16[3,64,512]{2,1,0:T(8,128)(2,1)S(1)}, bf16[3,64,512]{2,1,0:T(8,128)(2,1)S(1)}, u32[]{:S(2)}, u32[]{:S(2)}) %collective-permute-start.13) | collective-permute-done | bytes 196640 | tf_op jit(solution)/shard_map/ppermute | solution.py:297
  64.3 0.1 shard_map.197
  64.3 2.6 %collective-permute-start.14 = (bf16[64,512]{1,0:T(8,128)(2,1)S(1)}, bf16[64,512]{1,0:T(8,128)(2,1)S(1)}, u32[]{:S(2)}, u32[]{:S(2)}) collective-permute-start(bf16[64,512]{1,0:T(8,128)(2,1)S(1)} %get-tuple-element.45), channel_id=1, source_target_pairs={{0,8},{16,24},{32,40},{48,56},{64,72},{80,88},{96,104},{112,120},{... | collective-permute-start | bytes 196616 | tf_op jit(solution)/shard_map/ppermute | solution.py:297
  66.9 2.6 %collective-permute-start.15 = (bf16[64,512]{1,0:T(8,128)(2,1)S(1)}, bf16[64,512]{1,0:T(8,128)(2,1)S(1)}, u32[]{:S(2)}, u32[]{:S(2)}) collective-permute-start(bf16[64,512]{1,0:T(8,128)(2,1)S(1)} %get-tuple-element.46), channel_id=1, source_target_pairs={{8,16},{24,32},{40,48},{56,64},{72,80},{88,96},{104,112},{120,0},{... | collective-permute-start | bytes 196616 | tf_op jit(solution)/shard_map/ppermute | solution.py:297
  69.5 3.4 %shard_map.195.lower = bf16[1024,256]{1,0:T(8,128)(2,1)S(1)} custom-call(s32[1,9]{1,0:T(1,128)S(1)} %copy-done.8, s32[9,1,512]{2,1,0:T(1,128)S(1)} %bitcast.32, bf16[9,512,512]{2,1,0:T(8,128)(2,1)S(1)} %get-tuple-element.40.values.messages), custom_call_target="tpu_custom_call" | custom-call | flops 2415919104 | tf_op jit(solution)/shard_map/pallas_call | solution.py:332
  72.9 0.5 collective-permute-done.15.second
  73.4 0.5 shard_map.198
  73.8 2.6 %collective-permute-start.17 = (bf16[64,512]{1,0:T(8,128)(2,1)S(1)}, bf16[64,512]{1,0:T(8,128)(2,1)S(1)}, u32[]{:S(2)}, u32[]{:S(2)}) collective-permute-start(bf16[64,512]{1,0:T(8,128)(2,1)S(1)} %get-tuple-element.47), channel_id=1, source_target_pairs={{8,16},{24,32},{40,48},{56,64},{72,80},{88,96},{104,112},{120,0},{... | collective-permute-start | bytes 196616 | tf_op jit(solution)/shard_map/ppermute | solution.py:297
  76.5 5.1 %shard_map.196 = bf16[1024,512]{1,0:T(8,128)(2,1)} custom-call(s32[1,9]{1,0:T(1,128)S(1)} %copy-done.8, s32[9,1,512]{2,1,0:T(1,128)S(1)} %bitcast.33, bf16[9,512,512]{2,1,0:T(8,128)(2,1)S(1)} %get-tuple-element.40.values.messages, bf16[1024,512]{1,0:T(8,128)(2,1)S(1)} %copy-done.9, bf16[1024,256]{1,0:T(8,128)(2,1)S(1)} %shard_map.195.lower, ...), custom_call_target="tpu_custom_call" | custom-call | flops 2415919104 | tf_op jit(solution)/shard_map/pallas_call | solution.py:332
  81.6 1.6 %collective-permute-start.19 = (bf16[3,64,512]{2,1,0:T(8,128)(2,1)S(1)}, bf16[3,64,512]{2,1,0:T(8,128)(2,1)S(1)}, u32[]{:S(2)}, u32[]{:S(2)}) collective-permute-start(bf16[3,64,512]{2,1,0:T(8,128)(2,1)S(1)} %pad_maximum_fusion.2.refs_0_), channel_id=1, source_target_pairs={{1,2},{3,4},{5,6},{7,0},{2,1},{4,3},{6,5},{0,7},{9,10},{11,12},{13... | collective-permute-start | bytes 589832 | tf_op jit(solution)/shard_map/ppermute | solution.py:297
  83.1 1.0 collective-permute-start.18
  84.2 3.4 %shard_map.203.lower = bf16[1024,256]{1,0:T(8,128)(2,1)S(1)} custom-call(s32[1,9]{1,0:T(1,128)S(1)} %copy-done.8, s32[9,1,512]{2,1,0:T(1,128)S(1)} %bitcast.34, bf16[9,512,512]{2,1,0:T(8,128)(2,1)S(1)} %get-tuple-element.58.values.grads), custom_call_target="tpu_custom_call" | custom-call | flops 2415919104 | tf_op jit(solution)/shard_map/pallas_call | solution.py:332
  87.6 1.9 %shard_map.199 = (bf16[3,64,512]{2,1,0:T(8,128)(2,1)S(1)}, bf16[3,64,512]{2,1,0:T(8,128)(2,1)S(1)}, bf16[9,256,512]{2,1,0:T(8,128)(2,1)S(1)}) custom-call(s32[1,9]{1,0:T(1,128)S(1)} %copy-done.7, s32[2]{0:T(128)S(1)} %pad_add_fusion.flips, s32[9,1,256]{2,1,0:T(1,128)S(1)} %bitcast.21, bf16[3,64,512]{2,1,0:T(8,128)(2,1)S(1)} %collective-permute-done.18.refs_0_, ...), custom_call_target="tpu_custom_call" | custom-call | flops 402653184 | tf_op jit(solution)/shard_map/pallas_call | solution.py:332
  89.5 2.9 %collective-permute-start.20 = (bf16[3,64,512]{2,1,0:T(8,128)(2,1)S(1)}, bf16[3,64,512]{2,1,0:T(8,128)(2,1)S(1)}, u32[]{:S(2)}, u32[]{:S(2)}) collective-permute-start(bf16[3,64,512]{2,1,0:T(8,128)(2,1)S(1)} %get-tuple-element.51), channel_id=1, source_target_pairs={{0,1},{2,3},{4,5},{6,7},{1,0},{3,2},{5,4},{7,6},{8,9},{10,11},{12,... | collective-permute-start | bytes 589832 | tf_op jit(solution)/shard_map/ppermute | solution.py:297
  92.4 4.1 %shard_map.204.partial = f32[1024,512]{1,0:T(8,128)S(1)} custom-call(s32[1,9]{1,0:T(1,128)S(1)} %copy-done.8, s32[9,1,512]{2,1,0:T(1,128)S(1)} %bitcast.35, bf16[9,512,512]{2,1,0:T(8,128)(2,1)S(1)} %get-tuple-element.58.values.grads, bf16[1024,512]{1,0:T(8,128)(2,1)S(1)} %copy-done.10, bf16[1024,256]{1,0:T(8,128)(2,1)S(1)} %shard_map.203.lower, ...), custom_call_target="tpu_custom_call" | custom-call | flops 2415919104 | tf_op jit(solution)/shard_map/pallas_call | solution.py:332
  96.5 0.0 copy-start.13
  96.5 0.0 copy-start.15
  96.5 1.2 %shard_map.200 = (bf16[3,64,512]{2,1,0:T(8,128)(2,1)S(1)}, bf16[9,256,512]{2,1,0:T(8,128)(2,1)S(1)}) custom-call(s32[1,9]{1,0:T(1,128)S(1)} %copy-done.7, s32[2]{0:T(128)S(1)} %pad_add_fusion.flips, s32[9,1,256]{2,1,0:T(1,128)S(1)} %bitcast.22, bf16[3,64,512]{2,1,0:T(8,128)(2,1)S(1)} %pad_maximum_fusion.2.refs_0_, ...), custom_call_target="tpu_custom_call", output_to_operand_aliasing={{1}: (5, {})} | custom-call | flops 201326592 | tf_op jit(solution)/shard_map/pallas_call | solution.py:332
  97.8 0.1 shard_map.201
  97.9 3.8 %collective-permute-start.22 = (bf16[64,512]{1,0:T(8,128)(2,1)S(1)}, bf16[64,512]{1,0:T(8,128)(2,1)S(1)}, u32[]{:S(2)}, u32[]{:S(2)}) collective-permute-start(bf16[64,512]{1,0:T(8,128)(2,1)S(1)} %get-tuple-element.54), channel_id=1, source_target_pairs={{0,8},{16,24},{32,40},{48,56},{64,72},{80,88},{96,104},{112,120},{... | collective-permute-start | bytes 196616 | tf_op jit(solution)/shard_map/ppermute | solution.py:297
  101.7 2.2 %collective-permute-start.23 = (bf16[64,512]{1,0:T(8,128)(2,1)S(1)}, bf16[64,512]{1,0:T(8,128)(2,1)S(1)}, u32[]{:S(2)}, u32[]{:S(2)}) collective-permute-start(bf16[64,512]{1,0:T(8,128)(2,1)S(1)} %get-tuple-element.55), channel_id=1, source_target_pairs={{8,16},{24,32},{40,48},{56,64},{72,80},{88,96},{104,112},{120,0},{... | collective-permute-start | bytes 196616 | tf_op jit(solution)/shard_map/ppermute | solution.py:297
  104.0 4.5 %shard_map.205 = bf16[1024,512]{1,0:T(8,128)(2,1)} custom-call(s32[1,9]{1,0:T(1,128)S(1)} %copy-done.7, s32[9,1,256]{2,1,0:T(1,128)S(1)} %bitcast.37, bf16[9,256,512]{2,1,0:T(8,128)(2,1)S(1)} %get-tuple-element.57.grads, f32[1024,512]{1,0:T(8,128)S(1)} %shard_map.204.partial, bf16[512,512]{1,0:T(8,128)(2,1)S(1)} %copy-done.13), custom_call_target="tpu_custom_call" | custom-call | flops 2415919104 | tf_op jit(solution)/shard_map/pallas_call | solution.py:332
  108.5 0.0 collective-permute-done.23.second
  108.5 0.9 shard_map.202
  (44 shorter events, 0.1 us)
Async XLA Ops:
  0.6 7.6 %collective-permute-start = (bf16[64,512]{1,0:T(8,128)(2,1)}, bf16[64,512]{1,0:T(8,128)(2,1)S(1)}, u32[]{:S(2)}, u32[]{:S(2)}) collective-permute-start(bf16[64,512]{1,0:T(8,128)(2,1)} %feat.6), channel_id=1, source_target_pairs={{0,8},{16,24},{32,40},{48,56},{64,72},{80,88},{96,104},{112,120},{... | collective-permute-start | bytes 196616 | tf_op jit(solution)/shard_map/ppermute | solution.py:297
  2.8 7.3 %collective-permute-start.1 = (bf16[64,512]{1,0:T(8,128)(2,1)}, bf16[64,512]{1,0:T(8,128)(2,1)S(1)}, u32[]{:S(2)}, u32[]{:S(2)}) collective-permute-start(bf16[64,512]{1,0:T(8,128)(2,1)} %feat.6), channel_id=1, source_target_pairs={{8,16},{24,32},{40,48},{56,64},{72,80},{88,96},{104,112},{120,0},{... | collective-permute-start | bytes 196616 | tf_op jit(solution)/shard_map/ppermute | solution.py:297
  11.0 8.3 %collective-permute-start.3 = (bf16[3,64,512]{2,1,0:T(8,128)(2,1)S(1)}, bf16[3,64,512]{2,1,0:T(8,128)(2,1)S(1)}, u32[]{:S(2)}, u32[]{:S(2)}) collective-permute-start(bf16[3,64,512]{2,1,0:T(8,128)(2,1)S(1)} %pad_maximum_fusion.refs_0_), channel_id=1, source_target_pairs={{1,2},{3,4},{5,6},{7,0},{2,1},{4,3},{6,5},{0,7},{9,10},{11,12},{13... | collective-permute-start | bytes 589832 | tf_op jit(solution)/shard_map/ppermute | solution.py:297
  14.0 5.3 %collective-permute-start.2 = (bf16[3,64,512]{2,1,0:T(8,128)(2,1)S(1)}, bf16[3,64,512]{2,1,0:T(8,128)(2,1)S(1)}, u32[]{:S(2)}, u32[]{:S(2)}) collective-permute-start(bf16[3,64,512]{2,1,0:T(8,128)(2,1)S(1)} %pad_maximum_fusion.refs_0_), channel_id=1, source_target_pairs={{0,1},{2,3},{4,5},{6,7},{1,0},{3,2},{5,4},{7,6},{8,9},{10,11},{12,... | collective-permute-start | bytes 589832 | tf_op jit(solution)/shard_map/ppermute | solution.py:297
  14.0 5.3 %copy-start = (bf16[512,512]{1,0:T(8,128)(2,1)S(1)}, bf16[512,512]{1,0:T(8,128)(2,1)}, u32[]{:S(2)}) copy-start(bf16[512,512]{1,0:T(8,128)(2,1)} %weight.19) | copy-start | bytes 1572868
  14.0 5.3 %copy-start.4 = (s32[1,9,256]{2,0,1:T(1,128)S(1)}, s32[1,9,256]{2,0,1:T(1,128)}, u32[]{:S(2)}) copy-start(s32[1,9,256]{2,0,1:T(1,128)} %param.20) | copy-start | bytes 27652
  14.0 5.3 %copy-start.6 = (f32[512]{0:T(512)S(1)}, f32[512]{0:T(512)}, u32[]{:S(2)}) copy-start(f32[512]{0:T(512)} %param.27) | copy-start | bytes 6148
  14.0 5.3 %copy-start.7 = (s32[1,9]{1,0:T(1,128)S(1)}, s32[1,9]{1,0:T(1,128)}, u32[]{:S(2)}) copy-start(s32[1,9]{1,0:T(1,128)} %counts.31) | copy-start | bytes 112
  19.2 4.6 %copy-start.8 = (s32[1,9]{1,0:T(1,128)S(1)}, s32[1,9]{1,0:T(1,128)}, u32[]{:S(2)}) copy-start(s32[1,9]{1,0:T(1,128)} %counts.30) | copy-start | bytes 112
  19.2 4.6 %copy-start.10 = (bf16[1024,512]{1,0:T(8,128)(2,1)S(1)}, bf16[1024,512]{1,0:T(8,128)(2,1)}, u32[]{:S(2)}) copy-start(bf16[1024,512]{1,0:T(8,128)(2,1)} %cot.5) | copy-start | bytes 3145732
  19.2 4.6 %copy-start.11 = (bf16[512,512]{1,0:T(8,128)(2,1)S(1)}, bf16[512,512]{1,0:T(8,128)(2,1)}, u32[]{:S(2)}) copy-start(bf16[512,512]{1,0:T(8,128)(2,1)} %weight.17) | copy-start | bytes 1572868
  19.2 4.6 %copy-start.14 = (s32[1,9,512]{2,0,1:T(1,128)S(1)}, s32[1,9,512]{2,0,1:T(1,128)}, u32[]{:S(2)}) copy-start(s32[1,9,512]{2,0,1:T(1,128)} %param.23) | copy-start | bytes 55300
  22.0 7.6 %collective-permute-start.4 = (bf16[3,64,512]{2,1,0:T(8,128)(2,1)S(1)}, bf16[3,64,512]{2,1,0:T(8,128)(2,1)S(1)}, u32[]{:S(2)}, u32[]{:S(2)}) collective-permute-start(bf16[3,64,512]{2,1,0:T(8,128)(2,1)S(1)} %get-tuple-element.33), channel_id=1, source_target_pairs={{0,1},{2,3},{4,5},{6,7},{1,0},{3,2},{5,4},{7,6},{8,9},{10,11},{12,... | collective-permute-start | bytes 589832 | tf_op jit(solution)/shard_map/ppermute | solution.py:297
  22.6 7.0 %collective-permute-start.5 = (bf16[3,64,512]{2,1,0:T(8,128)(2,1)S(1)}, bf16[3,64,512]{2,1,0:T(8,128)(2,1)S(1)}, u32[]{:S(2)}, u32[]{:S(2)}) collective-permute-start(bf16[3,64,512]{2,1,0:T(8,128)(2,1)S(1)} %get-tuple-element.34), channel_id=1, source_target_pairs={{1,2},{3,4},{5,6},{7,0},{2,1},{4,3},{6,5},{0,7},{9,10},{11,12},{13... | collective-permute-start | bytes 589832 | tf_op jit(solution)/shard_map/ppermute | solution.py:297
  29.7 9.5 %collective-permute-start.6 = (bf16[64,512]{1,0:T(8,128)(2,1)S(1)}, bf16[64,512]{1,0:T(8,128)(2,1)S(1)}, u32[]{:S(2)}, u32[]{:S(2)}) collective-permute-start(bf16[64,512]{1,0:T(8,128)(2,1)S(1)} %get-tuple-element.36), channel_id=1, source_target_pairs={{0,8},{16,24},{32,40},{48,56},{64,72},{80,88},{96,104},{112,120},{... | collective-permute-start | bytes 196616 | tf_op jit(solution)/shard_map/ppermute | solution.py:297
  29.8 9.4 %copy-start.1 = (bf16[512,512]{1,0:T(8,128)(2,1)S(1)}, bf16[512,512]{1,0:T(8,128)(2,1)}, u32[]{:S(2)}) copy-start(bf16[512,512]{1,0:T(8,128)(2,1)} %out_weight.3) | copy-start | bytes 1572868
  29.8 9.4 %copy-start.2 = (bf16[512,512]{1,0:T(8,128)(2,1)S(1)}, bf16[512,512]{1,0:T(8,128)(2,1)}, u32[]{:S(2)}) copy-start(bf16[512,512]{1,0:T(8,128)(2,1)} %weight.18) | copy-start | bytes 1572868
  29.8 9.4 %copy-start.3 = (bf16[64,512]{1,0:T(8,128)(2,1)S(1)}, bf16[64,512]{1,0:T(8,128)(2,1)}, u32[]{:S(2)}) copy-start(bf16[64,512]{1,0:T(8,128)(2,1)} %feat.6) | copy-start | bytes 196612
  29.8 12.2 %copy-start.9 = (bf16[1024,512]{1,0:T(8,128)(2,1)S(1)}, bf16[1024,512]{1,0:T(8,128)(2,1)}, u32[]{:S(2)}) copy-start(bf16[1024,512]{1,0:T(8,128)(2,1)} %feat.9) | copy-start | bytes 3145732
  29.9 12.2 %copy-start.12 = (bf16[512,512]{1,0:T(8,128)(2,1)S(1)}, bf16[512,512]{1,0:T(8,128)(2,1)}, u32[]{:S(2)}) copy-start(bf16[512,512]{1,0:T(8,128)(2,1)} %weight.20) | copy-start | bytes 1572868
  29.9 12.2 %copy-start.16 = (f32[512]{0:T(512)S(1)}, f32[512]{0:T(512)}, u32[]{:S(2)}) copy-start(f32[512]{0:T(512)} %param.31) | copy-start | bytes 6148
  29.9 9.3 %collective-permute-start.7 = (bf16[64,512]{1,0:T(8,128)(2,1)S(1)}, bf16[64,512]{1,0:T(8,128)(2,1)S(1)}, u32[]{:S(2)}, u32[]{:S(2)}) collective-permute-start(bf16[64,512]{1,0:T(8,128)(2,1)S(1)} %get-tuple-element.37), channel_id=1, source_target_pairs={{8,16},{24,32},{40,48},{56,64},{72,80},{88,96},{104,112},{120,0},{... | collective-permute-start | bytes 196616 | tf_op jit(solution)/shard_map/ppermute | solution.py:297
  39.6 6.5 %collective-permute-start.9 = (bf16[64,512]{1,0:T(8,128)(2,1)S(1)}, bf16[64,512]{1,0:T(8,128)(2,1)S(1)}, u32[]{:S(2)}, u32[]{:S(2)}) collective-permute-start(bf16[64,512]{1,0:T(8,128)(2,1)S(1)} %shard_map.188), channel_id=1, source_target_pairs={{8,16},{24,32},{40,48},{56,64},{72,80},{88,96},{104,112},{120,0},{... | collective-permute-start | bytes 196616 | tf_op jit(solution)/shard_map/ppermute | solution.py:297
  42.0 4.1 %collective-permute-start.8 = (bf16[64,512]{1,0:T(8,128)(2,1)S(1)}, bf16[64,512]{1,0:T(8,128)(2,1)S(1)}, u32[]{:S(2)}, u32[]{:S(2)}) collective-permute-start(bf16[64,512]{1,0:T(8,128)(2,1)S(1)} %shard_map.188), channel_id=1, source_target_pairs={{0,8},{16,24},{32,40},{48,56},{64,72},{80,88},{96,104},{112,120},{... | collective-permute-start | bytes 196616 | tf_op jit(solution)/shard_map/ppermute | solution.py:297
  46.2 6.9 %copy-start.5 = (s32[1,9,512]{2,0,1:T(1,128)S(1)}, s32[1,9,512]{2,0,1:T(1,128)}, u32[]{:S(2)}) copy-start(s32[1,9,512]{2,0,1:T(1,128)} %param.22) | copy-start | bytes 55300
  46.2 6.8 %collective-permute-start.11 = (bf16[3,64,512]{2,1,0:T(8,128)(2,1)S(1)}, bf16[3,64,512]{2,1,0:T(8,128)(2,1)S(1)}, u32[]{:S(2)}, u32[]{:S(2)}) collective-permute-start(bf16[3,64,512]{2,1,0:T(8,128)(2,1)S(1)} %pad_maximum_fusion.1.refs_0_), channel_id=1, source_target_pairs={{1,2},{3,4},{5,6},{7,0},{2,1},{4,3},{6,5},{0,7},{9,10},{11,12},{13... | collective-permute-start | bytes 589832 | tf_op jit(solution)/shard_map/ppermute | solution.py:297
  48.7 4.3 %collective-permute-start.10 = (bf16[3,64,512]{2,1,0:T(8,128)(2,1)S(1)}, bf16[3,64,512]{2,1,0:T(8,128)(2,1)S(1)}, u32[]{:S(2)}, u32[]{:S(2)}) collective-permute-start(bf16[3,64,512]{2,1,0:T(8,128)(2,1)S(1)} %pad_maximum_fusion.1.refs_0_), channel_id=1, source_target_pairs={{0,1},{2,3},{4,5},{6,7},{1,0},{3,2},{5,4},{7,6},{8,9},{10,11},{12,... | collective-permute-start | bytes 589832 | tf_op jit(solution)/shard_map/ppermute | solution.py:297
  57.6 4.0 %collective-permute-start.12 = (bf16[3,64,512]{2,1,0:T(8,128)(2,1)S(1)}, bf16[3,64,512]{2,1,0:T(8,128)(2,1)S(1)}, u32[]{:S(2)}, u32[]{:S(2)}) collective-permute-start(bf16[3,64,512]{2,1,0:T(8,128)(2,1)S(1)} %get-tuple-element.42), channel_id=1, source_target_pairs={{0,1},{2,3},{4,5},{6,7},{1,0},{3,2},{5,4},{7,6},{8,9},{10,11},{12,... | collective-permute-start | bytes 589832 | tf_op jit(solution)/shard_map/ppermute | solution.py:297
  58.9 5.4 %collective-permute-start.13 = (bf16[3,64,512]{2,1,0:T(8,128)(2,1)S(1)}, bf16[3,64,512]{2,1,0:T(8,128)(2,1)S(1)}, u32[]{:S(2)}, u32[]{:S(2)}) collective-permute-start(bf16[3,64,512]{2,1,0:T(8,128)(2,1)S(1)} %get-tuple-element.43), channel_id=1, source_target_pairs={{1,2},{3,4},{5,6},{7,0},{2,1},{4,3},{6,5},{0,7},{9,10},{11,12},{13... | collective-permute-start | bytes 589832 | tf_op jit(solution)/shard_map/ppermute | solution.py:297
  64.3 8.6 %collective-permute-start.14 = (bf16[64,512]{1,0:T(8,128)(2,1)S(1)}, bf16[64,512]{1,0:T(8,128)(2,1)S(1)}, u32[]{:S(2)}, u32[]{:S(2)}) collective-permute-start(bf16[64,512]{1,0:T(8,128)(2,1)S(1)} %get-tuple-element.45), channel_id=1, source_target_pairs={{0,8},{16,24},{32,40},{48,56},{64,72},{80,88},{96,104},{112,120},{... | collective-permute-start | bytes 196616 | tf_op jit(solution)/shard_map/ppermute | solution.py:297
  66.9 6.4 %collective-permute-start.15 = (bf16[64,512]{1,0:T(8,128)(2,1)S(1)}, bf16[64,512]{1,0:T(8,128)(2,1)S(1)}, u32[]{:S(2)}, u32[]{:S(2)}) collective-permute-start(bf16[64,512]{1,0:T(8,128)(2,1)S(1)} %get-tuple-element.46), channel_id=1, source_target_pairs={{8,16},{24,32},{40,48},{56,64},{72,80},{88,96},{104,112},{120,0},{... | collective-permute-start | bytes 196616 | tf_op jit(solution)/shard_map/ppermute | solution.py:297
  73.8 7.7 %collective-permute-start.17 = (bf16[64,512]{1,0:T(8,128)(2,1)S(1)}, bf16[64,512]{1,0:T(8,128)(2,1)S(1)}, u32[]{:S(2)}, u32[]{:S(2)}) collective-permute-start(bf16[64,512]{1,0:T(8,128)(2,1)S(1)} %get-tuple-element.47), channel_id=1, source_target_pairs={{8,16},{24,32},{40,48},{56,64},{72,80},{88,96},{104,112},{120,0},{... | collective-permute-start | bytes 196616 | tf_op jit(solution)/shard_map/ppermute | solution.py:297
  76.5 5.1 %collective-permute-start.16 = (bf16[64,512]{1,0:T(8,128)(2,1)S(1)}, bf16[64,512]{1,0:T(8,128)(2,1)S(1)}, u32[]{:S(2)}, u32[]{:S(2)}) collective-permute-start(bf16[64,512]{1,0:T(8,128)(2,1)S(1)} %get-tuple-element.47), channel_id=1, source_target_pairs={{0,8},{16,24},{32,40},{48,56},{64,72},{80,88},{96,104},{112,120},{... | collective-permute-start | bytes 196616 | tf_op jit(solution)/shard_map/ppermute | solution.py:297
  81.6 6.0 %collective-permute-start.19 = (bf16[3,64,512]{2,1,0:T(8,128)(2,1)S(1)}, bf16[3,64,512]{2,1,0:T(8,128)(2,1)S(1)}, u32[]{:S(2)}, u32[]{:S(2)}) collective-permute-start(bf16[3,64,512]{2,1,0:T(8,128)(2,1)S(1)} %pad_maximum_fusion.2.refs_0_), channel_id=1, source_target_pairs={{1,2},{3,4},{5,6},{7,0},{2,1},{4,3},{6,5},{0,7},{9,10},{11,12},{13... | collective-permute-start | bytes 589832 | tf_op jit(solution)/shard_map/ppermute | solution.py:297
  83.1 4.4 %collective-permute-start.18 = (bf16[3,64,512]{2,1,0:T(8,128)(2,1)S(1)}, bf16[3,64,512]{2,1,0:T(8,128)(2,1)S(1)}, u32[]{:S(2)}, u32[]{:S(2)}) collective-permute-start(bf16[3,64,512]{2,1,0:T(8,128)(2,1)S(1)} %pad_maximum_fusion.2.refs_0_), channel_id=1, source_target_pairs={{0,1},{2,3},{4,5},{6,7},{1,0},{3,2},{5,4},{7,6},{8,9},{10,11},{12,... | collective-permute-start | bytes 589832 | tf_op jit(solution)/shard_map/ppermute | solution.py:297
  89.5 8.3 %collective-permute-start.20 = (bf16[3,64,512]{2,1,0:T(8,128)(2,1)S(1)}, bf16[3,64,512]{2,1,0:T(8,128)(2,1)S(1)}, u32[]{:S(2)}, u32[]{:S(2)}) collective-permute-start(bf16[3,64,512]{2,1,0:T(8,128)(2,1)S(1)} %get-tuple-element.51), channel_id=1, source_target_pairs={{0,1},{2,3},{4,5},{6,7},{1,0},{3,2},{5,4},{7,6},{8,9},{10,11},{12,... | collective-permute-start | bytes 589832 | tf_op jit(solution)/shard_map/ppermute | solution.py:297
  92.4 5.4 %collective-permute-start.21 = (bf16[3,64,512]{2,1,0:T(8,128)(2,1)S(1)}, bf16[3,64,512]{2,1,0:T(8,128)(2,1)S(1)}, u32[]{:S(2)}, u32[]{:S(2)}) collective-permute-start(bf16[3,64,512]{2,1,0:T(8,128)(2,1)S(1)} %get-tuple-element.52), channel_id=1, source_target_pairs={{1,2},{3,4},{5,6},{7,0},{2,1},{4,3},{6,5},{0,7},{9,10},{11,12},{13... | collective-permute-start | bytes 589832 | tf_op jit(solution)/shard_map/ppermute | solution.py:297
  96.5 7.4 %copy-start.13 = (bf16[512,512]{1,0:T(8,128)(2,1)S(1)}, bf16[512,512]{1,0:T(8,128)(2,1)}, u32[]{:S(2)}) copy-start(bf16[512,512]{1,0:T(8,128)(2,1)} %weight.21) | copy-start | bytes 1572868
  96.5 7.4 %copy-start.15 = (s32[1,9,256]{2,0,1:T(1,128)S(1)}, s32[1,9,256]{2,0,1:T(1,128)}, u32[]{:S(2)}) copy-start(s32[1,9,256]{2,0,1:T(1,128)} %param.19) | copy-start | bytes 27652
  97.9 10.6 %collective-permute-start.22 = (bf16[64,512]{1,0:T(8,128)(2,1)S(1)}, bf16[64,512]{1,0:T(8,128)(2,1)S(1)}, u32[]{:S(2)}, u32[]{:S(2)}) collective-permute-start(bf16[64,512]{1,0:T(8,128)(2,1)S(1)} %get-tuple-element.54), channel_id=1, source_target_pairs={{0,8},{16,24},{32,40},{48,56},{64,72},{80,88},{96,104},{112,120},{... | collective-permute-start | bytes 196616 | tf_op jit(solution)/shard_map/ppermute | solution.py:297
  101.7 6.8 %collective-permute-start.23 = (bf16[64,512]{1,0:T(8,128)(2,1)S(1)}, bf16[64,512]{1,0:T(8,128)(2,1)S(1)}, u32[]{:S(2)}, u32[]{:S(2)}) collective-permute-start(bf16[64,512]{1,0:T(8,128)(2,1)S(1)} %get-tuple-element.55), channel_id=1, source_target_pairs={{8,16},{24,32},{40,48},{56,64},{72,80},{88,96},{104,112},{120,0},{... | collective-permute-start | bytes 196616 | tf_op jit(solution)/shard_map/ppermute | solution.py:297

commit v5 on v4

--- a/solution.py
+++ b/solution.py
@@ -226,9 +226,11 @@
     edge_groups(counts, recv, flips, near, total, outs, chunk_list, edges)
 
 
-def scatter_slots(counts, index_ref, values, total, chunk_list, cols=slice(None)):
-    groups = list_chunks(counts, index_ref.shape[2], *chunk_list)
-    total[...] = jnp.zeros(total.shape, F32)
+def scatter_slots(
+    counts, index_ref, values, total, chunk_list, cols=slice(None), blocks=range(9), first=None
+):
+    groups = list_chunks(counts, index_ref.shape[2], *chunk_list, blocks=blocks)
+    total[...] = jnp.zeros(total.shape, F32) if first is None else first[...]
 
     def body(chunks):
         hots = [scatter_hot(rows_of(index_ref, c), total.shape[0], c[2]) for c in chunks]
@@ -252,18 +254,18 @@
     out[...] = (feat[...].astype(F32) + update).astype(BF16)
 
 
-def dec_grid_kernel(
-    cols, counts, recv, grads, cot, lower, weight, out, total, *chunk_list
-):
-    scatter_slots(counts, recv, grads, total, chunk_list, cols)
-    half = lower.shape[1]
-    back = mm_nt(lower[...], weight[:, :half])
-    back += mm_nt(total[...].astype(BF16), weight[:, half:])
-    out[...] = cot[...].astype(F32) + back
-
-
-def grid_grad_kernel(counts, send, grads, partial, weight, out, total, *chunk_list):
-    scatter_slots(counts, send, grads, total, chunk_list)
+def dec_grid_kernel(counts, recv, grads, cot, weight, out, total, *chunk_list):
+    scatter_slots(counts, recv, grads, total, chunk_list)
+    out[...] = cot[...].astype(F32) + mm_nt(total[...].astype(BF16), weight[...])
+
+
+def partner_total_kernel(counts, send, grads, out, *chunk_list):
+    partners = [k for k in range(9) if k % 3 != 1]
+    scatter_slots(counts, send, grads, out, chunk_list, blocks=partners)
+
+
+def grid_grad_kernel(counts, send, grads, first, partial, weight, out, total, *chunk_list):
+    scatter_slots(counts, send, grads, total, chunk_list, blocks=(1, 4, 7), first=first)
     back = mm_nt(total[...].astype(BF16), weight[...])
     out[...] = (partial[...] + back).astype(BF16)
 
@@ -359,6 +361,8 @@
     near = (mesh_rows, width), BF16
     near_split = (2 * mesh_rows, width), BF16
     near_total = (mesh_rows, width), F32
+    exact_grid = [pltpu.VMEM((grid_rows, width), F32)] + chunk_list
+    exact_tile_grid = [jax.ShapeDtypeStruct((grid_rows, width), F32)]
     enc_work = 2 * grid_rows * width * 9 * cap_e
     dec_work = 2 * grid_rows * width * 9 * cap_d
 
@@ -442,14 +446,9 @@
         functools.partial(grid_new_kernel, upper), grid_tile, exact_half,
         dec_count, dec_recv, messages, grid_feat, sum_lower, dec_out, work=dec_work // 2,
     )
-    (local_lower,) = kernel(
-        functools.partial(scatter_kernel, lower), half_grid, exact_half,
-        dec_count, dec_recv, dec_grads, work=dec_work // 2,
-    )
     (dec_grid,) = kernel(
-        functools.partial(dec_grid_kernel, upper),
-        [jax.ShapeDtypeStruct((grid_rows, width), F32)], exact_half,
-        dec_count, dec_recv, dec_grads, grid_cot, local_lower, dec_dst, work=dec_work // 2,
+        dec_grid_kernel, exact_tile_grid, exact_grid,
+        dec_count, dec_recv, dec_grads, grid_cot, dec_dst, work=dec_work,
     )
 
     grad_partial, (grads,) = edges(
@@ -461,10 +460,13 @@
         *fold(*grad_partial), mesh_back, enc_dst, smem=0,
     )
 
+    (partner_total,) = kernel(
+        partner_total_kernel, exact_tile_grid, chunk_list,
+        enc_count, enc_send, grads, work=2 * enc_work // 3,
+    )
     (grid_grad,) = kernel(
-        grid_grad_kernel, grid_tile,
-        [pltpu.VMEM((grid_rows, width), F32)] + chunk_list,
-        enc_count, enc_send, grads, dec_grid, enc_src, work=enc_work,
+        grid_grad_kernel, grid_tile, exact_grid,
+        enc_count, enc_send, grads, partner_total, dec_grid, enc_src, work=enc_work // 3,
     )
     return grid_new, mesh_grad, grid_grad
 

time: 110 us -> 114 us (1.036)
  waiting for transfers between devices: 5.06 us -> 8.53 us
  Pallas kernels: 58.8 us -> 57.6 us
    ppermute x24, waiting for transfers between devices: 5.06 us -> 8.53 us  [along(): return lambda value: lax.ppermute(value, axis, pairs)]
    pallas_call x22, Pallas kernels: 58.8 us -> 57.6 us  [kernel(): pl.pallas_call(body, out_shape=outs, in_specs=specs or [SMEM] * smem + [V...]
  transfers between devices with their start and end apart: 24 -> 24, of which waited for: 3 -> 4; matrix products, arithmetic and copies ran while one was open for 0% -> 0% of each run, Pallas kernels for 43% -> 41%
where the time goes in v5:
time: 114 us; the launch traced here: 113 us
  Pallas kernels  57.6 us (51%)
  starting transfers between devices  44.4 us (39%)
  waiting for transfers between devices  8.53 us (7%)
    pallas_call x22, Pallas kernels, kernel(): pl.pallas_call(body, out_shape=outs, in_specs=specs or [SMEM] * smem + [V...  57.6 us
    ppermute x24, starting transfers between devices, along(): return lambda value: lax.ppermute(value, axis, pairs)  44.4 us
    ppermute x24, waiting for transfers between devices, along(): return lambda value: lax.ppermute(value, axis, pairs)  8.53 us
  transfers between devices with their start and end apart: 24, of which 4 were waited for; matrix products, arithmetic and copies ran while one was open for 0% of the time, Pallas kernels for 41%

profile of v5, /device:TPU:1, one launch (start us, length us, event | category | flops | bytes accessed | tf_op | source)
XLA Modules:
  0.0 112.8 jit_solution(10466950140939878141)
XLA Ops:
  0.6 2.2 %collective-permute-start = (bf16[64,512]{1,0:T(8,128)(2,1)}, bf16[64,512]{1,0:T(8,128)(2,1)S(1)}, u32[]{:S(2)}, u32[]{:S(2)}) collective-permute-start(bf16[64,512]{1,0:T(8,128)(2,1)} %feat.6), channel_id=1, source_target_pairs={{0,8},{16,24},{32,40},{48,56},{64,72},{80,88},{96,104},{112,120},{... | collective-permute-start | bytes 196616 | tf_op jit(solution)/shard_map/ppermute | solution.py:299
  2.8 5.4 %collective-permute-start.1 = (bf16[64,512]{1,0:T(8,128)(2,1)}, bf16[64,512]{1,0:T(8,128)(2,1)S(1)}, u32[]{:S(2)}, u32[]{:S(2)}) collective-permute-start(bf16[64,512]{1,0:T(8,128)(2,1)} %feat.6), channel_id=1, source_target_pairs={{8,16},{24,32},{40,48},{56,64},{72,80},{88,96},{104,112},{120,0},{... | collective-permute-start | bytes 196616 | tf_op jit(solution)/shard_map/ppermute | solution.py:299
  8.2 0.1 pad_add_fusion.flips
  8.3 1.8 %collective-permute-done.1 = bf16[64,512]{1,0:T(8,128)(2,1)S(1)} collective-permute-done((bf16[64,512]{1,0:T(8,128)(2,1)}, bf16[64,512]{1,0:T(8,128)(2,1)S(1)}, u32[]{:S(2)}, u32[]{:S(2)}) %collective-permute-start.1) | collective-permute-done | bytes 65568 | tf_op jit(solution)/shard_map/ppermute | solution.py:299
  10.1 0.9 pad_maximum_fusion.refs_0_
  11.0 3.0 %collective-permute-start.3 = (bf16[3,64,512]{2,1,0:T(8,128)(2,1)S(1)}, bf16[3,64,512]{2,1,0:T(8,128)(2,1)S(1)}, u32[]{:S(2)}, u32[]{:S(2)}) collective-permute-start(bf16[3,64,512]{2,1,0:T(8,128)(2,1)S(1)} %pad_maximum_fusion.refs_0_), channel_id=1, source_target_pairs={{1,2},{3,4},{5,6},{7,0},{2,1},{4,3},{6,5},{0,7},{9,10},{11,12},{13... | collective-permute-start | bytes 589832 | tf_op jit(solution)/shard_map/ppermute | solution.py:299
  14.0 0.0 copy-start.9
  14.0 5.2 %shard_map.184.refs_4_.refs_3_ = bf16[9,256,512]{2,1,0:T(8,128)(2,1)S(1)} custom-call(s32[1,9]{1,0:T(1,128)} %counts.31, s32[9,1,256]{2,1,0:T(1,128)} %bitcast.26, bf16[1024,512]{1,0:T(8,128)(2,1)} %feat.9, bf16[512,512]{1,0:T(8,128)(2,1)} %weight.21), custom_call_target="tpu_custom_call" | custom-call | flops 2415919104 | tf_op jit(solution)/shard_map/pallas_call | solution.py:334
  19.2 0.0 copy-start.10
  19.2 0.0 copy-start.11
  19.2 0.0 copy-start.14
  19.2 0.0 copy-start.15
  19.2 0.0 collective-permute-done.3.refs_1_
  19.3 2.7 %shard_map.185 = (bf16[3,64,512]{2,1,0:T(8,128)(2,1)S(1)}, bf16[3,64,512]{2,1,0:T(8,128)(2,1)S(1)}, bf16[9,256,512]{2,1,0:T(8,128)(2,1)S(1)}) custom-call(s32[1,9]{1,0:T(1,128)S(1)} %copy-done.7, s32[2]{0:T(128)S(1)} %pad_add_fusion.flips, s32[9,1,256]{2,1,0:T(1,128)S(1)} %bitcast.19, bf16[3,64,512]{2,1,0:T(8,128)(2,1)S(1)} %collective-permute-done.2.refs_0_, ...), custom_call_target="tpu_custom_call" | custom-call | flops 402653184 | tf_op jit(solution)/shard_map/pallas_call | solution.py:334
  22.0 0.6 collective-permute-start.4
  22.6 1.2 %collective-permute-start.5 = (bf16[3,64,512]{2,1,0:T(8,128)(2,1)S(1)}, bf16[3,64,512]{2,1,0:T(8,128)(2,1)S(1)}, u32[]{:S(2)}, u32[]{:S(2)}) collective-permute-start(bf16[3,64,512]{2,1,0:T(8,128)(2,1)S(1)} %get-tuple-element.34), channel_id=1, source_target_pairs={{1,2},{3,4},{5,6},{7,0},{2,1},{4,3},{6,5},{0,7},{9,10},{11,12},{13... | collective-permute-start | bytes 589832 | tf_op jit(solution)/shard_map/ppermute | solution.py:299
  23.8 4.1 %shard_map.192.refs_5_.refs_4_ = bf16[9,512,256]{2,1,0:T(8,128)(2,1)S(1)} custom-call(s32[1,9]{1,0:T(1,128)S(1)} %copy-done.10, s32[9,1,512]{2,1,0:T(1,128)S(1)} %bitcast.31, bf16[1024,512]{1,0:T(8,128)(2,1)S(1)} %copy-done.11, bf16[512,512]{1,0:T(8,128)(2,1)S(1)} %copy-done.14), custom_call_target="tpu_custom_call" | custom-call | flops 2415919104 | tf_op jit(solution)/shard_map/pallas_call | solution.py:334
  27.9 1.7 %shard_map.186 = (bf16[3,64,512]{2,1,0:T(8,128)(2,1)S(1)}, bf16[9,256,512]{2,1,0:T(8,128)(2,1)S(1)}) custom-call(s32[1,9]{1,0:T(1,128)S(1)} %copy-done.7, s32[2]{0:T(128)S(1)} %pad_add_fusion.flips, s32[9,1,256]{2,1,0:T(1,128)S(1)} %bitcast.20, bf16[3,64,512]{2,1,0:T(8,128)(2,1)S(1)} %pad_maximum_fusion.refs_0_, ...), custom_call_target="tpu_custom_call", output_to_operand_aliasing={{1}: (7, {})} | custom-call | flops 201326592 | tf_op jit(solution)/shard_map/pallas_call | solution.py:334
  29.6 0.0 collective-permute-done.4.east
  29.6 0.1 shard_map.187
  29.7 0.1 collective-permute-start.6
  29.8 0.0 copy-start.1
  29.8 0.0 copy-start.2
  29.8 0.0 copy-start.4
  29.8 0.0 copy-start.12
  29.9 0.0 copy-start.13
  29.9 0.0 copy-start.16
  29.9 5.3 %collective-permute-start.7 = (bf16[64,512]{1,0:T(8,128)(2,1)S(1)}, bf16[64,512]{1,0:T(8,128)(2,1)S(1)}, u32[]{:S(2)}, u32[]{:S(2)}) collective-permute-start(bf16[64,512]{1,0:T(8,128)(2,1)S(1)} %get-tuple-element.37), channel_id=1, source_target_pairs={{8,16},{24,32},{40,48},{56,64},{72,80},{88,96},{104,112},{120,0},{... | collective-permute-start | bytes 196616 | tf_op jit(solution)/shard_map/ppermute | solution.py:299
  35.1 4.1 %shard_map.191.refs_4_.refs_3_ = bf16[9,512,256]{2,1,0:T(8,128)(2,1)S(1)} custom-call(s32[1,9]{1,0:T(1,128)S(1)} %copy-done.10, s32[9,1,512]{2,1,0:T(1,128)S(1)} %bitcast.32, bf16[1024,512]{1,0:T(8,128)(2,1)S(1)} %copy-done.11, bf16[512,512]{1,0:T(8,128)(2,1)S(1)} %copy-done.14), custom_call_target="tpu_custom_call" | custom-call | flops 2415919104 | tf_op jit(solution)/shard_map/pallas_call | solution.py:334
  39.2 0.0 collective-permute-done.6.first
  39.3 0.4 shard_map.188
  39.6 2.4 %collective-permute-start.9 = (bf16[64,512]{1,0:T(8,128)(2,1)S(1)}, bf16[64,512]{1,0:T(8,128)(2,1)S(1)}, u32[]{:S(2)}, u32[]{:S(2)}) collective-permute-start(bf16[64,512]{1,0:T(8,128)(2,1)S(1)} %shard_map.188), channel_id=1, source_target_pairs={{8,16},{24,32},{40,48},{56,64},{72,80},{88,96},{104,112},{120,0},{... | collective-permute-start | bytes 196616 | tf_op jit(solution)/shard_map/ppermute | solution.py:299
  42.1 4.0 %shard_map.190.refs_3_.refs_2_ = bf16[9,512,256]{2,1,0:T(8,128)(2,1)S(1)} custom-call(s32[1,9]{1,0:T(1,128)S(1)} %copy-done.10, s32[9,1,512]{2,1,0:T(1,128)S(1)} %bitcast.33, bf16[1024,512]{1,0:T(8,128)(2,1)S(1)} %copy-done.12, bf16[512,512]{1,0:T(8,128)(2,1)S(1)} %copy-done.13, f32[1,512]{1,0:T(1,128)S(1)} %bitcast.38), custom_call_target="tpu_custom_call" | custom-call | flops 2415919104 | tf_op jit(solution)/shard_map/pallas_call | solution.py:334
  46.1 0.0 collective-permute-done.9
  46.2 0.0 copy-start.6
  46.2 2.5 %collective-permute-start.11 = (bf16[3,64,512]{2,1,0:T(8,128)(2,1)S(1)}, bf16[3,64,512]{2,1,0:T(8,128)(2,1)S(1)}, u32[]{:S(2)}, u32[]{:S(2)}) collective-permute-start(bf16[3,64,512]{2,1,0:T(8,128)(2,1)S(1)} %pad_maximum_fusion.1.refs_0_), channel_id=1, source_target_pairs={{1,2},{3,4},{5,6},{7,0},{2,1},{4,3},{6,5},{0,7},{9,10},{11,12},{13... | collective-permute-start | bytes 589832 | tf_op jit(solution)/shard_map/ppermute | solution.py:299
  48.7 0.2 collective-permute-start.10
  49.0 4.0 %shard_map.189.refs_2_.refs_1_ = bf16[9,512,256]{2,1,0:T(8,128)(2,1)S(1)} custom-call(s32[1,9]{1,0:T(1,128)S(1)} %copy-done.10, s32[9,1,512]{2,1,0:T(1,128)S(1)} %bitcast.34, bf16[1024,512]{1,0:T(8,128)(2,1)S(1)} %copy-done.12, bf16[512,512]{1,0:T(8,128)(2,1)S(1)} %copy-done.13, f32[1,512]{1,0:T(1,128)S(1)} %bitcast.39), custom_call_target="tpu_custom_call" | custom-call | flops 2415919104 | tf_op jit(solution)/shard_map/pallas_call | solution.py:334
  53.1 4.6 %shard_map.193 = (bf16[3,64,512]{2,1,0:T(8,128)(2,1)S(1)}, bf16[3,64,512]{2,1,0:T(8,128)(2,1)S(1)}, bf16[9,512,512]{2,1,0:T(8,128)(2,1)S(1)}, bf16[9,512,512]{2,1,0:T(8,128)(2,1)S(1)}) custom-call(s32[1,9]{1,0:T(1,128)S(1)} %copy-done.10, s32[2]{0:T(128)S(1)} %pad_add_fusion.flips, s32[9,1,512]{2,1,0:T(1,128)S(1)} %bitcast.23, ...), custom_call_target="tpu_custom_call" | custom-call | flops 805306368 | tf_op jit(solution)/shard_map/pallas_call | solution.py:334
  57.6 1.2 %collective-permute-start.12 = (bf16[3,64,512]{2,1,0:T(8,128)(2,1)S(1)}, bf16[3,64,512]{2,1,0:T(8,128)(2,1)S(1)}, u32[]{:S(2)}, u32[]{:S(2)}) collective-permute-start(bf16[3,64,512]{2,1,0:T(8,128)(2,1)S(1)} %get-tuple-element.42), channel_id=1, source_target_pairs={{0,1},{2,3},{4,5},{6,7},{1,0},{3,2},{5,4},{7,6},{8,9},{10,11},{12,... | collective-permute-start | bytes 589832 | tf_op jit(solution)/shard_map/ppermute | solution.py:299
  58.9 2.7 %shard_map.194 = (bf16[3,64,512]{2,1,0:T(8,128)(2,1)S(1)}, bf16[9,512,512]{2,1,0:T(8,128)(2,1)S(1)}, bf16[9,512,512]{2,1,0:T(8,128)(2,1)S(1)}) custom-call(s32[1,9]{1,0:T(1,128)S(1)} %copy-done.10, s32[2]{0:T(128)S(1)} %pad_add_fusion.flips, s32[9,1,512]{2,1,0:T(1,128)S(1)} %bitcast.24, ...), custom_call_target="tpu_custom_call", output_to_operand_aliasing={{1}: (8, {}), {2}: (9, {})} | custom-call | flops 402653184 | tf_op jit(solution)/shard_map/pallas_call | solution.py:334
  61.6 2.6 %collective-permute-done.13.west = bf16[3,64,512]{2,1,0:T(8,128)(2,1)S(1)} collective-permute-done((bf16[3,64,512]{2,1,0:T(8,128)(2,1)S(1)}, bf16[3,64,512]{2,1,0:T(8,128)(2,1)S(1)}, u32[]{:S(2)}, u32[]{:S(2)}) %collective-permute-start.13) | collective-permute-done | bytes 196640 | tf_op jit(solution)/shard_map/ppermute | solution.py:299
  64.3 0.1 shard_map.197
  64.3 2.6 %collective-permute-start.14 = (bf16[64,512]{1,0:T(8,128)(2,1)S(1)}, bf16[64,512]{1,0:T(8,128)(2,1)S(1)}, u32[]{:S(2)}, u32[]{:S(2)}) collective-permute-start(bf16[64,512]{1,0:T(8,128)(2,1)S(1)} %get-tuple-element.45), channel_id=1, source_target_pairs={{0,8},{16,24},{32,40},{48,56},{64,72},{80,88},{96,104},{112,120},{... | collective-permute-start | bytes 196616 | tf_op jit(solution)/shard_map/ppermute | solution.py:299
  66.9 2.6 %collective-permute-start.15 = (bf16[64,512]{1,0:T(8,128)(2,1)S(1)}, bf16[64,512]{1,0:T(8,128)(2,1)S(1)}, u32[]{:S(2)}, u32[]{:S(2)}) collective-permute-start(bf16[64,512]{1,0:T(8,128)(2,1)S(1)} %get-tuple-element.46), channel_id=1, source_target_pairs={{8,16},{24,32},{40,48},{56,64},{72,80},{88,96},{104,112},{120,0},{... | collective-permute-start | bytes 196616 | tf_op jit(solution)/shard_map/ppermute | solution.py:299
  69.5 3.9 %collective-permute-done.15.second = bf16[64,512]{1,0:T(8,128)(2,1)S(1)} collective-permute-done((bf16[64,512]{1,0:T(8,128)(2,1)S(1)}, bf16[64,512]{1,0:T(8,128)(2,1)S(1)}, u32[]{:S(2)}, u32[]{:S(2)}) %collective-permute-start.15) | collective-permute-done | bytes 65568 | tf_op jit(solution)/shard_map/ppermute | solution.py:299
  73.4 0.5 shard_map.198
  73.8 2.6 %collective-permute-start.17 = (bf16[64,512]{1,0:T(8,128)(2,1)S(1)}, bf16[64,512]{1,0:T(8,128)(2,1)S(1)}, u32[]{:S(2)}, u32[]{:S(2)}) collective-permute-start(bf16[64,512]{1,0:T(8,128)(2,1)S(1)} %get-tuple-element.47), channel_id=1, source_target_pairs={{8,16},{24,32},{40,48},{56,64},{72,80},{88,96},{104,112},{120,0},{... | collective-permute-start | bytes 196616 | tf_op jit(solution)/shard_map/ppermute | solution.py:299
  76.5 5.7 %shard_map.204.partial = f32[1024,512]{1,0:T(8,128)S(1)} custom-call(s32[1,9]{1,0:T(1,128)S(1)} %copy-done.10, s32[9,1,512]{2,1,0:T(1,128)S(1)} %bitcast.35, bf16[9,512,512]{2,1,0:T(8,128)(2,1)S(1)} %get-tuple-element.58.grads, bf16[1024,512]{1,0:T(8,128)(2,1)S(1)} %copy-done.11, bf16[512,512]{1,0:T(8,128)(2,1)S(1)} %copy-done.13), custom_call_target="tpu_custom_call" | custom-call | flops 4831838208 | tf_op jit(solution)/shard_map/pallas_call | solution.py:334
  82.2 0.9 collective-permute-start.19
  83.1 1.3 %collective-permute-start.18 = (bf16[3,64,512]{2,1,0:T(8,128)(2,1)S(1)}, bf16[3,64,512]{2,1,0:T(8,128)(2,1)S(1)}, u32[]{:S(2)}, u32[]{:S(2)}) collective-permute-start(bf16[3,64,512]{2,1,0:T(8,128)(2,1)S(1)} %pad_maximum_fusion.2.refs_0_), channel_id=1, source_target_pairs={{0,1},{2,3},{4,5},{6,7},{1,0},{3,2},{5,4},{7,6},{8,9},{10,11},{12,... | collective-permute-start | bytes 589832 | tf_op jit(solution)/shard_map/ppermute | solution.py:299
  84.4 3.4 %shard_map.195.lower = bf16[1024,256]{1,0:T(8,128)(2,1)S(1)} custom-call(s32[1,9]{1,0:T(1,128)S(1)} %copy-done.10, s32[9,1,512]{2,1,0:T(1,128)S(1)} %bitcast.36, bf16[9,512,512]{2,1,0:T(8,128)(2,1)S(1)} %get-tuple-element.40.values.messages), custom_call_target="tpu_custom_call" | custom-call | flops 2415919104 | tf_op jit(solution)/shard_map/pallas_call | solution.py:334
  87.9 1.9 %shard_map.199 = (bf16[3,64,512]{2,1,0:T(8,128)(2,1)S(1)}, bf16[3,64,512]{2,1,0:T(8,128)(2,1)S(1)}, bf16[9,256,512]{2,1,0:T(8,128)(2,1)S(1)}) custom-call(s32[1,9]{1,0:T(1,128)S(1)} %copy-done.7, s32[2]{0:T(128)S(1)} %pad_add_fusion.flips, s32[9,1,256]{2,1,0:T(1,128)S(1)} %bitcast.21, bf16[3,64,512]{2,1,0:T(8,128)(2,1)S(1)} %collective-permute-done.18.refs_0_, ...), custom_call_target="tpu_custom_call" | custom-call | flops 402653184 | tf_op jit(solution)/shard_map/pallas_call | solution.py:334
  89.8 2.9 %collective-permute-start.20 = (bf16[3,64,512]{2,1,0:T(8,128)(2,1)S(1)}, bf16[3,64,512]{2,1,0:T(8,128)(2,1)S(1)}, u32[]{:S(2)}, u32[]{:S(2)}) collective-permute-start(bf16[3,64,512]{2,1,0:T(8,128)(2,1)S(1)} %get-tuple-element.51), channel_id=1, source_target_pairs={{0,1},{2,3},{4,5},{6,7},{1,0},{3,2},{5,4},{7,6},{8,9},{10,11},{12,... | collective-permute-start | bytes 589832 | tf_op jit(solution)/shard_map/ppermute | solution.py:299
  92.7 5.0 %shard_map.196 = bf16[1024,512]{1,0:T(8,128)(2,1)} custom-call(s32[1,9]{1,0:T(1,128)S(1)} %copy-done.10, s32[9,1,512]{2,1,0:T(1,128)S(1)} %bitcast.37, bf16[9,512,512]{2,1,0:T(8,128)(2,1)S(1)} %get-tuple-element.40.values.messages, bf16[1024,512]{1,0:T(8,128)(2,1)S(1)} %copy-done.12, bf16[1024,256]{1,0:T(8,128)(2,1)S(1)} %shard_map.195.lower, ...), custom_call_target="tpu_custom_call" | custom-call | flops 2415919104 | tf_op jit(solution)/shard_map/pallas_call | solution.py:334
  97.7 1.2 %shard_map.200 = (bf16[3,64,512]{2,1,0:T(8,128)(2,1)S(1)}, bf16[9,256,512]{2,1,0:T(8,128)(2,1)S(1)}) custom-call(s32[1,9]{1,0:T(1,128)S(1)} %copy-done.7, s32[2]{0:T(128)S(1)} %pad_add_fusion.flips, s32[9,1,256]{2,1,0:T(1,128)S(1)} %bitcast.22, bf16[3,64,512]{2,1,0:T(8,128)(2,1)S(1)} %pad_maximum_fusion.2.refs_0_, ...), custom_call_target="tpu_custom_call", output_to_operand_aliasing={{1}: (5, {})} | custom-call | flops 201326592 | tf_op jit(solution)/shard_map/pallas_call | solution.py:334
  99.0 0.0 copy-start.3
  99.0 2.1 %shard_map.203.first = f32[1024,512]{1,0:T(8,128)S(1)} custom-call(s32[1,9]{1,0:T(1,128)S(1)} %copy-done.7, s32[9,1,256]{2,1,0:T(1,128)S(1)} %bitcast.27, bf16[9,256,512]{2,1,0:T(8,128)(2,1)S(1)} %get-tuple-element.57.grads), custom_call_target="tpu_custom_call" | custom-call | flops 1610612736 | tf_op jit(solution)/shard_map/pallas_call | solution.py:334
  101.1 0.1 shard_map.201
  101.2 4.2 %collective-permute-start.22 = (bf16[64,512]{1,0:T(8,128)(2,1)S(1)}, bf16[64,512]{1,0:T(8,128)(2,1)S(1)}, u32[]{:S(2)}, u32[]{:S(2)}) collective-permute-start(bf16[64,512]{1,0:T(8,128)(2,1)S(1)} %get-tuple-element.54), channel_id=1, source_target_pairs={{0,8},{16,24},{32,40},{48,56},{64,72},{80,88},{96,104},{112,120},{... | collective-permute-start | bytes 196616 | tf_op jit(solution)/shard_map/ppermute | solution.py:299
  105.4 3.2 %collective-permute-start.23 = (bf16[64,512]{1,0:T(8,128)(2,1)S(1)}, bf16[64,512]{1,0:T(8,128)(2,1)S(1)}, u32[]{:S(2)}, u32[]{:S(2)}) collective-permute-start(bf16[64,512]{1,0:T(8,128)(2,1)S(1)} %get-tuple-element.55), channel_id=1, source_target_pairs={{8,16},{24,32},{40,48},{56,64},{72,80},{88,96},{104,112},{120,0},{... | collective-permute-start | bytes 196616 | tf_op jit(solution)/shard_map/ppermute | solution.py:299
  108.6 3.1 %shard_map.205 = bf16[1024,512]{1,0:T(8,128)(2,1)} custom-call(s32[1,9]{1,0:T(1,128)S(1)} %copy-done.7, s32[9,1,256]{2,1,0:T(1,128)S(1)} %bitcast.28, bf16[9,256,512]{2,1,0:T(8,128)(2,1)S(1)} %get-tuple-element.57.grads, f32[1024,512]{1,0:T(8,128)S(1)} %shard_map.203.first, f32[1024,512]{1,0:T(8,128)S(1)} %shard_map.204.partial, bf16[512,512]{1,0:T(8,128)(2,1)S(1)} %copy-done.3), custom_call_target="tpu_custom_call" | custom-call | flops 805306368 | tf_op jit(solution)/shard_map/pallas_call | solution.py:334
  111.7 0.1 collective-permute-done.23.second
  111.9 0.9 shard_map.202
  (44 shorter events, 0.1 us)
Async XLA Ops:
  0.6 7.6 %collective-permute-start = (bf16[64,512]{1,0:T(8,128)(2,1)}, bf16[64,512]{1,0:T(8,128)(2,1)S(1)}, u32[]{:S(2)}, u32[]{:S(2)}) collective-permute-start(bf16[64,512]{1,0:T(8,128)(2,1)} %feat.6), channel_id=1, source_target_pairs={{0,8},{16,24},{32,40},{48,56},{64,72},{80,88},{96,104},{112,120},{... | collective-permute-start | bytes 196616 | tf_op jit(solution)/shard_map/ppermute | solution.py:299
  2.8 7.3 %collective-permute-start.1 = (bf16[64,512]{1,0:T(8,128)(2,1)}, bf16[64,512]{1,0:T(8,128)(2,1)S(1)}, u32[]{:S(2)}, u32[]{:S(2)}) collective-permute-start(bf16[64,512]{1,0:T(8,128)(2,1)} %feat.6), channel_id=1, source_target_pairs={{8,16},{24,32},{40,48},{56,64},{72,80},{88,96},{104,112},{120,0},{... | collective-permute-start | bytes 196616 | tf_op jit(solution)/shard_map/ppermute | solution.py:299
  11.0 8.3 %collective-permute-start.3 = (bf16[3,64,512]{2,1,0:T(8,128)(2,1)S(1)}, bf16[3,64,512]{2,1,0:T(8,128)(2,1)S(1)}, u32[]{:S(2)}, u32[]{:S(2)}) collective-permute-start(bf16[3,64,512]{2,1,0:T(8,128)(2,1)S(1)} %pad_maximum_fusion.refs_0_), channel_id=1, source_target_pairs={{1,2},{3,4},{5,6},{7,0},{2,1},{4,3},{6,5},{0,7},{9,10},{11,12},{13... | collective-permute-start | bytes 589832 | tf_op jit(solution)/shard_map/ppermute | solution.py:299
  14.0 5.3 %collective-permute-start.2 = (bf16[3,64,512]{2,1,0:T(8,128)(2,1)S(1)}, bf16[3,64,512]{2,1,0:T(8,128)(2,1)S(1)}, u32[]{:S(2)}, u32[]{:S(2)}) collective-permute-start(bf16[3,64,512]{2,1,0:T(8,128)(2,1)S(1)} %pad_maximum_fusion.refs_0_), channel_id=1, source_target_pairs={{0,1},{2,3},{4,5},{6,7},{1,0},{3,2},{5,4},{7,6},{8,9},{10,11},{12,... | collective-permute-start | bytes 589832 | tf_op jit(solution)/shard_map/ppermute | solution.py:299
  14.0 5.3 %copy-start = (bf16[512,512]{1,0:T(8,128)(2,1)S(1)}, bf16[512,512]{1,0:T(8,128)(2,1)}, u32[]{:S(2)}) copy-start(bf16[512,512]{1,0:T(8,128)(2,1)} %weight.19) | copy-start | bytes 1572868
  14.0 5.3 %copy-start.5 = (s32[1,9,256]{2,0,1:T(1,128)S(1)}, s32[1,9,256]{2,0,1:T(1,128)}, u32[]{:S(2)}) copy-start(s32[1,9,256]{2,0,1:T(1,128)} %param.20) | copy-start | bytes 27652
  14.0 5.3 %copy-start.7 = (s32[1,9]{1,0:T(1,128)S(1)}, s32[1,9]{1,0:T(1,128)}, u32[]{:S(2)}) copy-start(s32[1,9]{1,0:T(1,128)} %counts.31) | copy-start | bytes 112
  14.0 5.3 %copy-start.9 = (f32[512]{0:T(512)S(1)}, f32[512]{0:T(512)}, u32[]{:S(2)}) copy-start(f32[512]{0:T(512)} %param.27) | copy-start | bytes 6148
  19.2 4.6 %copy-start.10 = (s32[1,9]{1,0:T(1,128)S(1)}, s32[1,9]{1,0:T(1,128)}, u32[]{:S(2)}) copy-start(s32[1,9]{1,0:T(1,128)} %counts.30) | copy-start | bytes 112
  19.2 4.6 %copy-start.11 = (bf16[1024,512]{1,0:T(8,128)(2,1)S(1)}, bf16[1024,512]{1,0:T(8,128)(2,1)}, u32[]{:S(2)}) copy-start(bf16[1024,512]{1,0:T(8,128)(2,1)} %cot.5) | copy-start | bytes 3145732
  19.2 4.6 %copy-start.14 = (bf16[512,512]{1,0:T(8,128)(2,1)S(1)}, bf16[512,512]{1,0:T(8,128)(2,1)}, u32[]{:S(2)}) copy-start(bf16[512,512]{1,0:T(8,128)(2,1)} %weight.17) | copy-start | bytes 1572868
  19.2 4.6 %copy-start.15 = (s32[1,9,512]{2,0,1:T(1,128)S(1)}, s32[1,9,512]{2,0,1:T(1,128)}, u32[]{:S(2)}) copy-start(s32[1,9,512]{2,0,1:T(1,128)} %param.23) | copy-start | bytes 55300
  22.0 7.6 %collective-permute-start.4 = (bf16[3,64,512]{2,1,0:T(8,128)(2,1)S(1)}, bf16[3,64,512]{2,1,0:T(8,128)(2,1)S(1)}, u32[]{:S(2)}, u32[]{:S(2)}) collective-permute-start(bf16[3,64,512]{2,1,0:T(8,128)(2,1)S(1)} %get-tuple-element.33), channel_id=1, source_target_pairs={{0,1},{2,3},{4,5},{6,7},{1,0},{3,2},{5,4},{7,6},{8,9},{10,11},{12,... | collective-permute-start | bytes 589832 | tf_op jit(solution)/shard_map/ppermute | solution.py:299
  22.6 7.0 %collective-permute-start.5 = (bf16[3,64,512]{2,1,0:T(8,128)(2,1)S(1)}, bf16[3,64,512]{2,1,0:T(8,128)(2,1)S(1)}, u32[]{:S(2)}, u32[]{:S(2)}) collective-permute-start(bf16[3,64,512]{2,1,0:T(8,128)(2,1)S(1)} %get-tuple-element.34), channel_id=1, source_target_pairs={{1,2},{3,4},{5,6},{7,0},{2,1},{4,3},{6,5},{0,7},{9,10},{11,12},{13... | collective-permute-start | bytes 589832 | tf_op jit(solution)/shard_map/ppermute | solution.py:299
  29.7 9.5 %collective-permute-start.6 = (bf16[64,512]{1,0:T(8,128)(2,1)S(1)}, bf16[64,512]{1,0:T(8,128)(2,1)S(1)}, u32[]{:S(2)}, u32[]{:S(2)}) collective-permute-start(bf16[64,512]{1,0:T(8,128)(2,1)S(1)} %get-tuple-element.36), channel_id=1, source_target_pairs={{0,8},{16,24},{32,40},{48,56},{64,72},{80,88},{96,104},{112,120},{... | collective-permute-start | bytes 196616 | tf_op jit(solution)/shard_map/ppermute | solution.py:299
  29.8 9.4 %copy-start.1 = (bf16[512,512]{1,0:T(8,128)(2,1)S(1)}, bf16[512,512]{1,0:T(8,128)(2,1)}, u32[]{:S(2)}) copy-start(bf16[512,512]{1,0:T(8,128)(2,1)} %out_weight.3) | copy-start | bytes 1572868
  29.8 9.4 %copy-start.2 = (bf16[512,512]{1,0:T(8,128)(2,1)S(1)}, bf16[512,512]{1,0:T(8,128)(2,1)}, u32[]{:S(2)}) copy-start(bf16[512,512]{1,0:T(8,128)(2,1)} %weight.18) | copy-start | bytes 1572868
  29.8 9.4 %copy-start.4 = (bf16[64,512]{1,0:T(8,128)(2,1)S(1)}, bf16[64,512]{1,0:T(8,128)(2,1)}, u32[]{:S(2)}) copy-start(bf16[64,512]{1,0:T(8,128)(2,1)} %feat.6) | copy-start | bytes 196612
  29.8 12.2 %copy-start.12 = (bf16[1024,512]{1,0:T(8,128)(2,1)S(1)}, bf16[1024,512]{1,0:T(8,128)(2,1)}, u32[]{:S(2)}) copy-start(bf16[1024,512]{1,0:T(8,128)(2,1)} %feat.9) | copy-start | bytes 3145732
  29.9 12.2 %copy-start.13 = (bf16[512,512]{1,0:T(8,128)(2,1)S(1)}, bf16[512,512]{1,0:T(8,128)(2,1)}, u32[]{:S(2)}) copy-start(bf16[512,512]{1,0:T(8,128)(2,1)} %weight.20) | copy-start | bytes 1572868
  29.9 12.2 %copy-start.16 = (f32[512]{0:T(512)S(1)}, f32[512]{0:T(512)}, u32[]{:S(2)}) copy-start(f32[512]{0:T(512)} %param.31) | copy-start | bytes 6148
  29.9 9.3 %collective-permute-start.7 = (bf16[64,512]{1,0:T(8,128)(2,1)S(1)}, bf16[64,512]{1,0:T(8,128)(2,1)S(1)}, u32[]{:S(2)}, u32[]{:S(2)}) collective-permute-start(bf16[64,512]{1,0:T(8,128)(2,1)S(1)} %get-tuple-element.37), channel_id=1, source_target_pairs={{8,16},{24,32},{40,48},{56,64},{72,80},{88,96},{104,112},{120,0},{... | collective-permute-start | bytes 196616 | tf_op jit(solution)/shard_map/ppermute | solution.py:299
  39.6 6.5 %collective-permute-start.9 = (bf16[64,512]{1,0:T(8,128)(2,1)S(1)}, bf16[64,512]{1,0:T(8,128)(2,1)S(1)}, u32[]{:S(2)}, u32[]{:S(2)}) collective-permute-start(bf16[64,512]{1,0:T(8,128)(2,1)S(1)} %shard_map.188), channel_id=1, source_target_pairs={{8,16},{24,32},{40,48},{56,64},{72,80},{88,96},{104,112},{120,0},{... | collective-permute-start | bytes 196616 | tf_op jit(solution)/shard_map/ppermute | solution.py:299
  42.0 4.1 %collective-permute-start.8 = (bf16[64,512]{1,0:T(8,128)(2,1)S(1)}, bf16[64,512]{1,0:T(8,128)(2,1)S(1)}, u32[]{:S(2)}, u32[]{:S(2)}) collective-permute-start(bf16[64,512]{1,0:T(8,128)(2,1)S(1)} %shard_map.188), channel_id=1, source_target_pairs={{0,8},{16,24},{32,40},{48,56},{64,72},{80,88},{96,104},{112,120},{... | collective-permute-start | bytes 196616 | tf_op jit(solution)/shard_map/ppermute | solution.py:299
  46.2 6.9 %copy-start.6 = (s32[1,9,512]{2,0,1:T(1,128)S(1)}, s32[1,9,512]{2,0,1:T(1,128)}, u32[]{:S(2)}) copy-start(s32[1,9,512]{2,0,1:T(1,128)} %param.22) | copy-start | bytes 55300
  46.2 6.8 %collective-permute-start.11 = (bf16[3,64,512]{2,1,0:T(8,128)(2,1)S(1)}, bf16[3,64,512]{2,1,0:T(8,128)(2,1)S(1)}, u32[]{:S(2)}, u32[]{:S(2)}) collective-permute-start(bf16[3,64,512]{2,1,0:T(8,128)(2,1)S(1)} %pad_maximum_fusion.1.refs_0_), channel_id=1, source_target_pairs={{1,2},{3,4},{5,6},{7,0},{2,1},{4,3},{6,5},{0,7},{9,10},{11,12},{13... | collective-permute-start | bytes 589832 | tf_op jit(solution)/shard_map/ppermute | solution.py:299
  48.7 4.3 %collective-permute-start.10 = (bf16[3,64,512]{2,1,0:T(8,128)(2,1)S(1)}, bf16[3,64,512]{2,1,0:T(8,128)(2,1)S(1)}, u32[]{:S(2)}, u32[]{:S(2)}) collective-permute-start(bf16[3,64,512]{2,1,0:T(8,128)(2,1)S(1)} %pad_maximum_fusion.1.refs_0_), channel_id=1, source_target_pairs={{0,1},{2,3},{4,5},{6,7},{1,0},{3,2},{5,4},{7,6},{8,9},{10,11},{12,... | collective-permute-start | bytes 589832 | tf_op jit(solution)/shard_map/ppermute | solution.py:299
  57.6 4.0 %collective-permute-start.12 = (bf16[3,64,512]{2,1,0:T(8,128)(2,1)S(1)}, bf16[3,64,512]{2,1,0:T(8,128)(2,1)S(1)}, u32[]{:S(2)}, u32[]{:S(2)}) collective-permute-start(bf16[3,64,512]{2,1,0:T(8,128)(2,1)S(1)} %get-tuple-element.42), channel_id=1, source_target_pairs={{0,1},{2,3},{4,5},{6,7},{1,0},{3,2},{5,4},{7,6},{8,9},{10,11},{12,... | collective-permute-start | bytes 589832 | tf_op jit(solution)/shard_map/ppermute | solution.py:299
  58.9 5.4 %collective-permute-start.13 = (bf16[3,64,512]{2,1,0:T(8,128)(2,1)S(1)}, bf16[3,64,512]{2,1,0:T(8,128)(2,1)S(1)}, u32[]{:S(2)}, u32[]{:S(2)}) collective-permute-start(bf16[3,64,512]{2,1,0:T(8,128)(2,1)S(1)} %get-tuple-element.43), channel_id=1, source_target_pairs={{1,2},{3,4},{5,6},{7,0},{2,1},{4,3},{6,5},{0,7},{9,10},{11,12},{13... | collective-permute-start | bytes 589832 | tf_op jit(solution)/shard_map/ppermute | solution.py:299
  64.3 5.2 %collective-permute-start.14 = (bf16[64,512]{1,0:T(8,128)(2,1)S(1)}, bf16[64,512]{1,0:T(8,128)(2,1)S(1)}, u32[]{:S(2)}, u32[]{:S(2)}) collective-permute-start(bf16[64,512]{1,0:T(8,128)(2,1)S(1)} %get-tuple-element.45), channel_id=1, source_target_pairs={{0,8},{16,24},{32,40},{48,56},{64,72},{80,88},{96,104},{112,120},{... | collective-permute-start | bytes 196616 | tf_op jit(solution)/shard_map/ppermute | solution.py:299
  66.9 6.4 %collective-permute-start.15 = (bf16[64,512]{1,0:T(8,128)(2,1)S(1)}, bf16[64,512]{1,0:T(8,128)(2,1)S(1)}, u32[]{:S(2)}, u32[]{:S(2)}) collective-permute-start(bf16[64,512]{1,0:T(8,128)(2,1)S(1)} %get-tuple-element.46), channel_id=1, source_target_pairs={{8,16},{24,32},{40,48},{56,64},{72,80},{88,96},{104,112},{120,0},{... | collective-permute-start | bytes 196616 | tf_op jit(solution)/shard_map/ppermute | solution.py:299
  73.8 8.3 %collective-permute-start.17 = (bf16[64,512]{1,0:T(8,128)(2,1)S(1)}, bf16[64,512]{1,0:T(8,128)(2,1)S(1)}, u32[]{:S(2)}, u32[]{:S(2)}) collective-permute-start(bf16[64,512]{1,0:T(8,128)(2,1)S(1)} %get-tuple-element.47), channel_id=1, source_target_pairs={{8,16},{24,32},{40,48},{56,64},{72,80},{88,96},{104,112},{120,0},{... | collective-permute-start | bytes 196616 | tf_op jit(solution)/shard_map/ppermute | solution.py:299
  76.5 5.7 %collective-permute-start.16 = (bf16[64,512]{1,0:T(8,128)(2,1)S(1)}, bf16[64,512]{1,0:T(8,128)(2,1)S(1)}, u32[]{:S(2)}, u32[]{:S(2)}) collective-permute-start(bf16[64,512]{1,0:T(8,128)(2,1)S(1)} %get-tuple-element.47), channel_id=1, source_target_pairs={{0,8},{16,24},{32,40},{48,56},{64,72},{80,88},{96,104},{112,120},{... | collective-permute-start | bytes 196616 | tf_op jit(solution)/shard_map/ppermute | solution.py:299
  82.2 5.6 %collective-permute-start.19 = (bf16[3,64,512]{2,1,0:T(8,128)(2,1)S(1)}, bf16[3,64,512]{2,1,0:T(8,128)(2,1)S(1)}, u32[]{:S(2)}, u32[]{:S(2)}) collective-permute-start(bf16[3,64,512]{2,1,0:T(8,128)(2,1)S(1)} %pad_maximum_fusion.2.refs_0_), channel_id=1, source_target_pairs={{1,2},{3,4},{5,6},{7,0},{2,1},{4,3},{6,5},{0,7},{9,10},{11,12},{13... | collective-permute-start | bytes 589832 | tf_op jit(solution)/shard_map/ppermute | solution.py:299
  83.1 4.7 %collective-permute-start.18 = (bf16[3,64,512]{2,1,0:T(8,128)(2,1)S(1)}, bf16[3,64,512]{2,1,0:T(8,128)(2,1)S(1)}, u32[]{:S(2)}, u32[]{:S(2)}) collective-permute-start(bf16[3,64,512]{2,1,0:T(8,128)(2,1)S(1)} %pad_maximum_fusion.2.refs_0_), channel_id=1, source_target_pairs={{0,1},{2,3},{4,5},{6,7},{1,0},{3,2},{5,4},{7,6},{8,9},{10,11},{12,... | collective-permute-start | bytes 589832 | tf_op jit(solution)/shard_map/ppermute | solution.py:299
  89.8 11.3 %collective-permute-start.20 = (bf16[3,64,512]{2,1,0:T(8,128)(2,1)S(1)}, bf16[3,64,512]{2,1,0:T(8,128)(2,1)S(1)}, u32[]{:S(2)}, u32[]{:S(2)}) collective-permute-start(bf16[3,64,512]{2,1,0:T(8,128)(2,1)S(1)} %get-tuple-element.51), channel_id=1, source_target_pairs={{0,1},{2,3},{4,5},{6,7},{1,0},{3,2},{5,4},{7,6},{8,9},{10,11},{12,... | collective-permute-start | bytes 589832 | tf_op jit(solution)/shard_map/ppermute | solution.py:299
  92.7 8.4 %collective-permute-start.21 = (bf16[3,64,512]{2,1,0:T(8,128)(2,1)S(1)}, bf16[3,64,512]{2,1,0:T(8,128)(2,1)S(1)}, u32[]{:S(2)}, u32[]{:S(2)}) collective-permute-start(bf16[3,64,512]{2,1,0:T(8,128)(2,1)S(1)} %get-tuple-element.52), channel_id=1, source_target_pairs={{1,2},{3,4},{5,6},{7,0},{2,1},{4,3},{6,5},{0,7},{9,10},{11,12},{13... | collective-permute-start | bytes 589832 | tf_op jit(solution)/shard_map/ppermute | solution.py:299
  97.7 1.2 %copy-start.8 = (s32[1,9,256]{2,0,1:T(1,128)S(1)}, s32[1,9,256]{2,0,1:T(1,128)}, u32[]{:S(2)}) copy-start(s32[1,9,256]{2,0,1:T(1,128)} %param.19) | copy-start | bytes 27652
  99.0 9.7 %copy-start.3 = (bf16[512,512]{1,0:T(8,128)(2,1)S(1)}, bf16[512,512]{1,0:T(8,128)(2,1)}, u32[]{:S(2)}) copy-start(bf16[512,512]{1,0:T(8,128)(2,1)} %weight.21) | copy-start | bytes 1572868
  101.2 10.6 %collective-permute-start.22 = (bf16[64,512]{1,0:T(8,128)(2,1)S(1)}, bf16[64,512]{1,0:T(8,128)(2,1)S(1)}, u32[]{:S(2)}, u32[]{:S(2)}) collective-permute-start(bf16[64,512]{1,0:T(8,128)(2,1)S(1)} %get-tuple-element.54), channel_id=1, source_target_pairs={{0,8},{16,24},{32,40},{48,56},{64,72},{80,88},{96,104},{112,120},{... | collective-permute-start | bytes 196616 | tf_op jit(solution)/shard_map/ppermute | solution.py:299
  105.4 6.4 %collective-permute-start.23 = (bf16[64,512]{1,0:T(8,128)(2,1)S(1)}, bf16[64,512]{1,0:T(8,128)(2,1)S(1)}, u32[]{:S(2)}, u32[]{:S(2)}) collective-permute-start(bf16[64,512]{1,0:T(8,128)(2,1)S(1)} %get-tuple-element.55), channel_id=1, source_target_pairs={{8,16},{24,32},{40,48},{56,64},{72,80},{88,96},{104,112},{120,0},{... | collective-permute-start | bytes 196616 | tf_op jit(solution)/shard_map/ppermute | solution.py:299
